TPU v7x, 128 devices: a whole 4x4x4 slice. The times are simulated.
128 devices in a mesh: dev: 128 (over y, x, z, core).
Axes of the slice: x: 4, y: 4, z: 4, core: 2. Of those that a mesh axis runs over, the one named last changes fastest.
Arguments:
- prior_labels: bfloat16 [262144, 512], P('dev'), may hold values from 0.0009994507 to 1
- label_class: int32 [262144], P('dev'), may hold values from 0 to 511
- labeled: int32 [262144], P('dev'), may hold values 0 or 1
- features: bfloat16 [262144, 1024], P('dev'), may hold values from -6 to 6
- tile_cols: int32 [2048, 8], P('dev'), may hold values from 0 to 17, as said below
- tile_weights: bfloat16 [2048, 8, 128, 128], P('dev'), may hold values from 0 to 1, as said below
- halo_owner: int32 [32768, 1], P('dev'), may hold values from 0 to 127; in each aligned block of 256 rows (0 to 255, 256 to 511, ...) at most 4 rows name the same one
- halo_local: int32 [32768], P('dev'), may hold values from 0 to 2047
- batch_owner: int32 [65536, 1], P('dev'), may hold values from 0 to 127; in each aligned block of 512 rows (0 to 511, 512 to 1023, ...) at most 8 rows name the same one
- batch_local: int32 [65536], P('dev'), may hold values from 0 to 2047
- w_in: bfloat16 [4096, 1024], replicated, may hold values from -0.1875 to 0.1875
- w_out: bfloat16 [4096, 512], replicated, may hold values from -0.09375 to 0.09375
Outputs:
- propagated: bfloat16 [262144, 512], P('dev')
- row_error: float32 [65536], P('dev')
- grad_in: float32 [4096, 1024], P('dev')
- grad_out: float32 [4096, 512], P('dev')
Inputs may be any that keep to these rules, and one draw needn't show every extreme that they name: `tile_cols`: in each row tile's list the first 6 entries are tiles of the device's own rows (below 16), the first of them the row tile itself; the last 2 are halo tiles (16 and above). Entries may repeat. Every halo tile of a device is listed by some row tile of that device. `tile_weights`: strictly positive. `halo_owner`: within the 256 rows of one device no owner appears more than 4 times; in some device one owner appears exactly 4 times. `batch_owner`: within the 512 rows of one device no owner appears more than 8 times; in some device one owner appears exactly 8 times.
All inputs are finite; a program needn't handle non-finite values. No bound on the sum of `labeled` on one device may be relied on, other than what follows from the above.
Results may differ from a plain program's by a relative error of at most 0.0017.
Values may be sent and summed in bfloat16 or wider, within the bound.
No kernel may reach another device: no remote copies, remote signals or barrier semaphores. Data moves between devices by JAX's collectives and lax.ppermute only.
A program may use at most 128 MiB of HBM per device.

v0:
```python
import jax
import jax.numpy as jnp
from jax import lax
from jax.experimental import pallas as pl
from jax.experimental.pallas import tpu as pltpu
from jax.sharding import Mesh
from jax.sharding import PartitionSpec as P


DEV = "dev"
BF = jnp.bfloat16
F32 = jnp.float32
LANES = 128
HALO_SLOTS = 4
BATCH_SLOTS = 8
UNITS = 32
HBLK = 512


def params(mib=48, **more):
    return pltpu.CompilerParams(vmem_limit_bytes=mib * 2**20, **more)


def dot(left, right, dims):
    return lax.dot_general(left, right, ((dims[:1], dims[1:]), ((), ())), preferred_element_type=F32)


def ranks_of(owner_ref, blocks):
    below = lax.broadcasted_iota(jnp.int32, (LANES, LANES), 0)
    along = lax.broadcasted_iota(jnp.int32, (LANES, LANES), 1)
    rows = [owner_ref[b : b + 1, :] for b in range(blocks)]
    cols = [jnp.broadcast_to(row, (LANES, LANES)).T for row in rows]
    ranks = []
    for i in range(blocks):
        earlier = jnp.zeros((LANES, LANES), F32)
        for j in range(i + 1):
            same = cols[j] == rows[i]
            if j == i:
                same = same & (below < along)
            earlier = earlier + same.astype(F32)
        ranks.append(jnp.sum(earlier, axis=0, keepdims=True).astype(jnp.int32))
    return rows, ranks


def request_kernel(ho, hl, bo, bl, table, hslot, brank):
    device = lax.broadcasted_iota(jnp.int32, (LANES, LANES), 0)
    lane = lax.broadcasted_iota(jnp.int32, (LANES, LANES), 1)
    out = jnp.zeros((LANES, LANES), F32)
    at = 0
    for owner, local, count in ((ho, hl, HALO_SLOTS), (bo, bl, BATCH_SLOTS)):
        blocks = owner.shape[0]
        rows, ranks = ranks_of(owner, blocks)
        for s in range(count):
            total = jnp.zeros((LANES, LANES), F32)
            for i in range(blocks):
                hit = (device == rows[i]) & (ranks[i] == s)
                named = (local[i : i + 1, :] + 1).astype(F32)
                total = total + jnp.where(hit, jnp.broadcast_to(named, (LANES, LANES)), 0.0)
            out = jnp.where(lane == at, jnp.sum(total, axis=1, keepdims=True), out)
            at += 1
        for i in range(blocks):
            if owner is ho:
                hslot[i : i + 1, :] = rows[i] * HALO_SLOTS + ranks[i]
            else:
                brank[i : i + 1, :] = ranks[i]
    table[...] = out.astype(jnp.int32) - 1


def returned_kernel(errors, bo, brank, out):
    device = lax.broadcasted_iota(jnp.int32, (LANES, LANES), 0)
    for i in range(bo.shape[0]):
        total = jnp.zeros((LANES, LANES), F32)
        for s in range(BATCH_SLOTS):
            hit = (device == bo[i : i + 1, :]) & (brank[i : i + 1, :] == s)
            total = total + jnp.where(hit, errors[:, s : s + 1], 0.0)
        out[i : i + 1, :] = jnp.sum(total, axis=0, keepdims=True)


def pick_rows(table, first, count, nodes, onehot):
    node = lax.broadcasted_iota(jnp.int32, (LANES, nodes), 1)
    for s in range(count):
        wanted = table[:, first + s : first + s + 1]
        onehot[s * LANES : (s + 1) * LANES, :] = (node == wanted).astype(F32).astype(BF)


def forward_kernel(place, table, features, w_in, w_out, x, hidden, logits, w_out_to, onehot, acc, in_buf, out_buf, in_sem, out_sem):
    step = pl.program_id(0)
    steps = pl.num_programs(0)
    chunks = HBLK // UNITS
    core = place[3]

    def fetch(block, slot):
        half = block // 4
        holder = jnp.where(half == 1, core, 1 - core)
        turn = 1 - holder
        a = (block % 4 + turn) % 4
        for n in range(chunks):
            b = (n // 4 + turn) % 4
            c = (n % 4 + turn) % 4
            source = ((a * 4 + b) * 4 + c) * 2 + holder
            pltpu.make_async_copy(w_in.at[source], in_buf.at[slot, n], in_sem.at[slot]).start()
            pltpu.make_async_copy(w_out.at[source], out_buf.at[slot, n], out_sem.at[slot]).start()

    @pl.when(step == 0)
    def _():
        fetch(0, 0)
        pick_rows(table, HALO_SLOTS, BATCH_SLOTS, features.shape[0], onehot)
        x[...] = dot(onehot[...], features[...], (1, 0)).astype(BF)
        acc[...] = jnp.zeros(acc.shape, F32)

    slot = step % 2

    @pl.when(step + 1 < steps)
    def _():
        fetch(step + 1, 1 - slot)

    pltpu.make_async_copy(w_in.at[pl.ds(0, chunks)], in_buf.at[slot], in_sem.at[slot]).wait()
    pltpu.make_async_copy(w_out.at[pl.ds(0, chunks)], out_buf.at[slot], out_sem.at[slot]).wait()
    w_out_here = out_buf[slot].reshape(HBLK, out_buf.shape[3])
    w_out_to[...] = w_out_here
    h = jnp.tanh(dot(in_buf[slot].reshape(HBLK, in_buf.shape[3]), x[...], (1, 1))).astype(BF)
    hidden[...] = h
    acc[...] += dot(w_out_here, h, (0, 0))

    @pl.when(step == steps - 1)
    def _():
        logits[...] = acc[...].T


def spread_kernel(cols, weights, prior, halo, hslot, given, table, logits, prop, residue, errors, halo_tab, prop_all, onehot):
    step = pl.program_id(0)
    per = weights.shape[0]
    classes = prior.shape[1]

    @pl.when(step == 0)
    def _():
        slots = halo.shape[0]
        slot = lax.broadcasted_iota(jnp.int32, (slots, LANES), 0)
        for b in range(2):
            pick = (slot == hslot[b : b + 1, :]).astype(F32).astype(BF)
            halo_tab[b * LANES : (b + 1) * LANES, :] = dot(pick, halo[...], (0, 0)).astype(BF)

    for t in range(per):
        r = step * per + t
        acc = jnp.zeros((LANES, classes), F32)
        wide = jnp.zeros((LANES, LANES), F32)
        for m in range(4):
            pair = []
            for k in (2 * m, 2 * m + 1):
                wide = wide + weights[t, k].astype(F32)
                c = cols[r, k]
                if k < 6:
                    pair.append(prior[pl.ds(pl.multiple_of(c * LANES, LANES), LANES), :])
                else:
                    pair.append(halo_tab[pl.ds(pl.multiple_of((c - 16) * LANES, LANES), LANES), :])
            left = jnp.concatenate([weights[t, 2 * m], weights[t, 2 * m + 1]], axis=1)
            acc = acc + dot(left, jnp.concatenate(pair, axis=0), (1, 0))
        degree = jnp.sum(wide, axis=1, keepdims=True)
        mark = jnp.broadcast_to(given[pl.ds(r, 1), :], (LANES, LANES)).T
        lane = lax.broadcasted_iota(jnp.int32, (LANES, LANES), 1)
        seeds = jnp.concatenate([(mark == lane + g * LANES).astype(F32) for g in range(classes // LANES)], axis=1)
        mixed = (0.8 * (acc / degree) + 0.2 * seeds).astype(BF)
        prop[t * LANES : (t + 1) * LANES, :] = mixed
        prop_all[pl.ds(pl.multiple_of(r * LANES, LANES), LANES), :] = mixed

    @pl.when(step == pl.num_programs(0) - 1)
    def _():
        pick_rows(table, HALO_SLOTS, BATCH_SLOTS, prop_all.shape[0], onehot)
        lane = lax.broadcasted_iota(jnp.int32, (LANES, LANES), 1)
        out = jnp.zeros((LANES, LANES), F32)
        for s in range(BATCH_SLOTS):
            at = slice(s * LANES, (s + 1) * LANES)
            log_z = jnp.log(dot(onehot[at, :], prop_all[...], (1, 0)))
            target = log_z - jnp.mean(log_z, axis=1, keepdims=True)
            valid = table[:, HALO_SLOTS + s : HALO_SLOTS + s + 1] >= 0
            differ = jnp.where(valid, logits[at, :] - target, 0.0)
            out = jnp.where(lane == s, 0.5 * jnp.mean(differ * differ, axis=1, keepdims=True), out)
            residue[at, :] = (differ * (1.0 / 256.0)).astype(BF)
        errors[...] = out


def gradients(w_out, hidden, residue, x):
    h = hidden[...]
    wide = h.astype(F32)
    back = (dot(w_out[...], residue[...], (1, 1)) * (1.0 - wide * wide)).astype(BF)
    return dot(h, residue[...], (1, 0)), dot(back, x[...], (1, 0))


def peer_kernel(place, w_out, hidden, residue, x, grad):
    out, into = gradients(w_out, hidden, residue, x)
    grad[:, :512] = out.astype(BF)
    grad[:, 512:] = into.astype(BF)


def own_kernel(place, w_out, hidden, residue, x, arrived, errors, a, send_b, keep_b, send_c, keep_c, errors_to):
    out, into = gradients(w_out, hidden, residue, x)
    a[...] = (out + arrived[:, :512].astype(F32)).astype(BF)
    total = (into + arrived[:, 512:].astype(F32)).astype(BF)
    left = total[:, :512].reshape(2, 256, 512)
    right = total[:, 512:].reshape(4, 2, 64, 512)

    for half in range(2):

        @pl.when(place[1] == half)
        def _():
            keep_b[0] = left[half]
            send_b[0] = left[1 - half]

        @pl.when(place[2] == half)
        def _():
            keep_c[0] = right[:, half]
            send_c[0] = right[:, 1 - half]

    errors_to[...] = errors[...]


def pairing(level, dims):
    flip = 3 if level == 1 else 1
    pairs = []
    for source in range(128):
        core = source % 2
        spot = [source // 32, (source // 8) % 4, (source // 2) % 4]
        for d in dims:
            shifted = (spot[d] - (1 - core)) % 4
            spot[d] = ((shifted ^ flip) + (1 - core)) % 4
        pairs.append((source, ((spot[0] * 4 + spot[1]) * 4 + spot[2]) * 2 + core))
    return pairs


def exchange(x, level, dims):
    return lax.ppermute(x, DEV, pairing(level, dims))


def deal_kernel(bits, k0, r0, k1, r1, k2, r2, own, *sends):
    for m in range(8):
        a = bits[0] ^ (m >> 2)
        b = bits[1] ^ ((m >> 1) & 1)
        c = bits[2] ^ (m & 1)
        for j, (k, r) in enumerate(((k0, r0), (k1, r1), (k2, r2))):
            piece = k[a, b, c].astype(F32) + r[a, b, c].astype(F32)
            if m == 0:
                own[:, j * 512 : (j + 1) * 512] = piece
            else:
                sends[m - 1][:, j * 512 : (j + 1) * 512] = piece.astype(BF)


def summed_over_chips(first, second, halves, bits):
    shape_a, shape_b, shape_c = (2, 4, 4, UNITS, 512), (2, 2, 4, UNITS, 512), (2, 4, 2, UNITS, 512)
    send_a, send_b1, keep_b1, send_c1, keep_c1 = first
    keep_a, send_b2, keep_b2, send_c2, keep_c2 = second
    got_a = exchange(send_a, 1, (0,)).reshape(shape_a)
    got_b1, got_b2 = (exchange(v, 1, (1,)).reshape(shape_b) for v in (send_b1, send_b2))
    got_c1, got_c2 = (exchange(v, 1, (2,)).reshape(shape_c) for v in (send_c1, send_c2))
    keep_a = keep_a.reshape(shape_a)
    keep_b1, keep_b2 = keep_b1.reshape(shape_b), keep_b2.reshape(shape_b)
    keep_c1, keep_c2 = keep_c1.reshape(shape_c), keep_c2.reshape(shape_c)

    def added(kept, got, dim=None, half=None):
        if dim is not None:
            kept, got = (lax.dynamic_slice_in_dim(v, 2 * half, 2, dim) for v in (kept, got))
        return kept.astype(F32) + got.astype(F32)

    def sent(value, dim):
        return exchange(value.astype(BF), 1, (dim,))

    _, hb, hc = halves
    b_send = added(keep_b1, got_b1).astype(BF)
    b_got = sent(b_send, 0)
    a_got = sent(added(keep_a, got_a, 2, 1 - hc), 2)
    c_got = sent(jnp.stack([added(keep_c1, got_c1, 1, 1 - hb), added(keep_c2, got_c2, 1, 1 - hb)]), 1)
    b = added(keep_b2, got_b2).astype(BF)
    a = added(keep_a, got_a, 2, hc).astype(BF)
    c1 = added(keep_c1, got_c1, 1, hb).astype(BF)
    c2 = added(keep_c2, got_c2, 1, hb).astype(BF)
    b_last = sent(added(b, b_got, 2, 1 - hc), 2)
    a_last = sent(added(a, a_got, 1, 1 - hb), 1)
    c_last = sent(added(c1, c_got[0]), 0)
    b = added(b, b_got, 2, hc)
    a = added(a, a_got, 1, hb)
    c = added(c2, c_got[1])
    piece = jax.ShapeDtypeStruct((UNITS, 1536), BF)
    own, *pieces = pl.pallas_call(
        deal_kernel,
        in_specs=[pl.BlockSpec(memory_space=pltpu.SMEM)] + [pl.BlockSpec(memory_space=pltpu.VMEM)] * 6,
        out_shape=[jax.ShapeDtypeStruct((UNITS, 1536), F32)] + [piece] * 7,
        compiler_params=params(16),
        name="deal",
    )(bits, a, a_last, b, b_last, c, c_last)
    total = own
    for m in range(1, 8):
        dims = [d for d in range(3) if (m >> (2 - d)) & 1]
        total = total + exchange(pieces[m - 1], 2, dims).astype(F32)
    return total


def on_device(prior, label_class, labeled, features, tile_cols, tile_weights, halo_owner, halo_local, batch_owner, batch_local, w_in, w_out):
    nodes, classes = prior.shape
    feat = features.shape[1]
    hid = w_in.shape[0]
    halo_count = halo_local.shape[0]
    batch = batch_local.shape[0]
    rows = BATCH_SLOTS * LANES
    me = lax.axis_index(DEV)
    core = me % 2
    chip = (me // 32, (me // 8) % 4, (me // 2) % 4)
    spots = [(s + 3 + core) % 4 for s in chip]
    halves = [s // 2 for s in spots]
    peer_half = (chip[0] + 4 - core) % 4 // 2
    place = jnp.stack([*halves, core, peer_half]).astype(jnp.int32)
    bits = jnp.stack([s % 2 for s in spots]).astype(jnp.int32)
    vmem = pl.BlockSpec(memory_space=pltpu.VMEM)
    smem = pl.BlockSpec(memory_space=pltpu.SMEM)
    hbm = pl.BlockSpec(memory_space=pl.ANY)
    i32 = jnp.int32

    bo = batch_owner.reshape(batch // LANES, LANES)
    table, hslot, brank = pl.pallas_call(
        request_kernel,
        in_specs=[vmem] * 4,
        out_shape=[
            jax.ShapeDtypeStruct((LANES, LANES), i32),
            jax.ShapeDtypeStruct((halo_count // LANES, LANES), i32),
            jax.ShapeDtypeStruct((batch // LANES, LANES), i32),
        ],
        name="request",
    )(
        halo_owner.reshape(halo_count // LANES, LANES),
        halo_local.reshape(halo_count // LANES, LANES),
        bo,
        batch_local.reshape(batch // LANES, LANES),
    )
    asked = lax.all_to_all(table[:, : HALO_SLOTS + BATCH_SLOTS], DEV, 0, 0, tiled=True)

    served = prior[jnp.maximum(asked[:, :HALO_SLOTS], 0)]
    halo = lax.all_to_all(served, DEV, 0, 0, tiled=True).reshape(LANES * HALO_SLOTS, classes)

    def whole(shape):
        return pl.BlockSpec(shape, lambda i, *_: (0,) * len(shape))

    def once(shape):
        return pl.BlockSpec(shape, lambda i, *_: (0,) * len(shape), pipeline_mode=pl.Buffered(1))

    def rows_at(offset, width):
        return pl.BlockSpec((HBLK, width), lambda i, *_: (i + offset, 0))

    slots = HALO_SLOTS + BATCH_SLOTS
    chunks = HBLK // UNITS
    x, hidden, logits, w_out_o = pl.pallas_call(
        forward_kernel,
        grid=(hid // HBLK,),
        in_specs=[smem, once((LANES, slots)), once((nodes, feat)), hbm, hbm],
        out_specs=[whole((rows, feat)), rows_at(0, rows), whole((rows, classes)), rows_at(0, classes)],
        out_shape=[
            jax.ShapeDtypeStruct((rows, feat), BF),
            jax.ShapeDtypeStruct((hid, rows), BF),
            jax.ShapeDtypeStruct((rows, classes), F32),
            jax.ShapeDtypeStruct((hid, classes), BF),
        ],
        scratch_shapes=[
            pltpu.VMEM((rows, nodes), BF),
            pltpu.VMEM((classes, rows), F32),
            pltpu.VMEM((2, chunks, UNITS, feat), BF),
            pltpu.VMEM((2, chunks, UNITS, classes), BF),
            pltpu.SemaphoreType.DMA((2,)),
            pltpu.SemaphoreType.DMA((2,)),
        ],
        compiler_params=params(36),
        name="forward",
    )(place, asked, features, w_in.reshape(128, UNITS, feat), w_out.reshape(128, UNITS, classes))

    row_tiles = tile_weights.shape[0]
    per = 2
    given = jnp.where(labeled == 1, label_class, -1).reshape(row_tiles, LANES)
    prop, residue, errors = pl.pallas_call(
        spread_kernel,
        grid=(row_tiles // per,),
        in_specs=[
            smem,
            pl.BlockSpec((per, 8, LANES, LANES), lambda i: (i, 0, 0, 0)),
            once((nodes, classes)),
            once((LANES * HALO_SLOTS, classes)),
            once((halo_count // LANES, LANES)),
            once((row_tiles, LANES)),
            once((LANES, slots)),
            once((rows, classes)),
        ],
        out_specs=[
            pl.BlockSpec((per * LANES, classes), lambda i: (i, 0)),
            whole((rows, classes)),
            whole((LANES, LANES)),
        ],
        out_shape=[
            jax.ShapeDtypeStruct((nodes, classes), BF),
            jax.ShapeDtypeStruct((rows, classes), BF),
            jax.ShapeDtypeStruct((LANES, LANES), F32),
        ],
        scratch_shapes=[
            pltpu.VMEM((halo_count, classes), BF),
            pltpu.VMEM((nodes, classes), BF),
            pltpu.VMEM((rows, nodes), BF),
        ],
        compiler_params=params(24),
        name="spread",
    )(tile_cols, tile_weights, prior, halo, hslot, given, asked, logits)

    partner = [(d, d ^ 1) for d in range(128)]
    part_rows = 2 * HBLK

    def peer_part(part):
        def block(i, p):
            half = p[4] if part else 1 - p[4]
            return (2 * half + i, 0)

        grad = pl.pallas_call(
            peer_kernel,
            grid_spec=pltpu.PrefetchScalarGridSpec(
                num_scalar_prefetch=1,
                grid=(2,),
                in_specs=[
                    pl.BlockSpec((HBLK, classes), block),
                    pl.BlockSpec((HBLK, rows), block),
                    once((rows, classes)),
                    once((rows, feat)),
                ],
                out_specs=rows_at(0, classes + feat),
            ),
            out_shape=jax.ShapeDtypeStruct((part_rows, classes + feat), BF),
            compiler_params=params(24),
        )(place, w_out_o, hidden, residue, x)
        return lax.ppermute(grad, DEV, partner)

    b_spec = pl.BlockSpec((1, 256, 512), lambda i, p: (i, 0, 0))
    c_spec = pl.BlockSpec((1, 4, 64, 512), lambda i, p: (i, 0, 0, 0))
    b_shape = jax.ShapeDtypeStruct((2, 256, 512), BF)
    c_shape = jax.ShapeDtypeStruct((2, 4, 64, 512), BF)

    def own_part(part, arrived):
        def block(i, p):
            half = p[0] if part else 1 - p[0]
            return (4 + 2 * half + i, 0)

        return pl.pallas_call(
            own_kernel,
            grid_spec=pltpu.PrefetchScalarGridSpec(
                num_scalar_prefetch=1,
                grid=(2,),
                in_specs=[
                    pl.BlockSpec((HBLK, classes), block),
                    pl.BlockSpec((HBLK, rows), block),
                    once((rows, classes)),
                    once((rows, feat)),
                    rows_at(0, classes + feat),
                    once((LANES, LANES)),
                ],
                out_specs=[rows_at(0, classes), b_spec, b_spec, c_spec, c_spec, whole((LANES, LANES))],
            ),
            out_shape=[
                jax.ShapeDtypeStruct((part_rows, classes), BF),
                b_shape,
                b_shape,
                c_shape,
                c_shape,
                jax.ShapeDtypeStruct((LANES, LANES), F32),
            ],
            compiler_params=params(28),
        )(place, w_out_o, hidden, residue, x, arrived, errors)

    arrived = [peer_part(0), peer_part(1)]
    *first, _ = own_part(0, arrived[0])
    *second, errors_out = own_part(1, arrived[1])
    total = summed_over_chips(first, second, halves, bits)

    back_errors = lax.all_to_all(errors_out[:, :BATCH_SLOTS], DEV, 0, 0, tiled=True)
    row_error = pl.pallas_call(
        returned_kernel,
        in_specs=[vmem] * 3,
        out_shape=jax.ShapeDtypeStruct((batch // LANES, LANES), F32),
        name="returned",
    )(back_errors, bo, brank).reshape(batch)
    return prop, row_error, total[:, 512:], total[:, :512]


def solution(mesh):
    split = Mesh(mesh.devices.reshape(128), (DEV,))
    in_specs = (
        P(DEV, None),
        P(DEV),
        P(DEV),
        P(DEV, None),
        P(DEV, None),
        P(DEV, None, None, None),
        P(DEV, None),
        P(DEV),
        P(DEV, None),
        P(DEV),
        P(),
        P(),
    )
    out_specs = (P(DEV, None), P(DEV), P(DEV, None), P(DEV, None))
    return jax.shard_map(on_device, mesh=split, in_specs=in_specs, out_specs=out_specs, check_vma=False)
```

profile of v0, /device:TPU:1, one launch (start us, length us, event | category | flops | bytes accessed | tf_op | source)
XLA Modules:
  0.0 196.2 jit_solution(6144181521970721537)
XLA Ops:
  0.6 1.9 request.1
  2.5 20.9 %all_to_all.27 = s32[128,1,12]{2,1,0:T(1,128)S(1)} all-to-all(s32[128,1,12]{2,1,0:T(1,128)} %bitcast.67), channel_id=1, replica_groups=mesh['dev'=128] {'dev'}, dimensions={0} | all-to-all | bytes 12288 | tf_op jit(solution)/shard_map/all_to_all | solution.py:332
  23.4 0.1 reshape.92
  23.5 3.9 %gather_fusion = bf16[512,512]{1,0:T(8,128)(2,1)S(1)} fusion(bf16[2048,512]{1,0:T(8,128)(2,1)} %prior.1, s32[1024]{0:T(1024)S(1)} %pad_clamp_fusion), kind=kCustom, calls=%fused_computation | custom fusion | bytes 1050624 | tf_op jit(solution)/shard_map/gather | solution.py:334
  27.4 0.9 reshape.91
  28.3 5.6 %all-to-all-start.1 = ((bf16[128,4,512]{2,1,0:T(4,128)(2,1)}), bf16[128,4,512]{2,1,0:T(4,128)(2,1)}, u32[]{:S(2)}, u32[]{:S(2)}) async-start(bf16[128,4,512]{2,1,0:T(4,128)(2,1)} %reshape.91), calls=%async_computation.1 | async-start | bytes 1048576 | tf_op jit(solution)/shard_map/all_to_all | solution.py:335
  34.3 0.1 stack.47.place
  34.4 2.2 %copy-done.5 = bf16[2048,1024]{1,0:T(8,128)(2,1)S(1)} copy-done((bf16[2048,1024]{1,0:T(8,128)(2,1)S(1)}, bf16[2048,1024]{1,0:T(8,128)(2,1)}, u32[]{:S(2)}) %copy-start.5) | copy-done | bytes 4194328
  36.6 2.2 %copy-done.6 = bf16[4096,512]{1,0:T(8,128)(2,1)S(1)} copy-done((bf16[4096,512]{1,0:T(8,128)(2,1)S(1)}, bf16[4096,512]{1,0:T(8,128)(2,1)}, u32[]{:S(2)}) %copy-start.6) | copy-done | bytes 4194328
  38.8 28.1 %forward.1 = (bf16[1024,1024]{1,0:T(8,128)(2,1)S(1)}, bf16[4096,1024]{1,0:T(8,128)(2,1)}, f32[1024,512]{1,0:T(8,128)S(1)}, bf16[4096,512]{1,0:T(8,128)(2,1)S(1)}) custom-call(s32[5]{0:T(128)S(1)} %stack.47.place, s32[128,12]{1,0:T(8,128)S(1)} %bitcast.51, bf16[2048,1024]{1,0:T(8,128)(2,1)S(1)} %copy-done.5, bf16[128,32,1024]{2,1,0:T(8,128)(2,1)} %bitcast.59, ...), custom_call_target="tpu_custom_call" | custom-call | tf_op jit(solution)/shard_map/forward/pallas_call | solution.py:348
  66.9 2.0 %copy-done.1 = bf16[4096,512]{1,0:T(8,128)(2,1)} copy-done((bf16[4096,512]{1,0:T(8,128)(2,1)}, bf16[4096,512]{1,0:T(8,128)(2,1)S(1)}, u32[]{:S(2)}) %copy-start.1) | copy-done | bytes 4194328
  68.9 1.3 copy-done.10
  70.2 1.2 reshape.77.halo
  71.4 1.6 copy-done.4
  73.0 2.2 %copy-done.7 = bf16[16,8,128,128]{3,2,1,0:T(8,128)(2,1)S(1)} copy-done((bf16[16,8,128,128]{3,2,1,0:T(8,128)(2,1)S(1)}, bf16[16,8,128,128]{3,2,1,0:T(8,128)(2,1)}, u32[]{:S(2)}) %copy-start.7) | copy-done | bytes 4194328
  75.2 1.6 copy-done.11
  76.8 9.0 %spread.1 = (bf16[2048,512]{1,0:T(8,128)(2,1)}, bf16[1024,512]{1,0:T(8,128)(2,1)S(1)}, f32[128,128]{1,0:T(8,128)S(1)}) custom-call(s32[16,8]{1,0:T(8,128)S(1)} %copy.19.cols, bf16[16,8,128,128]{3,2,1,0:T(8,128)(2,1)S(1)} %copy-done.7, bf16[2048,512]{1,0:T(8,128)(2,1)S(1)} %copy-done.4, bf16[512,512]{1,0:T(8,128)(2,1)S(1)} %reshape.77.halo, ...), custom_call_target="tpu_custom_call" | custom-call | tf_op jit(solution)/shard_map/spread/pallas_call | solution.py:374
  85.8 2.2 %copy-done.2 = bf16[4096,512]{1,0:T(8,128)(2,1)S(1)} copy-done((bf16[4096,512]{1,0:T(8,128)(2,1)S(1)}, bf16[4096,512]{1,0:T(8,128)(2,1)}, u32[]{:S(2)}) %copy-start.2) | copy-done | bytes 4194328
  88.0 5.4 %shard_map.149 = bf16[1024,1536]{1,0:T(8,128)(2,1)S(1)} custom-call(s32[5]{0:T(128)S(1)} %stack.47.place, bf16[4096,512]{1,0:T(8,128)(2,1)S(1)} %copy-done.2, bf16[4096,1024]{1,0:T(8,128)(2,1)S(1)} %copy-done, bf16[1024,512]{1,0:T(8,128)(2,1)S(1)} %get-tuple-element.39.residue, bf16[1024,1024]{1,0:T(8,128)(2,1)S(1)} %get-tuple-element.40.x), custom_call_target="tpu_custom_call" | custom-call | tf_op jit(solution)/shard_map/pallas_call | solution.py:414
  93.4 1.7 collective-permute-start.1
  95.2 5.4 %shard_map.147 = bf16[1024,1536]{1,0:T(8,128)(2,1)S(1)} custom-call(s32[5]{0:T(128)S(1)} %stack.47.place, bf16[4096,512]{1,0:T(8,128)(2,1)S(1)} %copy-done.2, bf16[4096,1024]{1,0:T(8,128)(2,1)S(1)} %copy-done, bf16[1024,512]{1,0:T(8,128)(2,1)S(1)} %get-tuple-element.39.residue, bf16[1024,1024]{1,0:T(8,128)(2,1)S(1)} %get-tuple-element.40.x), custom_call_target="tpu_custom_call" | custom-call | tf_op jit(solution)/shard_map/pallas_call | solution.py:414
  100.6 0.1 collective-permute-start
  100.7 1.6 copy-done.8
  102.3 1.9 copy-done.9
  104.2 6.7 %shard_map.150 = (bf16[1024,512]{1,0:T(8,128)(2,1)}, bf16[2,256,512]{2,1,0:T(8,128)(2,1)}, bf16[2,256,512]{2,1,0:T(8,128)(2,1)S(1)}, bf16[2,4,64,512]{3,2,1,0:T(...) custom-call(s32[5]{0:T(128)S(1)} %stack.47.place, bf16[4096,512]{1,0:T(8,128)(2,1)S(1)} %copy-done.3, ...), custom_call_target="tpu_custom_call" | custom-call | tf_op jit(solution)/shard_map/pallas_call | solution.py:442
  110.9 1.7 collective-permute-start.6
  112.6 2.6 %collective-permute-start.2 = (bf16[1024,512]{1,0:T(8,128)(2,1)}, bf16[1024,512]{1,0:T(8,128)(2,1)}, u32[]{:S(2)}, u32[]{:S(2)}) collective-permute-start(bf16[1024,512]{1,0:T(8,128)(2,1)} %get-tuple-element.45), channel_id=1, source_target_pairs={{0,32},{1,97},{2,34},{3,99},{4,36},{5,101},{6,38},{7,103},{8,40},{... | collective-permute-start | bytes 3145736 | tf_op jit(solution)/shard_map/ppermute | solution.py:231
  115.2 6.3 %shard_map.148 = (bf16[1024,512]{1,0:T(8,128)(2,1)S(1)}, bf16[2,256,512]{2,1,0:T(8,128)(2,1)S(1)}, bf16[2,256,512]{2,1,0:T(8,128)(2,1)S(1)}, bf16[2,4,64,512]{3,...) custom-call(s32[5]{0:T(128)S(1)} %stack.47.place, bf16[4096,512]{1,0:T(8,128)(2,1)S(1)} %copy-done.3, ...), custom_call_target="tpu_custom_call" | custom-call | tf_op jit(solution)/shard_map/pallas_call | solution.py:442
  121.5 0.8 copy-done.12
  122.3 0.8 copy-done.17
  123.1 0.8 copy-done.20
  123.9 3.2 %collective-permute-start.9 = (bf16[2,4,64,512]{3,2,1,0:T(8,128)(2,1)}, bf16[2,4,64,512]{3,2,1,0:T(8,128)(2,1)S(1)}, u32[]{:S(2)}, u32[]{:S(2)}) collective-permute-start(bf16[2,4,64,512]{3,2,1,0:T(8,128)(2,1)} %get-tuple-element.51), channel_id=1, source_target_pairs={{0,2},{1,7},{2,0},{3,5},{4,6},{5,3},{6,4},{7,1},{8,10},{9,15},{10,... | collective-permute-start | bytes 1572872 | tf_op jit(solution)/shard_map/ppermute | solution.py:231
  127.1 0.2 collective-permute-start.5
  127.4 1.3 add_convert_fusion
  128.7 0.4 collective-permute-start.7
  129.1 4.8 %collective-permute-done.9 = bf16[2,4,64,512]{3,2,1,0:T(8,128)(2,1)S(1)} collective-permute-done((bf16[2,4,64,512]{3,2,1,0:T(8,128)(2,1)}, bf16[2,4,64,512]{3,2,1,0:T(8,128)(2,1)S(1)}, u32[]{:S(2)}, u32[]{:S(2)}) %collective-permute-start.9) | collective-permute-done | bytes 524320 | tf_op jit(solution)/shard_map/ppermute | solution.py:231
  133.9 1.2 fusion.2
  135.1 4.4 %collective-permute-done.10 = bf16[2,4,64,512]{3,2,1,0:T(8,128)(2,1)S(1)} collective-permute-done((bf16[2,4,64,512]{3,2,1,0:T(8,128)(2,1)}, bf16[2,4,64,512]{3,2,1,0:T(8,128)(2,1)S(1)}, u32[]{:S(2)}, u32[]{:S(2)}) %collective-permute-start.10) | collective-permute-done | bytes 524320 | tf_op jit(solution)/shard_map/ppermute | solution.py:231
  139.5 1.2 fusion.1
  140.8 0.3 collective-permute-start.11
  141.1 1.7 add_convert_fusion.3
  142.8 2.8 %collective-permute-start.3 = (bf16[2,4,2,32,512]{4,3,2,1,0:T(8,128)(2,1)S(1)}, bf16[2,4,2,32,512]{4,3,2,1,0:T(8,128)(2,1)S(1)}, u32[]{:S(2)}, u32[]{:S(2)}) collective-permute-start(bf16[2,4,2,32,512]{4,3,2,1,0:T(8,128)(2,1)S(1)} %get-tuple-element.63), channel_id=1, source_target_pairs={{0,2},{1,7},{2,0},{3,5},{4,6},{5,3},{6,4},{7,1},{8,10},{9,15},{10,... | collective-permute-start | bytes 1572872 | tf_op jit(solution)/shard_map/ppermute | solution.py:231
  145.6 0.1 add_convert_fusion.1
  145.7 0.1 add_convert_fusion.8
  145.9 0.1 collective-permute-start.8
  146.0 4.1 %collective-permute-done.11 = bf16[2,2,2,2,32,512]{5,4,3,2,1,0:T(8,128)(2,1)S(1)} collective-permute-done((bf16[2,2,2,2,32,512]{5,4,3,2,1,0:T(8,128)(2,1)S(1)}, bf16[2,2,2,2,32,512]{5,4,3,2,1,0:T(8,128)(2,1)S(1)}, u32[]{:S(2)}, u32[]{:S(2)}) %collective-permute-start.11) | collective-permute-done | bytes 524320 | tf_op jit(solution)/shard_map/ppermute | solution.py:231
  150.1 0.9 fusion
  151.1 1.0 collective-permute-done.3
  152.1 0.9 add_convert_fusion.9
  153.0 2.5 %collective-permute-start.4 = (bf16[2,2,2,32,512]{4,3,2,1,0:T(8,128)(2,1)}, bf16[2,2,2,32,512]{4,3,2,1,0:T(8,128)(2,1)S(1)}, u32[]{:S(2)}, u32[]{:S(2)}) collective-permute-start(bf16[2,2,2,32,512]{4,3,2,1,0:T(8,128)(2,1)} %get-tuple-element.66), channel_id=1, source_target_pairs={{0,8},{1,25},{2,10},{3,27},{4,12},{5,29},{6,14},{7,31},{8,0},{9,17... | collective-permute-start | bytes 786440 | tf_op jit(solution)/shard_map/ppermute | solution.py:231
  155.5 2.2 %collective-permute-done.12.r2 = bf16[2,2,2,32,512]{4,3,2,1,0:T(8,128)(2,1)S(1)} collective-permute-done((bf16[2,2,2,32,512]{4,3,2,1,0:T(8,128)(2,1)}, bf16[2,2,2,32,512]{4,3,2,1,0:T(8,128)(2,1)S(1)}, u32[]{:S(2)}, u32[]{:S(2)}) %collective-permute-start.12) | collective-permute-done | bytes 262176 | tf_op jit(solution)/shard_map/ppermute | solution.py:231
  157.7 1.9 collective-permute-done.4.r0
  159.6 0.7 deal.1
  160.3 0.1 collective-permute-start.19
  160.4 1.2 collective-permute-start.18
  161.6 2.0 %collective-permute-start.17 = (bf16[32,1536]{1,0:T(8,128)(2,1)S(1)}, bf16[32,1536]{1,0:T(8,128)(2,1)S(1)}, u32[]{:S(2)}, u32[]{:S(2)}) collective-permute-start(bf16[32,1536]{1,0:T(8,128)(2,1)S(1)} %get-tuple-element.59), channel_id=1, source_target_pairs={{0,102},{1,35},{2,100},{3,33},{4,98},{5,39},{6,96},{7,37},{8,110},... | collective-permute-start | bytes 294920 | tf_op jit(solution)/shard_map/ppermute | solution.py:231
  163.6 1.5 collective-permute-start.16
  165.1 0.6 collective-permute-done.19
  165.7 2.0 %collective-permute-start.13 = (bf16[32,1536]{1,0:T(8,128)(2,1)S(1)}, bf16[32,1536]{1,0:T(8,128)(2,1)S(1)}, u32[]{:S(2)}, u32[]{:S(2)}) collective-permute-start(bf16[32,1536]{1,0:T(8,128)(2,1)S(1)} %get-tuple-element.55), channel_id=1, source_target_pairs={{0,6},{1,3},{2,4},{3,1},{4,2},{5,7},{6,0},{7,5},{8,14},{9,11},{10,... | collective-permute-start | bytes 294920 | tf_op jit(solution)/shard_map/ppermute | solution.py:231
  167.8 24.9 %all_to_all.28 = f32[128,1,8]{2,1,0:T(1,128)} all-to-all(f32[128,1,8]{2,1,0:T(1,128)S(1)} %bitcast.58), channel_id=1, replica_groups=mesh['dev'=128] {'dev'}, dimensions={0} | all-to-all | bytes 8192 | tf_op jit(solution)/shard_map/all_to_all | solution.py:473
  192.6 2.2 %returned.1 = f32[4,128]{1,0:T(4,128)} custom-call(f32[128,8]{1,0:T(8,128)} %bitcast.66, s32[4,128]{1,0:T(4,128)} %bitcast.69, s32[4,128]{1,0:T(4,128)} %get-tuple-element.43.brank), custom_call_target="tpu_custom_call" | custom-call | tf_op jit(solution)/shard_map/returned/pallas_call | solution.py:474
  194.8 0.1 convert_add_fusion.4
  194.9 0.7 slice.33
  195.6 0.6 slice.34
  (67 shorter events, 0.5 us)
Async XLA Ops:
  23.5 10.6 %copy-start.27 = (s32[16,8]{0,1:T(8,128)S(1)}, s32[16,8]{0,1:T(8,128)}, u32[]{:S(2)}) copy-start(s32[16,8]{0,1:T(8,128)} %param.16) | copy-start | bytes 1540
  23.5 10.8 %copy-start.25 = (s32[2048]{0:T(1024)S(1)}, s32[2048]{0:T(1024)}, u32[]{:S(2)}) copy-start(s32[2048]{0:T(1024)} %param.13) | copy-start | bytes 24580
  23.5 10.8 %copy-start.26 = (s32[2048]{0:T(1024)S(1)}, s32[2048]{0:T(1024)}, u32[]{:S(2)}) copy-start(s32[2048]{0:T(1024)} %param.14) | copy-start | bytes 24580
  28.3 41.9 %all-to-all-start.1 = ((bf16[128,4,512]{2,1,0:T(4,128)(2,1)}), bf16[128,4,512]{2,1,0:T(4,128)(2,1)}, u32[]{:S(2)}, u32[]{:S(2)}) async-start(bf16[128,4,512]{2,1,0:T(4,128)(2,1)} %reshape.91), calls=%async_computation.1 | async-start | bytes 1048576 | tf_op jit(solution)/shard_map/all_to_all | solution.py:335
  34.4 2.2 %copy-start.5 = (bf16[2048,1024]{1,0:T(8,128)(2,1)S(1)}, bf16[2048,1024]{1,0:T(8,128)(2,1)}, u32[]{:S(2)}) copy-start(bf16[2048,1024]{1,0:T(8,128)(2,1)} %features.1) | copy-start | bytes 12582916
  36.6 2.2 %copy-start.6 = (bf16[4096,512]{1,0:T(8,128)(2,1)S(1)}, bf16[4096,512]{1,0:T(8,128)(2,1)}, u32[]{:S(2)}) copy-start(bf16[4096,512]{1,0:T(8,128)(2,1)} %param.23) | copy-start | bytes 12582916
  38.8 32.6 %copy-start.19 = (s32[2,128]{1,0:T(2,128)S(1)}, s32[2,128]{1,0:T(2,128)}, u32[]{:S(2)}) copy-start(s32[2,128]{1,0:T(2,128)} %get-tuple-element.34.hslot) | copy-start | bytes 3076
  66.8 2.1 %copy-start.1 = (bf16[4096,512]{1,0:T(8,128)(2,1)}, bf16[4096,512]{1,0:T(8,128)(2,1)S(1)}, u32[]{:S(2)}) copy-start(bf16[4096,512]{1,0:T(8,128)(2,1)S(1)} %get-tuple-element.37.w_out) | copy-start | bytes 12582916
  68.9 1.3 copy-start.10
  71.4 1.6 copy-start.4
  73.0 2.2 %copy-start.7 = (bf16[16,8,128,128]{3,2,1,0:T(8,128)(2,1)S(1)}, bf16[16,8,128,128]{3,2,1,0:T(8,128)(2,1)}, u32[]{:S(2)}) copy-start(bf16[16,8,128,128]{3,2,1,0:T(8,128)(2,1)} %weights.1) | copy-start | bytes 12582916
  75.2 1.6 copy-start.11
  76.8 9.0 %copy-start = (bf16[4096,1024]{1,0:T(8,128)(2,1)S(1)}, bf16[4096,1024]{1,0:T(8,128)(2,1)}, u32[]{:S(2)}) copy-start(bf16[4096,1024]{1,0:T(8,128)(2,1)} %get-tuple-element.38.hidden) | copy-start | bytes 25165828
  85.8 2.2 %copy-start.2 = (bf16[4096,512]{1,0:T(8,128)(2,1)S(1)}, bf16[4096,512]{1,0:T(8,128)(2,1)}, u32[]{:S(2)}) copy-start(bf16[4096,512]{1,0:T(8,128)(2,1)} %copy-done.1) | copy-start | bytes 12582916
  93.4 8.9 %copy-start.3 = (bf16[4096,512]{1,0:T(8,128)(2,1)S(1)}, bf16[4096,512]{1,0:T(8,128)(2,1)}, u32[]{:S(2)}) copy-start(bf16[4096,512]{1,0:T(8,128)(2,1)} %copy-done.1) | copy-start | bytes 12582916
  93.4 7.2 %collective-permute-start.1 = (bf16[1024,1536]{1,0:T(8,128)(2,1)S(1)}, bf16[1024,1536]{1,0:T(8,128)(2,1)S(1)}, u32[]{:S(2)}, u32[]{:S(2)}) collective-permute-start(bf16[1024,1536]{1,0:T(8,128)(2,1)S(1)} %shard_map.149), channel_id=1, source_target_pairs={{0,1},{1,0},{2,3},{3,2},{4,5},{5,4},{6,7},{7,6},{8,9},{9,8},{10,11... | collective-permute-start | bytes 9437192 | tf_op jit(solution)/shard_map/ppermute | solution.py:430
  100.6 14.6 %collective-permute-start = (bf16[1024,1536]{1,0:T(8,128)(2,1)S(1)}, bf16[1024,1536]{1,0:T(8,128)(2,1)S(1)}, u32[]{:S(2)}, u32[]{:S(2)}) collective-permute-start(bf16[1024,1536]{1,0:T(8,128)(2,1)S(1)} %shard_map.147), channel_id=1, source_target_pairs={{0,1},{1,0},{2,3},{3,2},{4,5},{5,4},{6,7},{7,6},{8,9},{9,8},{10,11... | collective-permute-start | bytes 9437192 | tf_op jit(solution)/shard_map/ppermute | solution.py:430
  100.7 1.6 copy-start.8
  102.3 1.9 copy-start.9
  110.8 10.7 %copy-start.14 = (bf16[2,256,512]{2,1,0:T(8,128)(2,1)}, bf16[2,256,512]{2,1,0:T(8,128)(2,1)S(1)}, u32[]{:S(2)}) copy-start(bf16[2,256,512]{2,1,0:T(8,128)(2,1)S(1)} %get-tuple-element.48) | copy-start | bytes 1572868
  110.8 10.7 %copy-start.15 = (bf16[2,4,64,512]{3,2,1,0:T(8,128)(2,1)}, bf16[2,4,64,512]{3,2,1,0:T(8,128)(2,1)S(1)}, u32[]{:S(2)}) copy-start(bf16[2,4,64,512]{3,2,1,0:T(8,128)(2,1)S(1)} %get-tuple-element.52) | copy-start | bytes 1572868
  110.9 16.5 %collective-permute-start.6 = (bf16[2,256,512]{2,1,0:T(8,128)(2,1)}, bf16[2,256,512]{2,1,0:T(8,128)(2,1)}, u32[]{:S(2)}, u32[]{:S(2)}) collective-permute-start(bf16[2,256,512]{2,1,0:T(8,128)(2,1)} %get-tuple-element.49), channel_id=1, source_target_pairs={{0,8},{1,25},{2,10},{3,27},{4,12},{5,29},{6,14},{7,31},{8,0},{9,17... | collective-permute-start | bytes 1572872 | tf_op jit(solution)/shard_map/ppermute | solution.py:231
  112.6 28.5 %collective-permute-start.2 = (bf16[1024,512]{1,0:T(8,128)(2,1)}, bf16[1024,512]{1,0:T(8,128)(2,1)}, u32[]{:S(2)}, u32[]{:S(2)}) collective-permute-start(bf16[1024,512]{1,0:T(8,128)(2,1)} %get-tuple-element.45), channel_id=1, source_target_pairs={{0,32},{1,97},{2,34},{3,99},{4,36},{5,101},{6,38},{7,103},{8,40},{... | collective-permute-start | bytes 3145736 | tf_op jit(solution)/shard_map/ppermute | solution.py:231
  121.5 0.8 copy-start.12
  122.3 0.8 copy-start.17
  123.1 0.8 copy-start.20
  123.9 10.0 %collective-permute-start.9 = (bf16[2,4,64,512]{3,2,1,0:T(8,128)(2,1)}, bf16[2,4,64,512]{3,2,1,0:T(8,128)(2,1)S(1)}, u32[]{:S(2)}, u32[]{:S(2)}) collective-permute-start(bf16[2,4,64,512]{3,2,1,0:T(8,128)(2,1)} %get-tuple-element.51), channel_id=1, source_target_pairs={{0,2},{1,7},{2,0},{3,5},{4,6},{5,3},{6,4},{7,1},{8,10},{9,15},{10,... | collective-permute-start | bytes 1572872 | tf_op jit(solution)/shard_map/ppermute | solution.py:231
  127.1 12.4 %collective-permute-start.10 = (bf16[2,4,64,512]{3,2,1,0:T(8,128)(2,1)}, bf16[2,4,64,512]{3,2,1,0:T(8,128)(2,1)S(1)}, u32[]{:S(2)}, u32[]{:S(2)}) collective-permute-start(bf16[2,4,64,512]{3,2,1,0:T(8,128)(2,1)} %get-tuple-element.53), channel_id=1, source_target_pairs={{0,2},{1,7},{2,0},{3,5},{4,6},{5,3},{6,4},{7,1},{8,10},{9,15},{10,... | collective-permute-start | bytes 1572872 | tf_op jit(solution)/shard_map/ppermute | solution.py:231
  127.1 18.4 %collective-permute-start.5 = (bf16[2,256,512]{2,1,0:T(8,128)(2,1)}, bf16[2,256,512]{2,1,0:T(8,128)(2,1)S(1)}, u32[]{:S(2)}, u32[]{:S(2)}) collective-permute-start(bf16[2,256,512]{2,1,0:T(8,128)(2,1)} %copy-done.20), channel_id=1, source_target_pairs={{0,8},{1,25},{2,10},{3,27},{4,12},{5,29},{6,14},{7,31},{8,0},{9,17... | collective-permute-start | bytes 1572872 | tf_op jit(solution)/shard_map/ppermute | solution.py:231
  128.7 16.8 %copy-start.13 = (bf16[2,256,512]{2,1,0:T(8,128)(2,1)S(1)}, bf16[2,256,512]{2,1,0:T(8,128)(2,1)}, u32[]{:S(2)}) copy-start(bf16[2,256,512]{2,1,0:T(8,128)(2,1)} %copy-done.12) | copy-start | bytes 1572868
  128.7 17.0 %collective-permute-start.7 = (bf16[2,2,4,32,512]{4,3,2,1,0:T(8,128)(2,1)S(1)}, bf16[2,2,4,32,512]{4,3,2,1,0:T(8,128)(2,1)S(1)}, u32[]{:S(2)}, u32[]{:S(2)}) collective-permute-start(bf16[2,2,4,32,512]{4,3,2,1,0:T(8,128)(2,1)S(1)} %bitcast.61), channel_id=1, source_target_pairs={{0,32},{1,97},{2,34},{3,99},{4,36},{5,101},{6,38},{7,103},{8,40},{... | collective-permute-start | bytes 1572872 | tf_op jit(solution)/shard_map/ppermute | solution.py:231
  133.9 7.2 %copy-start.21 = (bf16[2,4,64,512]{3,2,1,0:T(8,128)(2,1)}, bf16[2,4,64,512]{3,2,1,0:T(8,128)(2,1)S(1)}, u32[]{:S(2)}) copy-start(bf16[2,4,64,512]{3,2,1,0:T(8,128)(2,1)S(1)} %collective-permute-done.9) | copy-start | bytes 1572868
  139.5 3.3 %copy-start.23 = (bf16[2,4,64,512]{3,2,1,0:T(8,128)(2,1)}, bf16[2,4,64,512]{3,2,1,0:T(8,128)(2,1)S(1)}, u32[]{:S(2)}) copy-start(bf16[2,4,64,512]{3,2,1,0:T(8,128)(2,1)S(1)} %collective-permute-done.10) | copy-start | bytes 1572868
  140.8 9.3 %collective-permute-start.11 = (bf16[2,2,2,2,32,512]{5,4,3,2,1,0:T(8,128)(2,1)S(1)}, bf16[2,2,2,2,32,512]{5,4,3,2,1,0:T(8,128)(2,1)S(1)}, u32[]{:S(2)}, u32[]{:S(2)}) collective-permute-start(bf16[2,2,2,2,32,512]{5,4,3,2,1,0:T(8,128)(2,1)S(1)} %pad_maximum_fusion), channel_id=1, source_target_pairs={{0,8},{1,25},{2,10},{3,27},{4,12},{5,29},{6,14},{7,31},{8,0},{9,17... | collective-permute-start | bytes 1572872 | tf_op jit(solution)/shard_map/ppermute | solution.py:231
  141.1 9.0 %copy-start.16 = (bf16[2,4,64,512]{3,2,1,0:T(8,128)(2,1)S(1)}, bf16[2,4,64,512]{3,2,1,0:T(8,128)(2,1)}, u32[]{:S(2)}) copy-start(bf16[2,4,64,512]{3,2,1,0:T(8,128)(2,1)} %copy-done.15) | copy-start | bytes 1572868
  141.1 9.0 %copy-start.18 = (bf16[2,4,64,512]{3,2,1,0:T(8,128)(2,1)S(1)}, bf16[2,4,64,512]{3,2,1,0:T(8,128)(2,1)}, u32[]{:S(2)}) copy-start(bf16[2,4,64,512]{3,2,1,0:T(8,128)(2,1)} %copy-done.17) | copy-start | bytes 1572868
  141.1 9.0 %copy-start.22 = (bf16[2,4,64,512]{3,2,1,0:T(8,128)(2,1)S(1)}, bf16[2,4,64,512]{3,2,1,0:T(8,128)(2,1)}, u32[]{:S(2)}) copy-start(bf16[2,4,64,512]{3,2,1,0:T(8,128)(2,1)} %copy-done.21) | copy-start | bytes 1572868
  142.8 7.3 %copy-start.24 = (bf16[2,4,64,512]{3,2,1,0:T(8,128)(2,1)S(1)}, bf16[2,4,64,512]{3,2,1,0:T(8,128)(2,1)}, u32[]{:S(2)}) copy-start(bf16[2,4,64,512]{3,2,1,0:T(8,128)(2,1)} %copy-done.23) | copy-start | bytes 1572868
  142.8 9.3 %collective-permute-start.3 = (bf16[2,4,2,32,512]{4,3,2,1,0:T(8,128)(2,1)S(1)}, bf16[2,4,2,32,512]{4,3,2,1,0:T(8,128)(2,1)S(1)}, u32[]{:S(2)}, u32[]{:S(2)}) collective-permute-start(bf16[2,4,2,32,512]{4,3,2,1,0:T(8,128)(2,1)S(1)} %get-tuple-element.63), channel_id=1, source_target_pairs={{0,2},{1,7},{2,0},{3,5},{4,6},{5,3},{6,4},{7,1},{8,10},{9,15},{10,... | collective-permute-start | bytes 1572872 | tf_op jit(solution)/shard_map/ppermute | solution.py:231
  145.9 9.7 %collective-permute-start.8 = (bf16[2,2,2,32,512]{4,3,2,1,0:T(8,128)(2,1)S(1)}, bf16[2,2,2,32,512]{4,3,2,1,0:T(8,128)(2,1)S(1)}, u32[]{:S(2)}, u32[]{:S(2)}) collective-permute-start(bf16[2,2,2,32,512]{4,3,2,1,0:T(8,128)(2,1)S(1)} %get-tuple-element.64), channel_id=1, source_target_pairs={{0,2},{1,7},{2,0},{3,5},{4,6},{5,3},{6,4},{7,1},{8,10},{9,15},{10,... | collective-permute-start | bytes 786440 | tf_op jit(solution)/shard_map/ppermute | solution.py:231
  151.1 6.6 %collective-permute-start.12 = (bf16[2,2,2,32,512]{4,3,2,1,0:T(8,128)(2,1)}, bf16[2,2,2,32,512]{4,3,2,1,0:T(8,128)(2,1)S(1)}, u32[]{:S(2)}, u32[]{:S(2)}) collective-permute-start(bf16[2,2,2,32,512]{4,3,2,1,0:T(8,128)(2,1)} %get-tuple-element.68), channel_id=1, source_target_pairs={{0,32},{1,97},{2,34},{3,99},{4,36},{5,101},{6,38},{7,103},{8,40},{... | collective-permute-start | bytes 786440 | tf_op jit(solution)/shard_map/ppermute | solution.py:231
  153.0 6.6 %collective-permute-start.4 = (bf16[2,2,2,32,512]{4,3,2,1,0:T(8,128)(2,1)}, bf16[2,2,2,32,512]{4,3,2,1,0:T(8,128)(2,1)S(1)}, u32[]{:S(2)}, u32[]{:S(2)}) collective-permute-start(bf16[2,2,2,32,512]{4,3,2,1,0:T(8,128)(2,1)} %get-tuple-element.66), channel_id=1, source_target_pairs={{0,8},{1,25},{2,10},{3,27},{4,12},{5,29},{6,14},{7,31},{8,0},{9,17... | collective-permute-start | bytes 786440 | tf_op jit(solution)/shard_map/ppermute | solution.py:231
  160.3 5.4 %collective-permute-start.19 = (bf16[32,1536]{1,0:T(8,128)(2,1)S(1)}, bf16[32,1536]{1,0:T(8,128)(2,1)S(1)}, u32[]{:S(2)}, u32[]{:S(2)}) collective-permute-start(bf16[32,1536]{1,0:T(8,128)(2,1)S(1)} %get-tuple-element.61), channel_id=1, source_target_pairs={{0,126},{1,43},{2,124},{3,41},{4,122},{5,47},{6,120},{7,45},{8,118... | collective-permute-start | bytes 294920 | tf_op jit(solution)/shard_map/ppermute | solution.py:231
  160.4 5.3 %collective-permute-start.18 = (bf16[32,1536]{1,0:T(8,128)(2,1)S(1)}, bf16[32,1536]{1,0:T(8,128)(2,1)S(1)}, u32[]{:S(2)}, u32[]{:S(2)}) collective-permute-start(bf16[32,1536]{1,0:T(8,128)(2,1)S(1)} %get-tuple-element.60), channel_id=1, source_target_pairs={{0,120},{1,41},{2,122},{3,43},{4,124},{5,45},{6,126},{7,47},{8,112... | collective-permute-start | bytes 294920 | tf_op jit(solution)/shard_map/ppermute | solution.py:231
  161.6 33.2 %collective-permute-start.17 = (bf16[32,1536]{1,0:T(8,128)(2,1)S(1)}, bf16[32,1536]{1,0:T(8,128)(2,1)S(1)}, u32[]{:S(2)}, u32[]{:S(2)}) collective-permute-start(bf16[32,1536]{1,0:T(8,128)(2,1)S(1)} %get-tuple-element.59), channel_id=1, source_target_pairs={{0,102},{1,35},{2,100},{3,33},{4,98},{5,39},{6,96},{7,37},{8,110},... | collective-permute-start | bytes 294920 | tf_op jit(solution)/shard_map/ppermute | solution.py:231
  163.6 31.2 %collective-permute-start.16 = (bf16[32,1536]{1,0:T(8,128)(2,1)S(1)}, bf16[32,1536]{1,0:T(8,128)(2,1)S(1)}, u32[]{:S(2)}, u32[]{:S(2)}) collective-permute-start(bf16[32,1536]{1,0:T(8,128)(2,1)S(1)} %get-tuple-element.58), channel_id=1, source_target_pairs={{0,96},{1,33},{2,98},{3,35},{4,100},{5,37},{6,102},{7,39},{8,104},... | collective-permute-start | bytes 294920 | tf_op jit(solution)/shard_map/ppermute | solution.py:231
  165.1 29.7 %collective-permute-start.15 = (bf16[32,1536]{1,0:T(8,128)(2,1)S(1)}, bf16[32,1536]{1,0:T(8,128)(2,1)S(1)}, u32[]{:S(2)}, u32[]{:S(2)}) collective-permute-start(bf16[32,1536]{1,0:T(8,128)(2,1)S(1)} %get-tuple-element.57), channel_id=1, source_target_pairs={{0,30},{1,11},{2,28},{3,9},{4,26},{5,15},{6,24},{7,13},{8,22},{9,3... | collective-permute-start | bytes 294920 | tf_op jit(solution)/shard_map/ppermute | solution.py:231
  165.7 29.1 %collective-permute-start.14 = (bf16[32,1536]{1,0:T(8,128)(2,1)S(1)}, bf16[32,1536]{1,0:T(8,128)(2,1)S(1)}, u32[]{:S(2)}, u32[]{:S(2)}) collective-permute-start(bf16[32,1536]{1,0:T(8,128)(2,1)S(1)} %get-tuple-element.56), channel_id=1, source_target_pairs={{0,24},{1,9},{2,26},{3,11},{4,28},{5,13},{6,30},{7,15},{8,16},{9,1... | collective-permute-start | bytes 294920 | tf_op jit(solution)/shard_map/ppermute | solution.py:231
  165.7 29.1 %collective-permute-start.13 = (bf16[32,1536]{1,0:T(8,128)(2,1)S(1)}, bf16[32,1536]{1,0:T(8,128)(2,1)S(1)}, u32[]{:S(2)}, u32[]{:S(2)}) collective-permute-start(bf16[32,1536]{1,0:T(8,128)(2,1)S(1)} %get-tuple-element.55), channel_id=1, source_target_pairs={{0,6},{1,3},{2,4},{3,1},{4,2},{5,7},{6,0},{7,5},{8,14},{9,11},{10,... | collective-permute-start | bytes 294920 | tf_op jit(solution)/shard_map/ppermute | solution.py:231
where the time goes:
time: 197 us; the launch traced here: 196 us
  Pallas kernels  65.6 us (33%)
  blocking collectives  45.7 us (23%)
  local copies, waits for them, and re-layouts  28.8 us (15%)
  starting transfers between devices  28.2 us (14%)
  waiting for transfers between devices  19.1 us (10%)
  other arithmetic  7.68 us (4%)
    pallas_call x1, Pallas kernels, on_device(): pl.pallas_call(forward_kernel, grid=(hid // HBLK,), in_specs=[smem, once(...  28.1 us
    all_to_all x1, blocking collectives, on_device(): lax.all_to_all(errors_out[:, :BATCH_SLOTS], DEV, 0, 0, tiled=True)  24.9 us
    unnamed x57, local copies, waits for them, and re-layouts  21.3 us
    all_to_all x1, blocking collectives, on_device(): lax.all_to_all(table[:, :HALO_SLOTS + BATCH_SLOTS], DEV, 0, 0, tiled=True)  20.9 us
    ppermute x18, starting transfers between devices, exchange(): return lax.ppermute(x, DEV, pairing(level, dims))  20.7 us
    ppermute x18, waiting for transfers between devices, exchange(): return lax.ppermute(x, DEV, pairing(level, dims))  19.1 us
    pallas_call x2, Pallas kernels, own_part(): pl.pallas_call(own_kernel, grid_spec=pltpu.PrefetchScalarGridSpec(num_sca...  13 us
    pallas_call x2, Pallas kernels, peer_part(): pl.pallas_call(peer_kernel, grid_spec=pltpu.PrefetchScalarGridSpec(num_sc...  10.8 us
  transfers between devices with their start and end apart: 21, of which 7 were waited for; matrix products, arithmetic and copies ran while one was open for 4% of the time, Pallas kernels for 25%

commit v1 on v0

--- a/solution.py
+++ b/solution.py
@@ -19,6 +19,10 @@
 
 def params(mib=48, **more):
     return pltpu.CompilerParams(vmem_limit_bytes=mib * 2**20, **more)
+
+
+def in_hbm(x):
+    return pltpu.with_memory_space_constraint(x, pltpu.HBM)
 
 
 def dot(left, right, dims):
@@ -83,7 +87,7 @@
         onehot[s * LANES : (s + 1) * LANES, :] = (node == wanted).astype(F32).astype(BF)
 
 
-def forward_kernel(place, table, features, w_in, w_out, x, hidden, logits, w_out_to, onehot, acc, in_buf, out_buf, in_sem, out_sem):
+def forward_kernel(place, table, features, w_in, w_out, x, hidden, logits, w_out_to, onehot, acc, nodes_x, in_buf, out_buf, nodes_sem, in_sem, out_sem):
     step = pl.program_id(0)
     steps = pl.num_programs(0)
     chunks = HBLK // UNITS
@@ -103,9 +107,12 @@
 
     @pl.when(step == 0)
     def _():
+        whole = pltpu.make_async_copy(features, nodes_x, nodes_sem)
+        whole.start()
         fetch(0, 0)
         pick_rows(table, HALO_SLOTS, BATCH_SLOTS, features.shape[0], onehot)
-        x[...] = dot(onehot[...], features[...], (1, 0)).astype(BF)
+        whole.wait()
+        x[...] = dot(onehot[...], nodes_x[...], (1, 0)).astype(BF)
         acc[...] = jnp.zeros(acc.shape, F32)
 
     slot = step % 2
@@ -127,13 +134,16 @@
         logits[...] = acc[...].T
 
 
-def spread_kernel(cols, weights, prior, halo, hslot, given, table, logits, prop, residue, errors, halo_tab, prop_all, onehot):
+def spread_kernel(cols, weights, prior, halo, hslot, given, table, logits_far, prop, residue, errors, halo_tab, prop_all, onehot, logits, sem):
     step = pl.program_id(0)
     per = weights.shape[0]
     classes = prior.shape[1]
 
+    fetch = pltpu.make_async_copy(logits_far, logits, sem)
+
     @pl.when(step == 0)
     def _():
+        fetch.start()
         slots = halo.shape[0]
         slot = lax.broadcasted_iota(jnp.int32, (slots, LANES), 0)
         for b in range(2):
@@ -168,9 +178,13 @@
         pick_rows(table, HALO_SLOTS, BATCH_SLOTS, prop_all.shape[0], onehot)
         lane = lax.broadcasted_iota(jnp.int32, (LANES, LANES), 1)
         out = jnp.zeros((LANES, LANES), F32)
+        fetch.wait()
+        tall = 512
         for s in range(BATCH_SLOTS):
             at = slice(s * LANES, (s + 1) * LANES)
-            log_z = jnp.log(dot(onehot[at, :], prop_all[...], (1, 0)))
+            if s % 4 == 0:
+                picked = dot(onehot[s * LANES : s * LANES + tall, :], prop_all[...], (1, 0))
+            log_z = jnp.log(picked[s % 4 * LANES : (s % 4 + 1) * LANES])
             target = log_z - jnp.mean(log_z, axis=1, keepdims=True)
             valid = table[:, HALO_SLOTS + s : HALO_SLOTS + s + 1] >= 0
             differ = jnp.where(valid, logits[at, :] - target, 0.0)
@@ -231,26 +245,36 @@
     return lax.ppermute(x, DEV, pairing(level, dims))
 
 
-def deal_kernel(bits, k0, r0, k1, r1, k2, r2, own, *sends):
+def corners():
+    groups = []
+    for core in range(2):
+        for high in range(8):
+            group = []
+            for low in range(8):
+                shifted = [2 * ((high >> (2 - d)) & 1) + ((low >> (2 - d)) & 1) for d in range(3)]
+                a, b, c = ((v + 1 - core) % 4 for v in shifted)
+                group.append(((a * 4 + b) * 4 + c) * 2 + core)
+            groups.append(group)
+    return groups
+
+
+def deal_kernel(k0, r0, k1, r1, k2, r2, pieces):
     for m in range(8):
-        a = bits[0] ^ (m >> 2)
-        b = bits[1] ^ ((m >> 1) & 1)
-        c = bits[2] ^ (m & 1)
+        at = (m >> 2, (m >> 1) & 1, m & 1)
         for j, (k, r) in enumerate(((k0, r0), (k1, r1), (k2, r2))):
-            piece = k[a, b, c].astype(F32) + r[a, b, c].astype(F32)
-            if m == 0:
-                own[:, j * 512 : (j + 1) * 512] = piece
-            else:
-                sends[m - 1][:, j * 512 : (j + 1) * 512] = piece.astype(BF)
-
-
-def summed_over_chips(first, second, halves, bits):
+            piece = k[at].astype(F32) + r[at].astype(F32)
+            pieces[m, :, j * 512 : (j + 1) * 512] = piece.astype(BF)
+
+
+def summed_over_chips(first, second, halves):
     shape_a, shape_b, shape_c = (2, 4, 4, UNITS, 512), (2, 2, 4, UNITS, 512), (2, 4, 2, UNITS, 512)
     send_a, send_b1, keep_b1, send_c1, keep_c1 = first
     keep_a, send_b2, keep_b2, send_c2, keep_c2 = second
+    got_c1 = exchange(send_c1, 1, (2,)).reshape(shape_c)
+    got_b1 = exchange(send_b1, 1, (1,)).reshape(shape_b)
     got_a = exchange(send_a, 1, (0,)).reshape(shape_a)
-    got_b1, got_b2 = (exchange(v, 1, (1,)).reshape(shape_b) for v in (send_b1, send_b2))
-    got_c1, got_c2 = (exchange(v, 1, (2,)).reshape(shape_c) for v in (send_c1, send_c2))
+    got_c2 = exchange(send_c2, 1, (2,)).reshape(shape_c)
+    got_b2 = exchange(send_b2, 1, (1,)).reshape(shape_b)
     keep_a = keep_a.reshape(shape_a)
     keep_b1, keep_b2 = keep_b1.reshape(shape_b), keep_b2.reshape(shape_b)
     keep_c1, keep_c2 = keep_c1.reshape(shape_c), keep_c2.reshape(shape_c)
@@ -278,19 +302,16 @@
     b = added(b, b_got, 2, hc)
     a = added(a, a_got, 1, hb)
     c = added(c2, c_got[1])
-    piece = jax.ShapeDtypeStruct((UNITS, 1536), BF)
-    own, *pieces = pl.pallas_call(
+    pieces = pl.pallas_call(
         deal_kernel,
-        in_specs=[pl.BlockSpec(memory_space=pltpu.SMEM)] + [pl.BlockSpec(memory_space=pltpu.VMEM)] * 6,
-        out_shape=[jax.ShapeDtypeStruct((UNITS, 1536), F32)] + [piece] * 7,
+        in_specs=[pl.BlockSpec(memory_space=pltpu.VMEM)] * 6,
+        out_specs=pl.BlockSpec(memory_space=pltpu.VMEM),
+        out_shape=jax.ShapeDtypeStruct((8, UNITS, 1536), BF),
         compiler_params=params(16),
         name="deal",
-    )(bits, a, a_last, b, b_last, c, c_last)
-    total = own
-    for m in range(1, 8):
-        dims = [d for d in range(3) if (m >> (2 - d)) & 1]
-        total = total + exchange(pieces[m - 1], 2, dims).astype(F32)
-    return total
+    )(a, a_last, b, b_last, c, c_last)
+    dealt = lax.all_to_all(pieces, DEV, 0, 0, axis_index_groups=corners(), tiled=True)
+    return jnp.sum(dealt.astype(F32), axis=0)
 
 
 def on_device(prior, label_class, labeled, features, tile_cols, tile_weights, halo_owner, halo_local, batch_owner, batch_local, w_in, w_out):
@@ -307,7 +328,6 @@
     halves = [s // 2 for s in spots]
     peer_half = (chip[0] + 4 - core) % 4 // 2
     place = jnp.stack([*halves, core, peer_half]).astype(jnp.int32)
-    bits = jnp.stack([s % 2 for s in spots]).astype(jnp.int32)
     vmem = pl.BlockSpec(memory_space=pltpu.VMEM)
     smem = pl.BlockSpec(memory_space=pltpu.SMEM)
     hbm = pl.BlockSpec(memory_space=pl.ANY)
@@ -348,25 +368,33 @@
     x, hidden, logits, w_out_o = pl.pallas_call(
         forward_kernel,
         grid=(hid // HBLK,),
-        in_specs=[smem, once((LANES, slots)), once((nodes, feat)), hbm, hbm],
+        in_specs=[smem, once((LANES, slots)), hbm, hbm, hbm],
         out_specs=[whole((rows, feat)), rows_at(0, rows), whole((rows, classes)), rows_at(0, classes)],
         out_shape=[
             jax.ShapeDtypeStruct((rows, feat), BF),
-            jax.ShapeDtypeStruct((hid, rows), BF),
-            jax.ShapeDtypeStruct((rows, classes), F32),
-            jax.ShapeDtypeStruct((hid, classes), BF),
+            pltpu.HBM((hid, rows), BF),
+            pltpu.HBM((rows, classes), F32),
+            pltpu.HBM((hid, classes), BF),
         ],
         scratch_shapes=[
             pltpu.VMEM((rows, nodes), BF),
             pltpu.VMEM((classes, rows), F32),
+            pltpu.VMEM((nodes, feat), BF),
             pltpu.VMEM((2, chunks, UNITS, feat), BF),
             pltpu.VMEM((2, chunks, UNITS, classes), BF),
+            pltpu.SemaphoreType.DMA,
             pltpu.SemaphoreType.DMA((2,)),
             pltpu.SemaphoreType.DMA((2,)),
         ],
         compiler_params=params(36),
         name="forward",
-    )(place, asked, features, w_in.reshape(128, UNITS, feat), w_out.reshape(128, UNITS, classes))
+    )(
+        place,
+        asked,
+        in_hbm(features),
+        in_hbm(w_in.reshape(128, UNITS, feat)),
+        in_hbm(w_out.reshape(128, UNITS, classes)),
+    )
 
     row_tiles = tile_weights.shape[0]
     per = 2
@@ -382,7 +410,7 @@
             once((halo_count // LANES, LANES)),
             once((row_tiles, LANES)),
             once((LANES, slots)),
-            once((rows, classes)),
+            hbm,
         ],
         out_specs=[
             pl.BlockSpec((per * LANES, classes), lambda i: (i, 0)),
@@ -398,10 +426,12 @@
             pltpu.VMEM((halo_count, classes), BF),
             pltpu.VMEM((nodes, classes), BF),
             pltpu.VMEM((rows, nodes), BF),
+            pltpu.VMEM((rows, classes), F32),
+            pltpu.SemaphoreType.DMA,
         ],
         compiler_params=params(24),
         name="spread",
-    )(tile_cols, tile_weights, prior, halo, hslot, given, asked, logits)
+    )(tile_cols, in_hbm(tile_weights), in_hbm(prior), halo, hslot, given, asked, in_hbm(logits))
 
     partner = [(d, d ^ 1) for d in range(128)]
     part_rows = 2 * HBLK
@@ -426,13 +456,13 @@
             ),
             out_shape=jax.ShapeDtypeStruct((part_rows, classes + feat), BF),
             compiler_params=params(24),
-        )(place, w_out_o, hidden, residue, x)
+        )(place, in_hbm(w_out_o), in_hbm(hidden), residue, x)
         return lax.ppermute(grad, DEV, partner)
 
     b_spec = pl.BlockSpec((1, 256, 512), lambda i, p: (i, 0, 0))
     c_spec = pl.BlockSpec((1, 4, 64, 512), lambda i, p: (i, 0, 0, 0))
-    b_shape = jax.ShapeDtypeStruct((2, 256, 512), BF)
-    c_shape = jax.ShapeDtypeStruct((2, 4, 64, 512), BF)
+    b_shape = pltpu.HBM((2, 256, 512), BF)
+    c_shape = pltpu.HBM((2, 4, 64, 512), BF)
 
     def own_part(part, arrived):
         def block(i, p):
@@ -455,7 +485,7 @@
                 out_specs=[rows_at(0, classes), b_spec, b_spec, c_spec, c_spec, whole((LANES, LANES))],
             ),
             out_shape=[
-                jax.ShapeDtypeStruct((part_rows, classes), BF),
+                pltpu.HBM((part_rows, classes), BF),
                 b_shape,
                 b_shape,
                 c_shape,
@@ -463,12 +493,12 @@
                 jax.ShapeDtypeStruct((LANES, LANES), F32),
             ],
             compiler_params=params(28),
-        )(place, w_out_o, hidden, residue, x, arrived, errors)
+        )(place, in_hbm(w_out_o), in_hbm(hidden), residue, x, arrived, errors)
 
     arrived = [peer_part(0), peer_part(1)]
     *first, _ = own_part(0, arrived[0])
     *second, errors_out = own_part(1, arrived[1])
-    total = summed_over_chips(first, second, halves, bits)
+    total = summed_over_chips(first, second, halves)
 
     back_errors = lax.all_to_all(errors_out[:, :BATCH_SLOTS], DEV, 0, 0, tiled=True)
     row_error = pl.pallas_call(

time: 197 us -> 173 us (0.88)
  the two profiles are of different devices: /device:TPU:1 before, /device:TPU:0 now
where the time goes in v1:
time: 173 us; the launch traced here: 172 us
  Pallas kernels  75.4 us (44%)
  starting transfers between devices  35.3 us (20%)
  waiting for transfers between devices  27.5 us (16%)
  blocking collectives  20.6 us (12%)
  local copies, waits for them, and re-layouts  6.51 us (4%)
  other arithmetic  5.83 us (3%)
    pallas_call x1, Pallas kernels, on_device(): pl.pallas_call(forward_kernel, grid=(hid // HBLK,), in_specs=[smem, once(...  26.8 us
    all_to_all x1, blocking collectives, on_device(): lax.all_to_all(table[:, :HALO_SLOTS + BATCH_SLOTS], DEV, 0, 0, tiled=True)  20.6 us
    pallas_call x2, Pallas kernels, own_part(): pl.pallas_call(own_kernel, grid_spec=pltpu.PrefetchScalarGridSpec(num_sca...  16.6 us
    ppermute x11, waiting for transfers between devices, exchange(): return lax.ppermute(x, DEV, pairing(level, dims))  14.8 us
    pallas_call x2, Pallas kernels, peer_part(): pl.pallas_call(peer_kernel, grid_spec=pltpu.PrefetchScalarGridSpec(num_sc...  13.9 us
    pallas_call x1, Pallas kernels, on_device(): pl.pallas_call(spread_kernel, grid=(row_tiles // per,), in_specs=[smem, p...  13 us
    ppermute x11, starting transfers between devices, exchange(): return lax.ppermute(x, DEV, pairing(level, dims))  11.3 us
    all_to_all x1, starting transfers between devices, on_device(): lax.all_to_all(errors_out[:, :BATCH_SLOTS], DEV, 0, 0, tiled=True)  9.86 us
  transfers between devices with their start and end apart: 16, of which 6 were waited for; matrix products, arithmetic and copies ran while one was open for 3% of the time, Pallas kernels for 31%

profile of v1, /device:TPU:0, one launch (start us, length us, event | category | flops | bytes accessed | tf_op | source)
XLA Modules:
  0.0 172.3 jit_solution(3732523615644537644)
XLA Ops:
  0.6 1.9 %request.1 = (s32[128,128]{1,0:T(8,128)}, s32[2,128]{1,0:T(2,128)}, s32[4,128]{1,0:T(4,128)}) custom-call(s32[2,128]{1,0:T(2,128)} %bitcast.64, s32[2,128]{1,0:T(2,128)} %bitcast.65, s32[4,128]{1,0:T(4,128)} %bitcast.60, s32[4,128]{1,0:T(4,128)} %bitcast.62), custom_call_target="tpu_custom_call" | custom-call | tf_op jit(solution)/shard_map/request/pallas_call | solution.py:337
  2.5 20.6 %all_to_all.32 = s32[128,1,12]{2,1,0:T(1,128)S(1)} all-to-all(s32[128,1,12]{2,1,0:T(1,128)} %bitcast.59), channel_id=1, replica_groups=mesh['dev'=128] {'dev'}, dimensions={0} | all-to-all | bytes 12288 | tf_op jit(solution)/shard_map/all_to_all | solution.py:352
  23.2 0.1 reshape.92
  23.3 0.0 copy-start.9
  23.3 0.0 copy-start.7
  23.3 0.0 copy-start.8
  23.3 3.9 %gather_fusion = bf16[512,512]{1,0:T(8,128)(2,1)S(1)} fusion(bf16[2048,512]{1,0:T(8,128)(2,1)} %prior.1, s32[1024]{0:T(1024)S(1)} %pad_clamp_fusion), kind=kCustom, calls=%fused_computation | custom fusion | bytes 1050624 | tf_op jit(solution)/shard_map/gather | solution.py:354
  27.2 0.9 reshape.91
  28.1 4.8 %all-to-all-start.1 = ((bf16[128,4,512]{2,1,0:T(4,128)(2,1)}), bf16[128,4,512]{2,1,0:T(4,128)(2,1)S(1)}, u32[]{:S(2)}, u32[]{:S(2)}) async-start(bf16[128,4,512]{2,1,0:T(4,128)(2,1)} %reshape.91), calls=%async_computation.1 | async-start | bytes 1048576 | tf_op jit(solution)/shard_map/all_to_all | solution.py:355
  33.1 0.1 copy.19.cols
  33.2 0.1 stack.35.place
  33.3 0.0 copy-start
  33.3 26.8 %forward.1 = (bf16[1024,1024]{1,0:T(8,128)(2,1)S(1)}, bf16[4096,1024]{1,0:T(8,128)(2,1)}, f32[1024,512]{1,0:T(8,128)}, bf16[4096,512]{1,0:T(8,128)(2,1)}) custom-call(s32[5]{0:T(128)S(1)} %stack.35.place, s32[128,12]{1,0:T(8,128)S(1)} %bitcast.47, bf16[2048,1024]{1,0:T(8,128)(2,1)} %features.1, bf16[128,32,1024]{2,1,0:T(8,128)(2,1)} %bitcast.49, ...), custom_call_target="tpu_custom_call" | custom-call | tf_op jit(solution)/shard_map/forward/pallas_call | solution.py:368
  60.1 0.0 all-to-all-done.1
  60.1 0.1 reshape.77.halo
  60.2 13.0 %spread.1 = (bf16[2048,512]{1,0:T(8,128)(2,1)}, bf16[1024,512]{1,0:T(8,128)(2,1)S(1)}, f32[128,128]{1,0:T(8,128)S(1)}) custom-call(s32[16,8]{1,0:T(8,128)S(1)} %copy.19.cols, bf16[16,8,128,128]{3,2,1,0:T(8,128)(2,1)} %weights.1, bf16[2048,512]{1,0:T(8,128)(2,1)} %prior.1, bf16[512,512]{1,0:T(8,128)(2,1)S(1)} %reshape.77.halo, s32[2,128]{1,0:T(2,128)S(1)} %copy-done, ...), custom_call_target="tpu_custom_call" | custom-call | tf_op jit(solution)/shard_map/spread/pallas_call | solution.py:402
  73.2 7.1 %shard_map.149 = bf16[1024,1536]{1,0:T(8,128)(2,1)S(1)} custom-call(s32[5]{0:T(128)S(1)} %stack.35.place, bf16[4096,512]{1,0:T(8,128)(2,1)} %get-tuple-element.29.w_out, bf16[4096,1024]{1,0:T(8,128)(2,1)} %get-tuple-element.30.hidden, bf16[1024,512]{1,0:T(8,128)(2,1)S(1)} %get-tuple-element.31.residue, bf16[1024,1024]{1,0:T(8,128)(2,1)S(1)} %get-tuple-element.32.x), custom_call_target="tpu_custom_call" | custom-call | tf_op jit(solution)/shard_map/pallas_call | solution.py:444
  80.3 0.1 collective-permute-start.1
  80.4 6.9 %shard_map.147 = bf16[1024,1536]{1,0:T(8,128)(2,1)S(1)} custom-call(s32[5]{0:T(128)S(1)} %stack.35.place, bf16[4096,512]{1,0:T(8,128)(2,1)} %get-tuple-element.29.w_out, bf16[4096,1024]{1,0:T(8,128)(2,1)} %get-tuple-element.30.hidden, bf16[1024,512]{1,0:T(8,128)(2,1)S(1)} %get-tuple-element.31.residue, bf16[1024,1024]{1,0:T(8,128)(2,1)S(1)} %get-tuple-element.32.x), custom_call_target="tpu_custom_call" | custom-call | tf_op jit(solution)/shard_map/pallas_call | solution.py:444
  87.2 0.6 collective-permute-start
  87.8 0.0 collective-permute-done.1.arrived
  87.8 8.3 %shard_map.150 = (bf16[1024,512]{1,0:T(8,128)(2,1)}, bf16[2,256,512]{2,1,0:T(8,128)(2,1)}, bf16[2,256,512]{2,1,0:T(8,128)(2,1)}, bf16[2,4,64,512]{3,2,1,0:T(8,12...) custom-call(s32[5]{0:T(128)S(1)} %stack.35.place, bf16[4096,512]{1,0:T(8,128)(2,1)} %get-tuple-element.29.w_out, ...), custom_call_target="tpu_custom_call" | custom-call | tf_op jit(solution)/shard_map/pallas_call | solution.py:472
  96.1 0.7 collective-permute-start.6
  96.9 1.5 collective-permute-start.2
  98.4 0.0 collective-permute-done.arrived
  98.4 8.3 %shard_map.148 = (bf16[1024,512]{1,0:T(8,128)(2,1)}, bf16[2,256,512]{2,1,0:T(8,128)(2,1)}, bf16[2,256,512]{2,1,0:T(8,128)(2,1)}, bf16[2,4,64,512]{3,2,1,0:T(8,12...) custom-call(s32[5]{0:T(128)S(1)} %stack.35.place, bf16[4096,512]{1,0:T(8,128)(2,1)} %get-tuple-element.29.w_out, ...), custom_call_target="tpu_custom_call" | custom-call | tf_op jit(solution)/shard_map/pallas_call | solution.py:472
  106.7 1.8 %collective-permute-start.9 = (bf16[2,4,64,512]{3,2,1,0:T(8,128)(2,1)}, bf16[2,4,64,512]{3,2,1,0:T(8,128)(2,1)}, u32[]{:S(2)}, u32[]{:S(2)}) collective-permute-start(bf16[2,4,64,512]{3,2,1,0:T(8,128)(2,1)} %get-tuple-element.43), channel_id=1, source_target_pairs={{0,2},{1,7},{2,0},{3,5},{4,6},{5,3},{6,4},{7,1},{8,10},{9,15},{10,... | collective-permute-start | bytes 1572872 | tf_op jit(solution)/shard_map/ppermute | solution.py:245
  108.6 0.3 collective-permute-start.10
  108.8 0.6 collective-permute-start.5
  109.4 0.0 collective-permute-done.6
  109.4 0.1 add_convert_fusion
  109.6 1.4 collective-permute-start.7
  111.0 5.3 %collective-permute-done.9 = bf16[2,4,64,512]{3,2,1,0:T(8,128)(2,1)} collective-permute-done((bf16[2,4,64,512]{3,2,1,0:T(8,128)(2,1)}, bf16[2,4,64,512]{3,2,1,0:T(8,128)(2,1)}, u32[]{:S(2)}, u32[]{:S(2)}) %collective-permute-start.9) | collective-permute-done | bytes 524320 | tf_op jit(solution)/shard_map/ppermute | solution.py:245
  116.3 1.1 fusion.2
  117.4 4.5 %collective-permute-done.10 = bf16[2,4,64,512]{3,2,1,0:T(8,128)(2,1)} collective-permute-done((bf16[2,4,64,512]{3,2,1,0:T(8,128)(2,1)}, bf16[2,4,64,512]{3,2,1,0:T(8,128)(2,1)}, u32[]{:S(2)}, u32[]{:S(2)}) %collective-permute-start.10) | collective-permute-done | bytes 524320 | tf_op jit(solution)/shard_map/ppermute | solution.py:245
  121.9 1.1 fusion.1
  123.0 0.1 pad_maximum_fusion
  123.1 0.6 collective-permute-start.11
  123.7 0.0 collective-permute-done.2
  123.7 1.7 add_convert_fusion.3
  125.4 1.8 %collective-permute-start.3 = (bf16[2,4,2,32,512]{4,3,2,1,0:T(8,128)(2,1)S(1)}, bf16[2,4,2,32,512]{4,3,2,1,0:T(8,128)(2,1)S(1)}, u32[]{:S(2)}, u32[]{:S(2)}) collective-permute-start(bf16[2,4,2,32,512]{4,3,2,1,0:T(8,128)(2,1)S(1)} %get-tuple-element.47), channel_id=1, source_target_pairs={{0,2},{1,7},{2,0},{3,5},{4,6},{5,3},{6,4},{7,1},{8,10},{9,15},{10,... | collective-permute-start | bytes 1572872 | tf_op jit(solution)/shard_map/ppermute | solution.py:245
  127.2 0.0 collective-permute-done.5
  127.2 0.1 add_convert_fusion.1
  127.4 0.0 collective-permute-done.7
  127.4 0.1 add_convert_fusion.8
  127.5 0.4 collective-permute-start.8
  127.9 4.4 %collective-permute-done.11 = bf16[2,2,2,2,32,512]{5,4,3,2,1,0:T(8,128)(2,1)S(1)} collective-permute-done((bf16[2,2,2,2,32,512]{5,4,3,2,1,0:T(8,128)(2,1)S(1)}, bf16[2,2,2,2,32,512]{5,4,3,2,1,0:T(8,128)(2,1)S(1)}, u32[]{:S(2)}, u32[]{:S(2)}) %collective-permute-start.11) | collective-permute-done | bytes 524320 | tf_op jit(solution)/shard_map/ppermute | solution.py:245
  132.4 1.3 fusion
  133.6 0.6 collective-permute-start.12
  134.2 0.5 collective-permute-done.3
  134.7 0.1 add_convert_fusion.9
  134.8 1.5 collective-permute-start.4
  136.4 9.9 %all-to-all-start.2 = ((f32[128,1,8]{2,1,0:T(1,128)}), f32[128,1,8]{2,1,0:T(1,128)S(1)}, u32[]{:S(2)}, u32[]{:S(2)}) async-start(f32[128,1,8]{2,1,0:T(1,128)} %bitcast.16), calls=%async_computation.2 | async-start | bytes 131072 | tf_op jit(solution)/shard_map/all_to_all | solution.py:503
  146.2 0.0 collective-permute-done.8.r1
  146.2 0.0 collective-permute-done.12.r2
  146.2 0.0 collective-permute-done.4.r0
  146.3 1.0 deal.1
  147.3 8.4 %all-to-all-done.2 = f32[128,1,8]{2,1,0:T(1,128)S(1)} async-done(((f32[128,1,8]{2,1,0:T(1,128)}), f32[128,1,8]{2,1,0:T(1,128)S(1)}, u32[]{:S(2)}, u32[]{:S(2)}) %all-to-all-start.2) | async-done | bytes 4128 | tf_op jit(solution)/shard_map/all_to_all | solution.py:503
  155.7 8.7 %all-to-all-start.3 = ((bf16[8,32,1536]{2,1,0:T(8,128)(2,1)}), bf16[8,32,1536]{2,1,0:T(8,128)(2,1)S(1)}, u32[]{:S(2)}, u32[]{:S(2)}) async-start(bf16[8,32,1536]{2,1,0:T(8,128)(2,1)} %deal.1), calls=%async_computation.3 | async-start | bytes 1572864 | tf_op jit(solution)/shard_map/all_to_all | solution.py:313
  164.4 2.2 %returned.1 = f32[4,128]{1,0:T(4,128)} custom-call(f32[128,8]{1,0:T(8,128)} %bitcast.58, s32[4,128]{1,0:T(4,128)} %bitcast.61, s32[4,128]{1,0:T(4,128)} %get-tuple-element.35.brank), custom_call_target="tpu_custom_call" | custom-call | tf_op jit(solution)/shard_map/returned/pallas_call | solution.py:504
  166.6 4.3 %all-to-all-done.3 = bf16[8,32,1536]{2,1,0:T(8,128)(2,1)S(1)} async-done(((bf16[8,32,1536]{2,1,0:T(8,128)(2,1)}), bf16[8,32,1536]{2,1,0:T(8,128)(2,1)S(1)}, u32[]{:S(2)}, u32[]{:S(2)}) %all-to-all-start.3) | async-done | bytes 786464 | tf_op jit(solution)/shard_map/all_to_all | solution.py:313
  170.9 0.1 convert_reduce_fusion
  171.1 0.7 slice.33
  171.7 0.6 slice.34
  (19 shorter events, 0.0 us)
Async XLA Ops:
  23.3 9.8 %copy-start.9 = (s32[16,8]{0,1:T(8,128)S(1)}, s32[16,8]{0,1:T(8,128)}, u32[]{:S(2)}) copy-start(s32[16,8]{0,1:T(8,128)} %param.16) | copy-start | bytes 1540
  23.3 10.0 %copy-start.7 = (s32[2048]{0:T(1024)S(1)}, s32[2048]{0:T(1024)}, u32[]{:S(2)}) copy-start(s32[2048]{0:T(1024)} %param.13) | copy-start | bytes 24580
  23.3 10.0 %copy-start.8 = (s32[2048]{0:T(1024)S(1)}, s32[2048]{0:T(1024)}, u32[]{:S(2)}) copy-start(s32[2048]{0:T(1024)} %param.14) | copy-start | bytes 24580
  28.1 32.0 %all-to-all-start.1 = ((bf16[128,4,512]{2,1,0:T(4,128)(2,1)}), bf16[128,4,512]{2,1,0:T(4,128)(2,1)S(1)}, u32[]{:S(2)}, u32[]{:S(2)}) async-start(bf16[128,4,512]{2,1,0:T(4,128)(2,1)} %reshape.91), calls=%async_computation.1 | async-start | bytes 1048576 | tf_op jit(solution)/shard_map/all_to_all | solution.py:355
  33.3 26.9 %copy-start = (s32[2,128]{1,0:T(2,128)S(1)}, s32[2,128]{1,0:T(2,128)}, u32[]{:S(2)}) copy-start(s32[2,128]{1,0:T(2,128)} %get-tuple-element.26.hslot) | copy-start | bytes 3076
  80.3 7.5 %collective-permute-start.1 = (bf16[1024,1536]{1,0:T(8,128)(2,1)S(1)}, bf16[1024,1536]{1,0:T(8,128)(2,1)S(1)}, u32[]{:S(2)}, u32[]{:S(2)}) collective-permute-start(bf16[1024,1536]{1,0:T(8,128)(2,1)S(1)} %shard_map.149), channel_id=1, source_target_pairs={{0,1},{1,0},{2,3},{3,2},{4,5},{5,4},{6,7},{7,6},{8,9},{9,8},{10,11... | collective-permute-start | bytes 9437192 | tf_op jit(solution)/shard_map/ppermute | solution.py:460
  87.2 11.2 %collective-permute-start = (bf16[1024,1536]{1,0:T(8,128)(2,1)S(1)}, bf16[1024,1536]{1,0:T(8,128)(2,1)S(1)}, u32[]{:S(2)}, u32[]{:S(2)}) collective-permute-start(bf16[1024,1536]{1,0:T(8,128)(2,1)S(1)} %shard_map.147), channel_id=1, source_target_pairs={{0,1},{1,0},{2,3},{3,2},{4,5},{5,4},{6,7},{7,6},{8,9},{9,8},{10,11... | collective-permute-start | bytes 9437192 | tf_op jit(solution)/shard_map/ppermute | solution.py:460
  96.1 13.3 %collective-permute-start.6 = (bf16[2,256,512]{2,1,0:T(8,128)(2,1)}, bf16[2,256,512]{2,1,0:T(8,128)(2,1)S(1)}, u32[]{:S(2)}, u32[]{:S(2)}) collective-permute-start(bf16[2,256,512]{2,1,0:T(8,128)(2,1)} %get-tuple-element.41), channel_id=1, source_target_pairs={{0,8},{1,25},{2,10},{3,27},{4,12},{5,29},{6,14},{7,31},{8,0},{9,17... | collective-permute-start | bytes 1572872 | tf_op jit(solution)/shard_map/ppermute | solution.py:245
  96.9 12.5 %copy-start.3 = (bf16[2,256,512]{2,1,0:T(8,128)(2,1)S(1)}, bf16[2,256,512]{2,1,0:T(8,128)(2,1)}, u32[]{:S(2)}) copy-start(bf16[2,256,512]{2,1,0:T(8,128)(2,1)} %get-tuple-element.40) | copy-start | bytes 1572868
  96.9 26.8 %collective-permute-start.2 = (bf16[1024,512]{1,0:T(8,128)(2,1)}, bf16[1024,512]{1,0:T(8,128)(2,1)}, u32[]{:S(2)}, u32[]{:S(2)}) collective-permute-start(bf16[1024,512]{1,0:T(8,128)(2,1)} %get-tuple-element.37), channel_id=1, source_target_pairs={{0,32},{1,97},{2,34},{3,99},{4,36},{5,101},{6,38},{7,103},{8,40},{... | collective-permute-start | bytes 3145736 | tf_op jit(solution)/shard_map/ppermute | solution.py:245
  106.7 17.0 %copy-start.1 = (bf16[1024,512]{1,0:T(8,128)(2,1)S(1)}, bf16[1024,512]{1,0:T(8,128)(2,1)}, u32[]{:S(2)}) copy-start(bf16[1024,512]{1,0:T(8,128)(2,1)} %get-tuple-element.36) | copy-start | bytes 3145732
  106.7 9.6 %collective-permute-start.9 = (bf16[2,4,64,512]{3,2,1,0:T(8,128)(2,1)}, bf16[2,4,64,512]{3,2,1,0:T(8,128)(2,1)}, u32[]{:S(2)}, u32[]{:S(2)}) collective-permute-start(bf16[2,4,64,512]{3,2,1,0:T(8,128)(2,1)} %get-tuple-element.43), channel_id=1, source_target_pairs={{0,2},{1,7},{2,0},{3,5},{4,6},{5,3},{6,4},{7,1},{8,10},{9,15},{10,... | collective-permute-start | bytes 1572872 | tf_op jit(solution)/shard_map/ppermute | solution.py:245
  108.6 13.4 %collective-permute-start.10 = (bf16[2,4,64,512]{3,2,1,0:T(8,128)(2,1)}, bf16[2,4,64,512]{3,2,1,0:T(8,128)(2,1)}, u32[]{:S(2)}, u32[]{:S(2)}) collective-permute-start(bf16[2,4,64,512]{3,2,1,0:T(8,128)(2,1)} %get-tuple-element.45), channel_id=1, source_target_pairs={{0,2},{1,7},{2,0},{3,5},{4,6},{5,3},{6,4},{7,1},{8,10},{9,15},{10,... | collective-permute-start | bytes 1572872 | tf_op jit(solution)/shard_map/ppermute | solution.py:245
  108.8 18.4 %collective-permute-start.5 = (bf16[2,256,512]{2,1,0:T(8,128)(2,1)}, bf16[2,256,512]{2,1,0:T(8,128)(2,1)S(1)}, u32[]{:S(2)}, u32[]{:S(2)}) collective-permute-start(bf16[2,256,512]{2,1,0:T(8,128)(2,1)} %get-tuple-element.39), channel_id=1, source_target_pairs={{0,8},{1,25},{2,10},{3,27},{4,12},{5,29},{6,14},{7,31},{8,0},{9,17... | collective-permute-start | bytes 1572872 | tf_op jit(solution)/shard_map/ppermute | solution.py:245
  109.5 17.7 %copy-start.2 = (bf16[2,256,512]{2,1,0:T(8,128)(2,1)S(1)}, bf16[2,256,512]{2,1,0:T(8,128)(2,1)}, u32[]{:S(2)}) copy-start(bf16[2,256,512]{2,1,0:T(8,128)(2,1)} %get-tuple-element.38) | copy-start | bytes 1572868
  109.6 17.8 %collective-permute-start.7 = (bf16[2,2,4,32,512]{4,3,2,1,0:T(8,128)(2,1)S(1)}, bf16[2,2,4,32,512]{4,3,2,1,0:T(8,128)(2,1)S(1)}, u32[]{:S(2)}, u32[]{:S(2)}) collective-permute-start(bf16[2,2,4,32,512]{4,3,2,1,0:T(8,128)(2,1)S(1)} %bitcast.53), channel_id=1, source_target_pairs={{0,32},{1,97},{2,34},{3,99},{4,36},{5,101},{6,38},{7,103},{8,40},{... | collective-permute-start | bytes 1572872 | tf_op jit(solution)/shard_map/ppermute | solution.py:245
  123.1 9.3 %collective-permute-start.11 = (bf16[2,2,2,2,32,512]{5,4,3,2,1,0:T(8,128)(2,1)S(1)}, bf16[2,2,2,2,32,512]{5,4,3,2,1,0:T(8,128)(2,1)S(1)}, u32[]{:S(2)}, u32[]{:S(2)}) collective-permute-start(bf16[2,2,2,2,32,512]{5,4,3,2,1,0:T(8,128)(2,1)S(1)} %pad_maximum_fusion), channel_id=1, source_target_pairs={{0,8},{1,25},{2,10},{3,27},{4,12},{5,29},{6,14},{7,31},{8,0},{9,17... | collective-permute-start | bytes 1572872 | tf_op jit(solution)/shard_map/ppermute | solution.py:245
  123.7 8.6 %copy-start.4 = (bf16[2,4,64,512]{3,2,1,0:T(8,128)(2,1)S(1)}, bf16[2,4,64,512]{3,2,1,0:T(8,128)(2,1)}, u32[]{:S(2)}) copy-start(bf16[2,4,64,512]{3,2,1,0:T(8,128)(2,1)} %get-tuple-element.44) | copy-start | bytes 1572868
  123.7 8.6 %copy-start.5 = (bf16[2,4,64,512]{3,2,1,0:T(8,128)(2,1)S(1)}, bf16[2,4,64,512]{3,2,1,0:T(8,128)(2,1)}, u32[]{:S(2)}) copy-start(bf16[2,4,64,512]{3,2,1,0:T(8,128)(2,1)} %get-tuple-element.42) | copy-start | bytes 1572868
  125.4 9.3 %collective-permute-start.3 = (bf16[2,4,2,32,512]{4,3,2,1,0:T(8,128)(2,1)S(1)}, bf16[2,4,2,32,512]{4,3,2,1,0:T(8,128)(2,1)S(1)}, u32[]{:S(2)}, u32[]{:S(2)}) collective-permute-start(bf16[2,4,2,32,512]{4,3,2,1,0:T(8,128)(2,1)S(1)} %get-tuple-element.47), channel_id=1, source_target_pairs={{0,2},{1,7},{2,0},{3,5},{4,6},{5,3},{6,4},{7,1},{8,10},{9,15},{10,... | collective-permute-start | bytes 1572872 | tf_op jit(solution)/shard_map/ppermute | solution.py:245
  127.5 18.7 %collective-permute-start.8 = (bf16[2,2,2,32,512]{4,3,2,1,0:T(8,128)(2,1)S(1)}, bf16[2,2,2,32,512]{4,3,2,1,0:T(8,128)(2,1)S(1)}, u32[]{:S(2)}, u32[]{:S(2)}) collective-permute-start(bf16[2,2,2,32,512]{4,3,2,1,0:T(8,128)(2,1)S(1)} %get-tuple-element.48), channel_id=1, source_target_pairs={{0,2},{1,7},{2,0},{3,5},{4,6},{5,3},{6,4},{7,1},{8,10},{9,15},{10,... | collective-permute-start | bytes 786440 | tf_op jit(solution)/shard_map/ppermute | solution.py:245
  133.6 12.6 %collective-permute-start.12 = (bf16[2,2,2,32,512]{4,3,2,1,0:T(8,128)(2,1)S(1)}, bf16[2,2,2,32,512]{4,3,2,1,0:T(8,128)(2,1)S(1)}, u32[]{:S(2)}, u32[]{:S(2)}) collective-permute-start(bf16[2,2,2,32,512]{4,3,2,1,0:T(8,128)(2,1)S(1)} %get-tuple-element.52), channel_id=1, source_target_pairs={{0,32},{1,97},{2,34},{3,99},{4,36},{5,101},{6,38},{7,103},{8,40},{... | collective-permute-start | bytes 786440 | tf_op jit(solution)/shard_map/ppermute | solution.py:245
  134.8 11.4 %collective-permute-start.4 = (bf16[2,2,2,32,512]{4,3,2,1,0:T(8,128)(2,1)S(1)}, bf16[2,2,2,32,512]{4,3,2,1,0:T(8,128)(2,1)S(1)}, u32[]{:S(2)}, u32[]{:S(2)}) collective-permute-start(bf16[2,2,2,32,512]{4,3,2,1,0:T(8,128)(2,1)S(1)} %get-tuple-element.50), channel_id=1, source_target_pairs={{0,8},{1,25},{2,10},{3,27},{4,12},{5,29},{6,14},{7,31},{8,0},{9,17... | collective-permute-start | bytes 786440 | tf_op jit(solution)/shard_map/ppermute | solution.py:245
  136.4 19.3 %all-to-all-start.2 = ((f32[128,1,8]{2,1,0:T(1,128)}), f32[128,1,8]{2,1,0:T(1,128)S(1)}, u32[]{:S(2)}, u32[]{:S(2)}) async-start(f32[128,1,8]{2,1,0:T(1,128)} %bitcast.16), calls=%async_computation.2 | async-start | bytes 131072 | tf_op jit(solution)/shard_map/all_to_all | solution.py:503
  155.7 8.7 %copy-start.6 = (f32[128,1,8]{2,1,0:T(1,128)}, f32[128,1,8]{2,1,0:T(1,128)S(1)}, u32[]{:S(2)}) copy-start(f32[128,1,8]{2,1,0:T(1,128)S(1)} %all-to-all-done.2) | copy-start | bytes 12292
  155.7 15.3 %all-to-all-start.3 = ((bf16[8,32,1536]{2,1,0:T(8,128)(2,1)}), bf16[8,32,1536]{2,1,0:T(8,128)(2,1)S(1)}, u32[]{:S(2)}, u32[]{:S(2)}) async-start(bf16[8,32,1536]{2,1,0:T(8,128)(2,1)} %deal.1), calls=%async_computation.3 | async-start | bytes 1572864 | tf_op jit(solution)/shard_map/all_to_all | solution.py:313

commit v2 on v1

--- a/solution.py
+++ b/solution.py
@@ -1,3 +1,5 @@
+from functools import partial
+
 import jax
 import jax.numpy as jnp
 from jax import lax
@@ -19,6 +21,10 @@
 
 def params(mib=48, **more):
     return pltpu.CompilerParams(vmem_limit_bytes=mib * 2**20, **more)
+
+
+def cost(gigaflops, mib, gigaexp=0.0):
+    return pl.CostEstimate(flops=int(gigaflops * 1e9), bytes_accessed=int(mib * 2**20), transcendentals=int(gigaexp * 1e9))
 
 
 def in_hbm(x):
@@ -134,21 +140,29 @@
         logits[...] = acc[...].T
 
 
-def spread_kernel(cols, weights, prior, halo, hslot, given, table, logits_far, prop, residue, errors, halo_tab, prop_all, onehot, logits, sem):
+def spread_kernel(
+    cols, weights, prior_far, halo, hslot, given, table, logits_far, hidden_far, w_out_far,
+    prop, residue, errors, hidden, w_out,
+    halo_tab, prop_all, onehot, prior, logits, sems,
+):
     step = pl.program_id(0)
     per = weights.shape[0]
     classes = prior.shape[1]
-
-    fetch = pltpu.make_async_copy(logits_far, logits, sem)
+    pairs = ((prior_far, prior), (logits_far, logits), (w_out_far, w_out), (hidden_far, hidden))
+    copies = [pltpu.make_async_copy(far, near, sems.at[n]) for n, (far, near) in enumerate(pairs)]
 
     @pl.when(step == 0)
     def _():
-        fetch.start()
-        slots = halo.shape[0]
-        slot = lax.broadcasted_iota(jnp.int32, (slots, LANES), 0)
+        for copy in copies:
+            copy.start()
+        owner = lax.broadcasted_iota(jnp.int32, (LANES, LANES), 0) * HALO_SLOTS
         for b in range(2):
-            pick = (slot == hslot[b : b + 1, :]).astype(F32).astype(BF)
-            halo_tab[b * LANES : (b + 1) * LANES, :] = dot(pick, halo[...], (0, 0)).astype(BF)
+            near = jnp.zeros((LANES, classes), F32)
+            for k in range(HALO_SLOTS):
+                pick = (owner + k == hslot[b : b + 1, :]).astype(F32).astype(BF)
+                near = near + dot(pick, halo[:, k, :], (0, 0))
+            halo_tab[b * LANES : (b + 1) * LANES, :] = near.astype(BF)
+        copies[0].wait()
 
     for t in range(per):
         r = step * per + t
@@ -178,7 +192,7 @@
         pick_rows(table, HALO_SLOTS, BATCH_SLOTS, prop_all.shape[0], onehot)
         lane = lax.broadcasted_iota(jnp.int32, (LANES, LANES), 1)
         out = jnp.zeros((LANES, LANES), F32)
-        fetch.wait()
+        copies[1].wait()
         tall = 512
         for s in range(BATCH_SLOTS):
             at = slice(s * LANES, (s + 1) * LANES)
@@ -191,23 +205,28 @@
             out = jnp.where(lane == s, 0.5 * jnp.mean(differ * differ, axis=1, keepdims=True), out)
             residue[at, :] = (differ * (1.0 / 256.0)).astype(BF)
         errors[...] = out
-
-
-def gradients(w_out, hidden, residue, x):
-    h = hidden[...]
+        copies[2].wait()
+        copies[3].wait()
+
+
+def gradients(block, w_out, hidden, residue, x):
+    at = pl.ds(pl.multiple_of(block * HBLK, HBLK), HBLK)
+    h = hidden[at, :]
     wide = h.astype(F32)
-    back = (dot(w_out[...], residue[...], (1, 1)) * (1.0 - wide * wide)).astype(BF)
+    back = (dot(w_out[at, :], residue[...], (1, 1)) * (1.0 - wide * wide)).astype(BF)
     return dot(h, residue[...], (1, 0)), dot(back, x[...], (1, 0))
 
 
-def peer_kernel(place, w_out, hidden, residue, x, grad):
-    out, into = gradients(w_out, hidden, residue, x)
+def peer_kernel(part, place, w_out, hidden, residue, x, grad):
+    half = place[4] if part else 1 - place[4]
+    out, into = gradients(2 * half + pl.program_id(0), w_out, hidden, residue, x)
     grad[:, :512] = out.astype(BF)
     grad[:, 512:] = into.astype(BF)
 
 
-def own_kernel(place, w_out, hidden, residue, x, arrived, errors, a, send_b, keep_b, send_c, keep_c, errors_to):
-    out, into = gradients(w_out, hidden, residue, x)
+def own_kernel(part, place, w_out, hidden, residue, x, arrived, errors, a, send_b, keep_b, send_c, keep_c, errors_to):
+    half = place[0] if part else 1 - place[0]
+    out, into = gradients(4 + 2 * half + pl.program_id(0), w_out, hidden, residue, x)
     a[...] = (out + arrived[:, :512].astype(F32)).astype(BF)
     total = (into + arrived[:, 512:].astype(F32)).astype(BF)
     left = total[:, :512].reshape(2, 256, 512)
@@ -352,7 +371,7 @@
     asked = lax.all_to_all(table[:, : HALO_SLOTS + BATCH_SLOTS], DEV, 0, 0, tiled=True)
 
     served = prior[jnp.maximum(asked[:, :HALO_SLOTS], 0)]
-    halo = lax.all_to_all(served, DEV, 0, 0, tiled=True).reshape(LANES * HALO_SLOTS, classes)
+    halo = lax.all_to_all(served, DEV, 0, 0, tiled=True)
 
     def whole(shape):
         return pl.BlockSpec(shape, lambda i, *_: (0,) * len(shape))
@@ -369,9 +388,9 @@
         forward_kernel,
         grid=(hid // HBLK,),
         in_specs=[smem, once((LANES, slots)), hbm, hbm, hbm],
-        out_specs=[whole((rows, feat)), rows_at(0, rows), whole((rows, classes)), rows_at(0, classes)],
+        out_specs=[vmem, rows_at(0, rows), whole((rows, classes)), rows_at(0, classes)],
         out_shape=[
-            jax.ShapeDtypeStruct((rows, feat), BF),
+            pltpu.VMEM((rows, feat), BF),
             pltpu.HBM((hid, rows), BF),
             pltpu.HBM((rows, classes), F32),
             pltpu.HBM((hid, classes), BF),
@@ -386,7 +405,8 @@
             pltpu.SemaphoreType.DMA((2,)),
             pltpu.SemaphoreType.DMA((2,)),
         ],
-        compiler_params=params(36),
+        compiler_params=params(32),
+        cost_estimate=cost(17.2, 30, 0.0042),
         name="forward",
     )(
         place,
@@ -399,64 +419,69 @@
     row_tiles = tile_weights.shape[0]
     per = 2
     given = jnp.where(labeled == 1, label_class, -1).reshape(row_tiles, LANES)
-    prop, residue, errors = pl.pallas_call(
+    prop, residue, errors, hidden, w_out_o = pl.pallas_call(
         spread_kernel,
         grid=(row_tiles // per,),
         in_specs=[
             smem,
             pl.BlockSpec((per, 8, LANES, LANES), lambda i: (i, 0, 0, 0)),
-            once((nodes, classes)),
-            once((LANES * HALO_SLOTS, classes)),
+            hbm,
+            once((LANES, HALO_SLOTS, classes)),
             once((halo_count // LANES, LANES)),
             once((row_tiles, LANES)),
             once((LANES, slots)),
             hbm,
+            hbm,
+            hbm,
         ],
         out_specs=[
             pl.BlockSpec((per * LANES, classes), lambda i: (i, 0)),
-            whole((rows, classes)),
+            vmem,
             whole((LANES, LANES)),
+            vmem,
+            vmem,
         ],
         out_shape=[
             jax.ShapeDtypeStruct((nodes, classes), BF),
-            jax.ShapeDtypeStruct((rows, classes), BF),
+            pltpu.VMEM((rows, classes), BF),
             jax.ShapeDtypeStruct((LANES, LANES), F32),
+            pltpu.VMEM((hid, rows), BF),
+            pltpu.VMEM((hid, classes), BF),
         ],
         scratch_shapes=[
             pltpu.VMEM((halo_count, classes), BF),
             pltpu.VMEM((nodes, classes), BF),
             pltpu.VMEM((rows, nodes), BF),
+            pltpu.VMEM((nodes, classes), BF),
             pltpu.VMEM((rows, classes), F32),
-            pltpu.SemaphoreType.DMA,
-        ],
-        compiler_params=params(24),
+            pltpu.SemaphoreType.DMA((4,)),
+        ],
+        compiler_params=params(22),
+        cost_estimate=cost(4.3, 12, 0.0005),
         name="spread",
-    )(tile_cols, in_hbm(tile_weights), in_hbm(prior), halo, hslot, given, asked, in_hbm(logits))
+    )(tile_cols, in_hbm(tile_weights), in_hbm(prior), halo, hslot, given, asked, in_hbm(logits), in_hbm(hidden), in_hbm(w_out_o))
 
     partner = [(d, d ^ 1) for d in range(128)]
     part_rows = 2 * HBLK
 
     def peer_part(part):
-        def block(i, p):
-            half = p[4] if part else 1 - p[4]
-            return (2 * half + i, 0)
-
         grad = pl.pallas_call(
-            peer_kernel,
+            partial(peer_kernel, part),
             grid_spec=pltpu.PrefetchScalarGridSpec(
                 num_scalar_prefetch=1,
                 grid=(2,),
                 in_specs=[
-                    pl.BlockSpec((HBLK, classes), block),
-                    pl.BlockSpec((HBLK, rows), block),
-                    once((rows, classes)),
-                    once((rows, feat)),
+                    vmem,
+                    vmem,
+                    vmem,
+                    vmem,
                 ],
                 out_specs=rows_at(0, classes + feat),
             ),
             out_shape=jax.ShapeDtypeStruct((part_rows, classes + feat), BF),
-            compiler_params=params(24),
-        )(place, in_hbm(w_out_o), in_hbm(hidden), residue, x)
+            compiler_params=params(22),
+            cost_estimate=cost(4.3, 9),
+        )(place, w_out_o, hidden, residue, x)
         return lax.ppermute(grad, DEV, partner)
 
     b_spec = pl.BlockSpec((1, 256, 512), lambda i, p: (i, 0, 0))
@@ -465,20 +490,16 @@
     c_shape = pltpu.HBM((2, 4, 64, 512), BF)
 
     def own_part(part, arrived):
-        def block(i, p):
-            half = p[0] if part else 1 - p[0]
-            return (4 + 2 * half + i, 0)
-
         return pl.pallas_call(
-            own_kernel,
+            partial(own_kernel, part),
             grid_spec=pltpu.PrefetchScalarGridSpec(
                 num_scalar_prefetch=1,
                 grid=(2,),
                 in_specs=[
-                    pl.BlockSpec((HBLK, classes), block),
-                    pl.BlockSpec((HBLK, rows), block),
-                    once((rows, classes)),
-                    once((rows, feat)),
+                    vmem,
+                    vmem,
+                    vmem,
+                    vmem,
                     rows_at(0, classes + feat),
                     once((LANES, LANES)),
                 ],
@@ -492,8 +513,9 @@
                 c_shape,
                 jax.ShapeDtypeStruct((LANES, LANES), F32),
             ],
-            compiler_params=params(28),
-        )(place, in_hbm(w_out_o), in_hbm(hidden), residue, x, arrived, errors)
+            compiler_params=params(24),
+            cost_estimate=cost(4.3, 12),
+        )(place, w_out_o, hidden, residue, x, arrived, errors)
 
     arrived = [peer_part(0), peer_part(1)]
     *first, _ = own_part(0, arrived[0])

time: 173 us -> 167 us (0.965)
  blocking collectives: 20.6 us -> 0 us
  starting transfers between devices: 35.3 us -> 46.6 us
  waiting for transfers between devices: 27.5 us -> 32.6 us
  Pallas kernels: 75.4 us -> 73.2 us
    all_to_all x1 -> x0, blocking collectives: 20.6 us -> none  [on_device(): lax.all_to_all(table[:, :HALO_SLOTS + BATCH_SLOTS], DEV, 0, 0, tiled=True)]
    all_to_all x1 -> x2, starting transfers between devices: 4.8 us -> 15.8 us  [the longest x1 11.2 us: on_device(): lax.all_to_all(table[:, :HALO_SLOTS + BATCH_SLOTS], DEV, 0, 0, tiled=True)]
    all_to_all x1 -> x2, waiting for transfers between devices: 0.01 us -> 7.84 us  [the longest x1 7.83 us: on_device(): lax.all_to_all(table[:, :HALO_SLOTS + BATCH_SLOTS], DEV, 0, 0, tiled=True)]
    pallas_call x4, Pallas kernels: 30.6 us -> 24.8 us  [the longest x2 14 us: own_part(): pl.pallas_call(partial(own_kernel, part), grid_spec=pltpu.PrefetchScalarG...]
    pallas_call x1, Pallas kernels: 13 us -> 16.6 us  [on_device(): pl.pallas_call(spread_kernel, grid=(row_tiles // per,), in_specs=[smem, p...]
    ppermute x11, waiting for transfers between devices: 14.8 us -> 12 us  [exchange(): return lax.ppermute(x, DEV, pairing(level, dims))]
  transfers between devices with their start and end apart: 16 -> 17, of which waited for: 6 -> 6; matrix products, arithmetic and copies ran while one was open for 3% -> 4% of each run, Pallas kernels for 31% -> 30%
where the time goes in v2:
time: 167 us
  Pallas kernels  73.2 us (44%)
  starting transfers between devices  46.6 us (28%)
  waiting for transfers between devices  32.6 us (20%)
  local copies, waits for them, and re-layouts  7.04 us (4%)
  other arithmetic  6.4 us (4%)
    pallas_call x1, Pallas kernels, on_device(): pl.pallas_call(forward_kernel, grid=(hid // HBLK,), in_specs=[smem, once(...  26.8 us
    pallas_call x1, Pallas kernels, on_device(): pl.pallas_call(spread_kernel, grid=(row_tiles // per,), in_specs=[smem, p...  16.6 us
    pallas_call x2, Pallas kernels, own_part(): pl.pallas_call(partial(own_kernel, part), grid_spec=pltpu.PrefetchScalarG...  14 us
    ppermute x11, waiting for transfers between devices, exchange(): return lax.ppermute(x, DEV, pairing(level, dims))  12 us
    ppermute x11, starting transfers between devices, exchange(): return lax.ppermute(x, DEV, pairing(level, dims))  11.6 us
    all_to_all x1, starting transfers between devices, on_device(): lax.all_to_all(table[:, :HALO_SLOTS + BATCH_SLOTS], DEV, 0, 0, tiled=True)  11.2 us
    pallas_call x2, Pallas kernels, peer_part(): pl.pallas_call(partial(peer_kernel, part), grid_spec=pltpu.PrefetchScalar...  10.8 us
    all_to_all x1, starting transfers between devices, on_device(): lax.all_to_all(errors_out[:, :BATCH_SLOTS], DEV, 0, 0, tiled=True)  9.8 us
  transfers between devices with their start and end apart: 17, of which 6 were waited for; matrix products, arithmetic and copies ran while one was open for 4% of the time, Pallas kernels for 30%

profile of v2, /device:TPU:0, one launch (start us, length us, event | category | flops | bytes accessed | tf_op | source)
XLA Modules:
  0.0 166.7 jit_solution(8974507316377509881)
XLA Ops:
  0.6 1.9 %request.1 = (s32[128,128]{1,0:T(8,128)}, s32[2,128]{1,0:T(2,128)}, s32[4,128]{1,0:T(4,128)}) custom-call(s32[2,128]{1,0:T(2,128)} %bitcast.62, s32[2,128]{1,0:T(2,128)} %bitcast.63, s32[4,128]{1,0:T(4,128)} %bitcast.58, s32[4,128]{1,0:T(4,128)} %bitcast.60), custom_call_target="tpu_custom_call" | custom-call | tf_op jit(solution)/shard_map/request/pallas_call | solution.py:356
  2.5 11.2 %all-to-all-start = ((s32[128,1,12]{2,1,0:T(1,128)}), s32[128,1,12]{2,1,0:T(1,128)S(1)}, u32[]{:S(2)}, u32[]{:S(2)}) async-start(s32[128,1,12]{2,1,0:T(1,128)} %bitcast.57), calls=%async_computation | async-start | bytes 131072 | tf_op jit(solution)/shard_map/all_to_all | solution.py:371
  13.8 0.7 select_bitcast_fusion.given
  14.5 0.8 copy.19.cols
  15.3 0.1 stack.35.place
  15.3 7.8 %all-to-all-done = s32[128,1,12]{2,1,0:T(1,128)S(1)} async-done(((s32[128,1,12]{2,1,0:T(1,128)}), s32[128,1,12]{2,1,0:T(1,128)S(1)}, u32[]{:S(2)}, u32[]{:S(2)}) %all-to-all-start) | async-done | bytes 6176 | tf_op jit(solution)/shard_map/all_to_all | solution.py:371
  23.2 0.1 reshape.88
  23.3 3.8 %gather_fusion = bf16[512,512]{1,0:T(8,128)(2,1)S(1)} fusion(bf16[2048,512]{1,0:T(8,128)(2,1)} %prior_far.1, s32[1024]{0:T(1024)S(1)} %pad_clamp_fusion), kind=kCustom, calls=%fused_computation | custom fusion | bytes 1050624 | tf_op jit(solution)/shard_map/gather | solution.py:373
  27.2 0.9 reshape.87
  28.1 4.6 %all-to-all-start.1 = ((bf16[128,4,512]{2,1,0:T(4,128)(2,1)}), bf16[128,4,512]{2,1,0:T(4,128)(2,1)S(1)}, u32[]{:S(2)}, u32[]{:S(2)}) async-start(bf16[128,4,512]{2,1,0:T(4,128)(2,1)} %reshape.87), calls=%async_computation.1 | async-start | bytes 1048576 | tf_op jit(solution)/shard_map/all_to_all | solution.py:374
  32.7 0.0 copy-start
  32.7 26.8 %forward.1 = (bf16[1024,1024]{1,0:T(8,128)(2,1)S(1)}, bf16[4096,1024]{1,0:T(8,128)(2,1)}, f32[1024,512]{1,0:T(8,128)}, bf16[4096,512]{1,0:T(8,128)(2,1)}) custom-call(s32[5]{0:T(128)S(1)} %stack.35.place, s32[128,12]{1,0:T(8,128)S(1)} %bitcast.47, bf16[2048,1024]{1,0:T(8,128)(2,1)} %features.1, bf16[128,32,1024]{2,1,0:T(8,128)(2,1)} %bitcast.64, ...), custom_call_target="tpu_custom_call" | custom-call | flops 17200001024 | bytes 31457280 | tf_op jit(solution)/shard_map/forward/pallas_call | solution.py:387
  59.5 0.0 all-to-all-done.1.halo
  59.5 16.6 %spread.1 = (bf16[2048,512]{1,0:T(8,128)(2,1)}, bf16[1024,512]{1,0:T(8,128)(2,1)S(1)}, f32[128,128]{1,0:T(8,128)S(1)}, bf16[4096,1024]{1,0:T(8,128)(2,1)S(1)}, bf16[4096,512]{1,0:T(8,128)(2,1)S(1)}) custom-call(s32[16,8]{1,0:T(8,128)S(1)} %copy.19.cols, bf16[16,8,128,128]{3,2,1,0:T(8,128)(2,1)} %weights.1, bf16[2048,512]{1,0:T(8,128)(2,1)} %prior_far.1, ...), custom_call_target="tpu_custom_call" | custom-call | flops 4300000256 | bytes 12582912 | tf_op jit(solution)/shard_map/spread/pallas_call | solution.py:422
  76.1 5.4 %shard_map.149 = bf16[1024,1536]{1,0:T(8,128)(2,1)S(1)} custom-call(s32[5]{0:T(128)S(1)} %stack.35.place, bf16[4096,512]{1,0:T(8,128)(2,1)S(1)} %get-tuple-element.33.w_out, bf16[4096,1024]{1,0:T(8,128)(2,1)S(1)} %get-tuple-element.34.hidden, bf16[1024,512]{1,0:T(8,128)(2,1)S(1)} %get-tuple-element.35.residue, bf16[1024,1024]{1,0:T(8,128)(2,1)S(1)} %get-tuple-element.36.x), custom_call_target="tpu_custom_call" | custom-call | flops 4300000256 | bytes 9437184 | tf_op jit(solution)/shard_map/pallas_call | solution.py:468
  81.5 0.1 collective-permute-start.1
  81.6 5.4 %shard_map.147 = bf16[1024,1536]{1,0:T(8,128)(2,1)S(1)} custom-call(s32[5]{0:T(128)S(1)} %stack.35.place, bf16[4096,512]{1,0:T(8,128)(2,1)S(1)} %get-tuple-element.33.w_out, bf16[4096,1024]{1,0:T(8,128)(2,1)S(1)} %get-tuple-element.34.hidden, bf16[1024,512]{1,0:T(8,128)(2,1)S(1)} %get-tuple-element.35.residue, bf16[1024,1024]{1,0:T(8,128)(2,1)S(1)} %get-tuple-element.36.x), custom_call_target="tpu_custom_call" | custom-call | flops 4300000256 | bytes 9437184 | tf_op jit(solution)/shard_map/pallas_call | solution.py:468
  87.0 0.6 collective-permute-start
  87.6 0.0 collective-permute-done.1.arrived
  87.6 6.9 %shard_map.150 = (bf16[1024,512]{1,0:T(8,128)(2,1)}, bf16[2,256,512]{2,1,0:T(8,128)(2,1)}, bf16[2,256,512]{2,1,0:T(8,128)(2,1)}, bf16[2,4,64,512]{3,2,1,0:T(8,12...) custom-call(s32[5]{0:T(128)S(1)} %stack.35.place, bf16[4096,512]{1,0:T(8,128)(2,1)S(1)} %get-tuple-element.33.w_out, ...), custom_call_target="tpu_custom_call" | custom-call | flops 4300000256 | bytes 12582912 | tf_op jit(solution)/shard_map/pallas_call | solution.py:493
  94.5 1.2 collective-permute-start.10
  95.6 1.5 collective-permute-start.2
  97.2 0.0 collective-permute-done.arrived
  97.2 7.1 %shard_map.148 = (bf16[1024,512]{1,0:T(8,128)(2,1)}, bf16[2,256,512]{2,1,0:T(8,128)(2,1)}, bf16[2,256,512]{2,1,0:T(8,128)(2,1)}, bf16[2,4,64,512]{3,2,1,0:T(8,12...) custom-call(s32[5]{0:T(128)S(1)} %stack.35.place, bf16[4096,512]{1,0:T(8,128)(2,1)S(1)} %get-tuple-element.33.w_out, ...), custom_call_target="tpu_custom_call" | custom-call | flops 4300000256 | bytes 12582912 | tf_op jit(solution)/shard_map/pallas_call | solution.py:493
  104.3 0.4 collective-permute-start.9
  104.7 1.5 collective-permute-start.6
  106.2 0.5 collective-permute-start.5
  106.7 0.0 collective-permute-done.10
  106.7 0.0 copy-done.4
  106.7 1.0 fusion.1
  107.7 6.1 %collective-permute-done.9 = bf16[2,4,64,512]{3,2,1,0:T(8,128)(2,1)} collective-permute-done((bf16[2,4,64,512]{3,2,1,0:T(8,128)(2,1)}, bf16[2,4,64,512]{3,2,1,0:T(8,128)(2,1)}, u32[]{:S(2)}, u32[]{:S(2)}) %collective-permute-start.9) | collective-permute-done | bytes 524320 | tf_op jit(solution)/shard_map/ppermute | solution.py:264
  113.9 1.2 fusion.2
  115.0 0.1 pad_maximum_fusion
  115.1 1.6 collective-permute-start.11
  116.7 0.0 collective-permute-done.6
  116.7 0.1 add_convert_fusion
  116.8 0.6 collective-permute-start.7
  117.4 0.0 collective-permute-done.2
  117.4 1.5 add_convert_fusion.3
  118.9 0.4 collective-permute-start.3
  119.3 0.4 collective-permute-done.5
  119.7 0.0 copy-done.2
  119.7 0.1 add_convert_fusion.1
  119.8 5.5 %collective-permute-done.11 = bf16[2,2,2,2,32,512]{5,4,3,2,1,0:T(8,128)(2,1)S(1)} collective-permute-done((bf16[2,2,2,2,32,512]{5,4,3,2,1,0:T(8,128)(2,1)S(1)}, bf16[2,2,2,2,32,512]{5,4,3,2,1,0:T(8,128)(2,1)S(1)}, u32[]{:S(2)}, u32[]{:S(2)}) %collective-permute-start.11) | collective-permute-done | bytes 524320 | tf_op jit(solution)/shard_map/ppermute | solution.py:264
  125.3 1.3 fusion
  126.5 1.2 collective-permute-start.12
  127.8 0.0 collective-permute-done.7
  127.8 0.1 add_convert_fusion.8
  127.9 1.2 collective-permute-start.8
  129.1 0.0 collective-permute-done.3
  129.1 0.1 add_convert_fusion.9
  129.2 1.6 collective-permute-start.4
  130.8 9.8 %all-to-all-start.2 = ((f32[128,1,8]{2,1,0:T(1,128)}), f32[128,1,8]{2,1,0:T(1,128)S(1)}, u32[]{:S(2)}, u32[]{:S(2)}) async-start(f32[128,1,8]{2,1,0:T(1,128)} %bitcast.16), calls=%async_computation.2 | async-start | bytes 131072 | tf_op jit(solution)/shard_map/all_to_all | solution.py:525
  140.6 0.0 collective-permute-done.12.r2
  140.6 0.0 collective-permute-done.8.r1
  140.6 0.0 collective-permute-done.4.r0
  140.6 1.0 deal.1
  141.7 8.4 %all-to-all-done.2 = f32[128,1,8]{2,1,0:T(1,128)S(1)} async-done(((f32[128,1,8]{2,1,0:T(1,128)}), f32[128,1,8]{2,1,0:T(1,128)S(1)}, u32[]{:S(2)}, u32[]{:S(2)}) %all-to-all-start.2) | async-done | bytes 4128 | tf_op jit(solution)/shard_map/all_to_all | solution.py:525
  150.1 8.7 %all-to-all-start.3 = ((bf16[8,32,1536]{2,1,0:T(8,128)(2,1)}), bf16[8,32,1536]{2,1,0:T(8,128)(2,1)S(1)}, u32[]{:S(2)}, u32[]{:S(2)}) async-start(bf16[8,32,1536]{2,1,0:T(8,128)(2,1)} %deal.1), calls=%async_computation.3 | async-start | bytes 1572864 | tf_op jit(solution)/shard_map/all_to_all | solution.py:332
  158.8 2.2 %returned.1 = f32[4,128]{1,0:T(4,128)} custom-call(f32[128,8]{1,0:T(8,128)} %bitcast.56, s32[4,128]{1,0:T(4,128)} %bitcast.59, s32[4,128]{1,0:T(4,128)} %get-tuple-element.39.brank), custom_call_target="tpu_custom_call" | custom-call | tf_op jit(solution)/shard_map/returned/pallas_call | solution.py:526
  161.0 4.3 %all-to-all-done.3 = bf16[8,32,1536]{2,1,0:T(8,128)(2,1)S(1)} async-done(((bf16[8,32,1536]{2,1,0:T(8,128)(2,1)}), bf16[8,32,1536]{2,1,0:T(8,128)(2,1)S(1)}, u32[]{:S(2)}, u32[]{:S(2)}) %all-to-all-start.3) | async-done | bytes 786464 | tf_op jit(solution)/shard_map/all_to_all | solution.py:332
  165.3 0.1 convert_reduce_fusion
  165.4 0.7 slice.33
  166.1 0.6 slice.34
  (13 shorter events, 0.0 us)
Async XLA Ops:
  2.5 20.6 %all-to-all-start = ((s32[128,1,12]{2,1,0:T(1,128)}), s32[128,1,12]{2,1,0:T(1,128)S(1)}, u32[]{:S(2)}, u32[]{:S(2)}) async-start(s32[128,1,12]{2,1,0:T(1,128)} %bitcast.57), calls=%async_computation | async-start | bytes 131072 | tf_op jit(solution)/shard_map/all_to_all | solution.py:371
  28.1 31.4 %all-to-all-start.1 = ((bf16[128,4,512]{2,1,0:T(4,128)(2,1)}), bf16[128,4,512]{2,1,0:T(4,128)(2,1)S(1)}, u32[]{:S(2)}, u32[]{:S(2)}) async-start(bf16[128,4,512]{2,1,0:T(4,128)(2,1)} %reshape.87), calls=%async_computation.1 | async-start | bytes 1048576 | tf_op jit(solution)/shard_map/all_to_all | solution.py:374
  32.7 26.8 %copy-start = (s32[2,128]{1,0:T(2,128)S(1)}, s32[2,128]{1,0:T(2,128)}, u32[]{:S(2)}) copy-start(s32[2,128]{1,0:T(2,128)} %get-tuple-element.28.hslot) | copy-start | bytes 3076
  81.5 6.1 %collective-permute-start.1 = (bf16[1024,1536]{1,0:T(8,128)(2,1)S(1)}, bf16[1024,1536]{1,0:T(8,128)(2,1)S(1)}, u32[]{:S(2)}, u32[]{:S(2)}) collective-permute-start(bf16[1024,1536]{1,0:T(8,128)(2,1)S(1)} %shard_map.149), channel_id=1, source_target_pairs={{0,1},{1,0},{2,3},{3,2},{4,5},{5,4},{6,7},{7,6},{8,9},{9,8},{10,11... | collective-permute-start | bytes 9437192 | tf_op jit(solution)/shard_map/ppermute | solution.py:485
  87.0 10.1 %collective-permute-start = (bf16[1024,1536]{1,0:T(8,128)(2,1)S(1)}, bf16[1024,1536]{1,0:T(8,128)(2,1)S(1)}, u32[]{:S(2)}, u32[]{:S(2)}) collective-permute-start(bf16[1024,1536]{1,0:T(8,128)(2,1)S(1)} %shard_map.147), channel_id=1, source_target_pairs={{0,1},{1,0},{2,3},{3,2},{4,5},{5,4},{6,7},{7,6},{8,9},{9,8},{10,11... | collective-permute-start | bytes 9437192 | tf_op jit(solution)/shard_map/ppermute | solution.py:485
  94.5 12.2 %collective-permute-start.10 = (bf16[2,4,64,512]{3,2,1,0:T(8,128)(2,1)}, bf16[2,4,64,512]{3,2,1,0:T(8,128)(2,1)}, u32[]{:S(2)}, u32[]{:S(2)}) collective-permute-start(bf16[2,4,64,512]{3,2,1,0:T(8,128)(2,1)} %get-tuple-element.49), channel_id=1, source_target_pairs={{0,2},{1,7},{2,0},{3,5},{4,6},{5,3},{6,4},{7,1},{8,10},{9,15},{10,... | collective-permute-start | bytes 1572872 | tf_op jit(solution)/shard_map/ppermute | solution.py:264
  95.6 11.0 %copy-start.4 = (bf16[2,4,64,512]{3,2,1,0:T(8,128)(2,1)S(1)}, bf16[2,4,64,512]{3,2,1,0:T(8,128)(2,1)}, u32[]{:S(2)}) copy-start(bf16[2,4,64,512]{3,2,1,0:T(8,128)(2,1)} %get-tuple-element.48) | copy-start | bytes 1572868
  95.6 21.0 %copy-start.3 = (bf16[2,256,512]{2,1,0:T(8,128)(2,1)S(1)}, bf16[2,256,512]{2,1,0:T(8,128)(2,1)}, u32[]{:S(2)}) copy-start(bf16[2,256,512]{2,1,0:T(8,128)(2,1)} %get-tuple-element.44) | copy-start | bytes 1572868
  95.6 21.7 %collective-permute-start.2 = (bf16[1024,512]{1,0:T(8,128)(2,1)}, bf16[1024,512]{1,0:T(8,128)(2,1)}, u32[]{:S(2)}, u32[]{:S(2)}) collective-permute-start(bf16[1024,512]{1,0:T(8,128)(2,1)} %get-tuple-element.41), channel_id=1, source_target_pairs={{0,32},{1,97},{2,34},{3,99},{4,36},{5,101},{6,38},{7,103},{8,40},{... | collective-permute-start | bytes 3145736 | tf_op jit(solution)/shard_map/ppermute | solution.py:264
  104.3 13.1 %copy-start.1 = (bf16[1024,512]{1,0:T(8,128)(2,1)S(1)}, bf16[1024,512]{1,0:T(8,128)(2,1)}, u32[]{:S(2)}) copy-start(bf16[1024,512]{1,0:T(8,128)(2,1)} %get-tuple-element.40) | copy-start | bytes 3145732
  104.3 9.6 %collective-permute-start.9 = (bf16[2,4,64,512]{3,2,1,0:T(8,128)(2,1)}, bf16[2,4,64,512]{3,2,1,0:T(8,128)(2,1)}, u32[]{:S(2)}, u32[]{:S(2)}) collective-permute-start(bf16[2,4,64,512]{3,2,1,0:T(8,128)(2,1)} %get-tuple-element.47), channel_id=1, source_target_pairs={{0,2},{1,7},{2,0},{3,5},{4,6},{5,3},{6,4},{7,1},{8,10},{9,15},{10,... | collective-permute-start | bytes 1572872 | tf_op jit(solution)/shard_map/ppermute | solution.py:264
  104.7 12.0 %collective-permute-start.6 = (bf16[2,256,512]{2,1,0:T(8,128)(2,1)}, bf16[2,256,512]{2,1,0:T(8,128)(2,1)S(1)}, u32[]{:S(2)}, u32[]{:S(2)}) collective-permute-start(bf16[2,256,512]{2,1,0:T(8,128)(2,1)} %get-tuple-element.45), channel_id=1, source_target_pairs={{0,8},{1,25},{2,10},{3,27},{4,12},{5,29},{6,14},{7,31},{8,0},{9,17... | collective-permute-start | bytes 1572872 | tf_op jit(solution)/shard_map/ppermute | solution.py:264
  106.2 13.5 %collective-permute-start.5 = (bf16[2,256,512]{2,1,0:T(8,128)(2,1)}, bf16[2,256,512]{2,1,0:T(8,128)(2,1)S(1)}, u32[]{:S(2)}, u32[]{:S(2)}) collective-permute-start(bf16[2,256,512]{2,1,0:T(8,128)(2,1)} %get-tuple-element.43), channel_id=1, source_target_pairs={{0,8},{1,25},{2,10},{3,27},{4,12},{5,29},{6,14},{7,31},{8,0},{9,17... | collective-permute-start | bytes 1572872 | tf_op jit(solution)/shard_map/ppermute | solution.py:264
  113.9 5.8 %copy-start.2 = (bf16[2,256,512]{2,1,0:T(8,128)(2,1)S(1)}, bf16[2,256,512]{2,1,0:T(8,128)(2,1)}, u32[]{:S(2)}) copy-start(bf16[2,256,512]{2,1,0:T(8,128)(2,1)} %get-tuple-element.42) | copy-start | bytes 1572868
  115.1 10.2 %collective-permute-start.11 = (bf16[2,2,2,2,32,512]{5,4,3,2,1,0:T(8,128)(2,1)S(1)}, bf16[2,2,2,2,32,512]{5,4,3,2,1,0:T(8,128)(2,1)S(1)}, u32[]{:S(2)}, u32[]{:S(2)}) collective-permute-start(bf16[2,2,2,2,32,512]{5,4,3,2,1,0:T(8,128)(2,1)S(1)} %pad_maximum_fusion), channel_id=1, source_target_pairs={{0,8},{1,25},{2,10},{3,27},{4,12},{5,29},{6,14},{7,31},{8,0},{9,17... | collective-permute-start | bytes 1572872 | tf_op jit(solution)/shard_map/ppermute | solution.py:264
  116.7 8.6 %copy-start.5 = (bf16[2,4,64,512]{3,2,1,0:T(8,128)(2,1)S(1)}, bf16[2,4,64,512]{3,2,1,0:T(8,128)(2,1)}, u32[]{:S(2)}) copy-start(bf16[2,4,64,512]{3,2,1,0:T(8,128)(2,1)} %get-tuple-element.46) | copy-start | bytes 1572868
  116.8 11.0 %collective-permute-start.7 = (bf16[2,2,4,32,512]{4,3,2,1,0:T(8,128)(2,1)S(1)}, bf16[2,2,4,32,512]{4,3,2,1,0:T(8,128)(2,1)S(1)}, u32[]{:S(2)}, u32[]{:S(2)}) collective-permute-start(bf16[2,2,4,32,512]{4,3,2,1,0:T(8,128)(2,1)S(1)} %bitcast.51), channel_id=1, source_target_pairs={{0,32},{1,97},{2,34},{3,99},{4,36},{5,101},{6,38},{7,103},{8,40},{... | collective-permute-start | bytes 1572872 | tf_op jit(solution)/shard_map/ppermute | solution.py:264
  118.9 10.2 %collective-permute-start.3 = (bf16[2,4,2,32,512]{4,3,2,1,0:T(8,128)(2,1)S(1)}, bf16[2,4,2,32,512]{4,3,2,1,0:T(8,128)(2,1)S(1)}, u32[]{:S(2)}, u32[]{:S(2)}) collective-permute-start(bf16[2,4,2,32,512]{4,3,2,1,0:T(8,128)(2,1)S(1)} %get-tuple-element.51), channel_id=1, source_target_pairs={{0,2},{1,7},{2,0},{3,5},{4,6},{5,3},{6,4},{7,1},{8,10},{9,15},{10,... | collective-permute-start | bytes 1572872 | tf_op jit(solution)/shard_map/ppermute | solution.py:264
  126.5 14.1 %collective-permute-start.12 = (bf16[2,2,2,32,512]{4,3,2,1,0:T(8,128)(2,1)S(1)}, bf16[2,2,2,32,512]{4,3,2,1,0:T(8,128)(2,1)S(1)}, u32[]{:S(2)}, u32[]{:S(2)}) collective-permute-start(bf16[2,2,2,32,512]{4,3,2,1,0:T(8,128)(2,1)S(1)} %get-tuple-element.56), channel_id=1, source_target_pairs={{0,32},{1,97},{2,34},{3,99},{4,36},{5,101},{6,38},{7,103},{8,40},{... | collective-permute-start | bytes 786440 | tf_op jit(solution)/shard_map/ppermute | solution.py:264
  127.9 12.7 %collective-permute-start.8 = (bf16[2,2,2,32,512]{4,3,2,1,0:T(8,128)(2,1)S(1)}, bf16[2,2,2,32,512]{4,3,2,1,0:T(8,128)(2,1)S(1)}, u32[]{:S(2)}, u32[]{:S(2)}) collective-permute-start(bf16[2,2,2,32,512]{4,3,2,1,0:T(8,128)(2,1)S(1)} %get-tuple-element.52), channel_id=1, source_target_pairs={{0,2},{1,7},{2,0},{3,5},{4,6},{5,3},{6,4},{7,1},{8,10},{9,15},{10,... | collective-permute-start | bytes 786440 | tf_op jit(solution)/shard_map/ppermute | solution.py:264
  129.2 11.4 %collective-permute-start.4 = (bf16[2,2,2,32,512]{4,3,2,1,0:T(8,128)(2,1)S(1)}, bf16[2,2,2,32,512]{4,3,2,1,0:T(8,128)(2,1)S(1)}, u32[]{:S(2)}, u32[]{:S(2)}) collective-permute-start(bf16[2,2,2,32,512]{4,3,2,1,0:T(8,128)(2,1)S(1)} %get-tuple-element.54), channel_id=1, source_target_pairs={{0,8},{1,25},{2,10},{3,27},{4,12},{5,29},{6,14},{7,31},{8,0},{9,17... | collective-permute-start | bytes 786440 | tf_op jit(solution)/shard_map/ppermute | solution.py:264
  130.8 19.3 %all-to-all-start.2 = ((f32[128,1,8]{2,1,0:T(1,128)}), f32[128,1,8]{2,1,0:T(1,128)S(1)}, u32[]{:S(2)}, u32[]{:S(2)}) async-start(f32[128,1,8]{2,1,0:T(1,128)} %bitcast.16), calls=%async_computation.2 | async-start | bytes 131072 | tf_op jit(solution)/shard_map/all_to_all | solution.py:525
  150.1 8.7 %copy-start.6 = (f32[128,1,8]{2,1,0:T(1,128)}, f32[128,1,8]{2,1,0:T(1,128)S(1)}, u32[]{:S(2)}) copy-start(f32[128,1,8]{2,1,0:T(1,128)S(1)} %all-to-all-done.2) | copy-start | bytes 12292
  150.1 15.3 %all-to-all-start.3 = ((bf16[8,32,1536]{2,1,0:T(8,128)(2,1)}), bf16[8,32,1536]{2,1,0:T(8,128)(2,1)S(1)}, u32[]{:S(2)}, u32[]{:S(2)}) async-start(bf16[8,32,1536]{2,1,0:T(8,128)(2,1)} %deal.1), calls=%async_computation.3 | async-start | bytes 1572864 | tf_op jit(solution)/shard_map/all_to_all | solution.py:332

commit v3 on v2

--- a/solution.py
+++ b/solution.py
@@ -93,23 +93,33 @@
         onehot[s * LANES : (s + 1) * LANES, :] = (node == wanted).astype(F32).astype(BF)
 
 
-def forward_kernel(place, table, features, w_in, w_out, x, hidden, logits, w_out_to, onehot, acc, nodes_x, in_buf, out_buf, nodes_sem, in_sem, out_sem):
+def weight_chunks(core, block):
+    half = block // 4
+    holder = jnp.where(half == 1, core, 1 - core)
+    turn = 1 - holder
+    a = (block % 4 + turn) % 4
+    sources = []
+    for n in range(HBLK // UNITS):
+        b = (n // 4 + turn) % 4
+        c = (n % 4 + turn) % 4
+        sources.append(((a * 4 + b) * 4 + c) * 2 + holder)
+    return sources
+
+
+def fetch_chunks(core, block, far, near, sem):
+    for n, source in enumerate(weight_chunks(core, block)):
+        pltpu.make_async_copy(far.at[source], near.at[n], sem).start()
+
+
+def first_kernel(place, table, features, w_in, w_out, x, hidden, part, onehot, acc, nodes_x, in_buf, out_buf, nodes_sem, in_sem, out_sem):
     step = pl.program_id(0)
     steps = pl.num_programs(0)
     chunks = HBLK // UNITS
     core = place[3]
 
     def fetch(block, slot):
-        half = block // 4
-        holder = jnp.where(half == 1, core, 1 - core)
-        turn = 1 - holder
-        a = (block % 4 + turn) % 4
-        for n in range(chunks):
-            b = (n // 4 + turn) % 4
-            c = (n % 4 + turn) % 4
-            source = ((a * 4 + b) * 4 + c) * 2 + holder
-            pltpu.make_async_copy(w_in.at[source], in_buf.at[slot, n], in_sem.at[slot]).start()
-            pltpu.make_async_copy(w_out.at[source], out_buf.at[slot, n], out_sem.at[slot]).start()
+        fetch_chunks(core, block, w_in, in_buf.at[slot], in_sem.at[slot])
+        fetch_chunks(core, block, w_out, out_buf.at[slot], out_sem.at[slot])
 
     @pl.when(step == 0)
     def _():
@@ -129,32 +139,85 @@
 
     pltpu.make_async_copy(w_in.at[pl.ds(0, chunks)], in_buf.at[slot], in_sem.at[slot]).wait()
     pltpu.make_async_copy(w_out.at[pl.ds(0, chunks)], out_buf.at[slot], out_sem.at[slot]).wait()
-    w_out_here = out_buf[slot].reshape(HBLK, out_buf.shape[3])
-    w_out_to[...] = w_out_here
     h = jnp.tanh(dot(in_buf[slot].reshape(HBLK, in_buf.shape[3]), x[...], (1, 1))).astype(BF)
     hidden[...] = h
-    acc[...] += dot(w_out_here, h, (0, 0))
+    acc[...] += dot(out_buf[slot].reshape(HBLK, out_buf.shape[3]), h, (0, 0))
 
     @pl.when(step == steps - 1)
     def _():
-        logits[...] = acc[...].T
-
-
-def spread_kernel(
-    cols, weights, prior_far, halo, hslot, given, table, logits_far, hidden_far, w_out_far,
-    prop, residue, errors, hidden, w_out,
-    halo_tab, prop_all, onehot, prior, logits, sems,
+        part[...] = acc[...]
+
+
+def second_kernel(
+    place, x, w_in, w_out, hidden_far, part_far, prior_far, tiles_far, halo,
+    hidden, w_out_near, logits, prior, tiles,
+    acc, in_buf, in_sem, out_sem, sems,
 ):
     step = pl.program_id(0)
-    per = weights.shape[0]
+    steps = pl.num_programs(0)
+    chunks = HBLK // UNITS
+    core = place[3]
+    done = hidden_far.shape[0]
+    pairs = ((part_far, acc), (prior_far, prior), (tiles_far, tiles), (hidden_far, hidden.at[pl.ds(0, done)]))
+    copies = [pltpu.make_async_copy(far, near, sems.at[n]) for n, (far, near) in enumerate(pairs)]
+
+    def fetch(block, slot):
+        fetch_chunks(core, block, w_in, in_buf.at[slot], in_sem.at[slot])
+
+    def fetch_out(block):
+        for n, source in enumerate(weight_chunks(core, block)):
+            pltpu.make_async_copy(w_out.at[source], w_out_near.at[block * chunks + n], out_sem.at[block]).start()
+
+    @pl.when(step == 0)
+    def _():
+        fetch(steps, 0)
+        fetch_out(steps)
+        copies[0].start()
+
+    slot = step % 2
+
+    @pl.when(step + 1 < steps)
+    def _():
+        fetch(steps + step + 1, 1 - slot)
+        fetch_out(steps + step + 1)
+
+    @pl.when(step == 0)
+    def _():
+        for copy in copies[1:]:
+            copy.start()
+        for block in range(4):
+            fetch_out(block)
+        copies[0].wait()
+
+    def out_wait(block):
+        here = w_out_near.at[pl.ds(block * chunks, chunks)]
+        pltpu.make_async_copy(w_out.at[pl.ds(0, chunks)], here, out_sem.at[block]).wait()
+
+    pltpu.make_async_copy(w_in.at[pl.ds(0, chunks)], in_buf.at[slot], in_sem.at[slot]).wait()
+    out_wait(steps + step)
+    h = jnp.tanh(dot(in_buf[slot].reshape(HBLK, in_buf.shape[3]), x[...], (1, 1))).astype(BF)
+    hidden[pl.ds(pl.multiple_of(done + step * HBLK, HBLK), HBLK), :] = h
+    w_out_here = w_out_near[pl.ds((steps + step) * chunks, chunks)].reshape(HBLK, w_out_near.shape[2])
+    acc[...] += dot(w_out_here, h, (0, 0))
+
+    @pl.when(step == steps - 1)
+    def _():
+        logits[...] = acc[...].T
+        for copy in copies[1:]:
+            copy.wait()
+        for block in range(4):
+            out_wait(block)
+
+
+def spread_kernel(
+    cols, weights, prior, halo, hslot, given, table, logits, prop, residue, errors, halo_tab, prop_all, onehot
+):
+    step = pl.program_id(0)
+    per = weights.shape[0] // pl.num_programs(0)
     classes = prior.shape[1]
-    pairs = ((prior_far, prior), (logits_far, logits), (w_out_far, w_out), (hidden_far, hidden))
-    copies = [pltpu.make_async_copy(far, near, sems.at[n]) for n, (far, near) in enumerate(pairs)]
 
     @pl.when(step == 0)
     def _():
-        for copy in copies:
-            copy.start()
         owner = lax.broadcasted_iota(jnp.int32, (LANES, LANES), 0) * HALO_SLOTS
         for b in range(2):
             near = jnp.zeros((LANES, classes), F32)
@@ -162,7 +225,6 @@
                 pick = (owner + k == hslot[b : b + 1, :]).astype(F32).astype(BF)
                 near = near + dot(pick, halo[:, k, :], (0, 0))
             halo_tab[b * LANES : (b + 1) * LANES, :] = near.astype(BF)
-        copies[0].wait()
 
     for t in range(per):
         r = step * per + t
@@ -171,13 +233,13 @@
         for m in range(4):
             pair = []
             for k in (2 * m, 2 * m + 1):
-                wide = wide + weights[t, k].astype(F32)
+                wide = wide + weights[r, k].astype(F32)
                 c = cols[r, k]
                 if k < 6:
                     pair.append(prior[pl.ds(pl.multiple_of(c * LANES, LANES), LANES), :])
                 else:
                     pair.append(halo_tab[pl.ds(pl.multiple_of((c - 16) * LANES, LANES), LANES), :])
-            left = jnp.concatenate([weights[t, 2 * m], weights[t, 2 * m + 1]], axis=1)
+            left = jnp.concatenate([weights[r, 2 * m], weights[r, 2 * m + 1]], axis=1)
             acc = acc + dot(left, jnp.concatenate(pair, axis=0), (1, 0))
         degree = jnp.sum(wide, axis=1, keepdims=True)
         mark = jnp.broadcast_to(given[pl.ds(r, 1), :], (LANES, LANES)).T
@@ -192,7 +254,6 @@
         pick_rows(table, HALO_SLOTS, BATCH_SLOTS, prop_all.shape[0], onehot)
         lane = lax.broadcasted_iota(jnp.int32, (LANES, LANES), 1)
         out = jnp.zeros((LANES, LANES), F32)
-        copies[1].wait()
         tall = 512
         for s in range(BATCH_SLOTS):
             at = slice(s * LANES, (s + 1) * LANES)
@@ -205,15 +266,15 @@
             out = jnp.where(lane == s, 0.5 * jnp.mean(differ * differ, axis=1, keepdims=True), out)
             residue[at, :] = (differ * (1.0 / 256.0)).astype(BF)
         errors[...] = out
-        copies[2].wait()
-        copies[3].wait()
 
 
 def gradients(block, w_out, hidden, residue, x):
     at = pl.ds(pl.multiple_of(block * HBLK, HBLK), HBLK)
     h = hidden[at, :]
     wide = h.astype(F32)
-    back = (dot(w_out[at, :], residue[...], (1, 1)) * (1.0 - wide * wide)).astype(BF)
+    chunks = HBLK // UNITS
+    w_out_here = w_out[pl.ds(block * chunks, chunks)].reshape(HBLK, w_out.shape[2])
+    back = (dot(w_out_here, residue[...], (1, 1)) * (1.0 - wide * wide)).astype(BF)
     return dot(h, residue[...], (1, 0)), dot(back, x[...], (1, 0))
 
 
@@ -283,6 +344,12 @@
         for j, (k, r) in enumerate(((k0, r0), (k1, r1), (k2, r2))):
             piece = k[at].astype(F32) + r[at].astype(F32)
             pieces[m, :, j * 512 : (j + 1) * 512] = piece.astype(BF)
+
+
+def finish_kernel(dealt, into, out):
+    total = jnp.sum(dealt[...].astype(F32), axis=0)
+    out[...] = total[:, :512]
+    into[...] = total[:, 512:]
 
 
 def summed_over_chips(first, second, halves):
@@ -307,20 +374,24 @@
         return exchange(value.astype(BF), 1, (dim,))
 
     _, hb, hc = halves
-    b_send = added(keep_b1, got_b1).astype(BF)
+    c1_send = added(keep_c1, got_c1, 1, 1 - hb)
+    c1_got = sent(c1_send, 1)
+    b_send = added(keep_b1, got_b1)
     b_got = sent(b_send, 0)
-    a_got = sent(added(keep_a, got_a, 2, 1 - hc), 2)
-    c_got = sent(jnp.stack([added(keep_c1, got_c1, 1, 1 - hb), added(keep_c2, got_c2, 1, 1 - hb)]), 1)
+    a_send = added(keep_a, got_a, 2, 1 - hc)
+    a_got = sent(a_send, 2)
+    c2_send = added(keep_c2, got_c2, 1, 1 - hb).astype(BF)
+    c2_got = sent(c2_send, 1)
     b = added(keep_b2, got_b2).astype(BF)
     a = added(keep_a, got_a, 2, hc).astype(BF)
     c1 = added(keep_c1, got_c1, 1, hb).astype(BF)
     c2 = added(keep_c2, got_c2, 1, hb).astype(BF)
     b_last = sent(added(b, b_got, 2, 1 - hc), 2)
     a_last = sent(added(a, a_got, 1, 1 - hb), 1)
-    c_last = sent(added(c1, c_got[0]), 0)
+    c_last = sent(added(c1, c1_got), 0)
     b = added(b, b_got, 2, hc)
     a = added(a, a_got, 1, hb)
-    c = added(c2, c_got[1])
+    c = added(c2, c2_got)
     pieces = pl.pallas_call(
         deal_kernel,
         in_specs=[pl.BlockSpec(memory_space=pltpu.VMEM)] * 6,
@@ -330,7 +401,12 @@
         name="deal",
     )(a, a_last, b, b_last, c, c_last)
     dealt = lax.all_to_all(pieces, DEV, 0, 0, axis_index_groups=corners(), tiled=True)
-    return jnp.sum(dealt.astype(F32), axis=0)
+    return pl.pallas_call(
+        finish_kernel,
+        in_specs=[pl.BlockSpec(memory_space=pltpu.VMEM)],
+        out_shape=[jax.ShapeDtypeStruct((UNITS, 1024), F32), jax.ShapeDtypeStruct((UNITS, 512), F32)],
+        name="finish",
+    )(dealt)
 
 
 def on_device(prior, label_class, labeled, features, tile_cols, tile_weights, halo_owner, halo_local, batch_owner, batch_local, w_in, w_out):
@@ -384,17 +460,15 @@
 
     slots = HALO_SLOTS + BATCH_SLOTS
     chunks = HBLK // UNITS
-    x, hidden, logits, w_out_o = pl.pallas_call(
-        forward_kernel,
-        grid=(hid // HBLK,),
+    steps = hid // HBLK // 2
+    w_in = w_in.reshape(128, UNITS, feat)
+    w_out = w_out.reshape(128, UNITS, classes)
+    x, hidden_first, part = pl.pallas_call(
+        first_kernel,
+        grid=(steps,),
         in_specs=[smem, once((LANES, slots)), hbm, hbm, hbm],
-        out_specs=[vmem, rows_at(0, rows), whole((rows, classes)), rows_at(0, classes)],
-        out_shape=[
-            pltpu.VMEM((rows, feat), BF),
-            pltpu.HBM((hid, rows), BF),
-            pltpu.HBM((rows, classes), F32),
-            pltpu.HBM((hid, classes), BF),
-        ],
+        out_specs=[vmem, rows_at(0, rows), whole((classes, rows))],
+        out_shape=[pltpu.VMEM((rows, feat), BF), pltpu.HBM((hid // 2, rows), BF), pltpu.HBM((classes, rows), F32)],
         scratch_shapes=[
             pltpu.VMEM((rows, nodes), BF),
             pltpu.VMEM((classes, rows), F32),
@@ -406,60 +480,78 @@
             pltpu.SemaphoreType.DMA((2,)),
         ],
         compiler_params=params(32),
-        cost_estimate=cost(17.2, 30, 0.0042),
-        name="forward",
+        cost_estimate=cost(10.7, 16, 0.0021),
+        name="first",
+    )(place, asked, in_hbm(features), in_hbm(w_in), in_hbm(w_out))
+    hidden, w_out_o, logits, prior_near, tiles_near = pl.pallas_call(
+        second_kernel,
+        grid=(steps,),
+        in_specs=[smem, vmem, hbm, hbm, hbm, hbm, hbm, hbm, hbm],
+        out_specs=[vmem] * 5,
+        out_shape=[
+            pltpu.VMEM((hid, rows), BF),
+            pltpu.VMEM((128, UNITS, classes), BF),
+            pltpu.VMEM((rows, classes), F32),
+            pltpu.VMEM((nodes, classes), BF),
+            pltpu.VMEM(tile_weights.shape, BF),
+        ],
+        scratch_shapes=[
+            pltpu.VMEM((classes, rows), F32),
+            pltpu.VMEM((2, chunks, UNITS, feat), BF),
+            pltpu.SemaphoreType.DMA((2,)),
+            pltpu.SemaphoreType.DMA((8,)),
+            pltpu.SemaphoreType.DMA((4,)),
+        ],
+        compiler_params=params(16),
+        cost_estimate=cost(6.5, 22, 0.0021),
+        name="second",
     )(
         place,
-        asked,
-        in_hbm(features),
-        in_hbm(w_in.reshape(128, UNITS, feat)),
-        in_hbm(w_out.reshape(128, UNITS, classes)),
+        x,
+        in_hbm(w_in),
+        in_hbm(w_out),
+        in_hbm(hidden_first),
+        in_hbm(part),
+        in_hbm(prior),
+        in_hbm(tile_weights),
+        halo,
     )
 
     row_tiles = tile_weights.shape[0]
     per = 2
     given = jnp.where(labeled == 1, label_class, -1).reshape(row_tiles, LANES)
-    prop, residue, errors, hidden, w_out_o = pl.pallas_call(
+    prop, residue, errors = pl.pallas_call(
         spread_kernel,
         grid=(row_tiles // per,),
         in_specs=[
             smem,
-            pl.BlockSpec((per, 8, LANES, LANES), lambda i: (i, 0, 0, 0)),
-            hbm,
-            once((LANES, HALO_SLOTS, classes)),
+            vmem,
+            vmem,
+            vmem,
             once((halo_count // LANES, LANES)),
             once((row_tiles, LANES)),
             once((LANES, slots)),
-            hbm,
-            hbm,
-            hbm,
+            vmem,
         ],
         out_specs=[
             pl.BlockSpec((per * LANES, classes), lambda i: (i, 0)),
             vmem,
             whole((LANES, LANES)),
-            vmem,
-            vmem,
         ],
         out_shape=[
             jax.ShapeDtypeStruct((nodes, classes), BF),
             pltpu.VMEM((rows, classes), BF),
             jax.ShapeDtypeStruct((LANES, LANES), F32),
-            pltpu.VMEM((hid, rows), BF),
-            pltpu.VMEM((hid, classes), BF),
         ],
         scratch_shapes=[
             pltpu.VMEM((halo_count, classes), BF),
             pltpu.VMEM((nodes, classes), BF),
             pltpu.VMEM((rows, nodes), BF),
-            pltpu.VMEM((nodes, classes), BF),
-            pltpu.VMEM((rows, classes), F32),
-            pltpu.SemaphoreType.DMA((4,)),
         ],
         compiler_params=params(22),
         cost_estimate=cost(4.3, 12, 0.0005),
         name="spread",
-    )(tile_cols, in_hbm(tile_weights), in_hbm(prior), halo, hslot, given, asked, in_hbm(logits), in_hbm(hidden), in_hbm(w_out_o))
+    )(tile_cols, tiles_near, prior_near, halo, hslot, given, asked, logits)
 
     partner = [(d, d ^ 1) for d in range(128)]
     part_rows = 2 * HBLK
@@ -520,7 +612,7 @@
     arrived = [peer_part(0), peer_part(1)]
     *first, _ = own_part(0, arrived[0])
     *second, errors_out = own_part(1, arrived[1])
-    total = summed_over_chips(first, second, halves)
+    grad_in, grad_out = summed_over_chips(first, second, halves)
 
     back_errors = lax.all_to_all(errors_out[:, :BATCH_SLOTS], DEV, 0, 0, tiled=True)
     row_error = pl.pallas_call(
@@ -529,7 +621,7 @@
         out_shape=jax.ShapeDtypeStruct((batch // LANES, LANES), F32),
         name="returned",
     )(back_errors, bo, brank).reshape(batch)
-    return prop, row_error, total[:, 512:], total[:, :512]
+    return prop, row_error, grad_in, grad_out
 
 
 def solution(mesh):

time: 167 us -> 166 us (level)
  waiting for transfers between devices: 32.6 us -> 29.9 us
  other arithmetic: 6.4 us -> 8.28 us
    ppermute x11 -> x12, waiting for transfers between devices: 12 us -> 9.45 us  [exchange(): return lax.ppermute(x, DEV, pairing(level, dims))]
    convert_element_type x3 -> x5, other arithmetic: 1.52 us -> 4.03 us  [sent(): return exchange(value.astype(BF), 1, (dim,))]
    another operation x3 -> x0, other arithmetic: 2.23 us -> none  [summed_over_chips(): jnp.stack([added(keep_c1, got_c1, 1, 1 - hb), added(keep_c2, got_c2, 1, 1...]
    ppermute x11 -> x12, starting transfers between devices: 11.6 us -> 11.2 us  [exchange(): return lax.ppermute(x, DEV, pairing(level, dims))]
    pallas_call x2 -> x4, Pallas kernels: 43.4 us -> 43.1 us  [the longest x1 18.1 us: on_device(): pl.pallas_call(first_kernel, grid=(steps,), in_specs=[smem, once((LANES,...]
  transfers between devices with their start and end apart: 17 -> 18, of which waited for: 6 -> 7; matrix products, arithmetic and copies ran while one was open for 4% -> 6% of each run, Pallas kernels for 30% -> 25%
where the time goes in v3:
time: 166 us; the launch traced here: 165 us
  Pallas kernels  73 us (44%)
  starting transfers between devices  46.7 us (28%)
  waiting for transfers between devices  29.9 us (18%)
  other arithmetic  8.28 us (5%)
  local copies, waits for them, and re-layouts  6.63 us (4%)
    pallas_call x1, Pallas kernels, on_device(): pl.pallas_call(first_kernel, grid=(steps,), in_specs=[smem, once((LANES,...  18.1 us
    pallas_call x2, Pallas kernels, own_part(): pl.pallas_call(partial(own_kernel, part), grid_spec=pltpu.PrefetchScalarG...  14 us
    pallas_call x1, Pallas kernels, on_device(): pl.pallas_call(second_kernel, grid=(steps,), in_specs=[smem, vmem, hbm, h...  11.8 us
    pallas_call x1, Pallas kernels, on_device(): pl.pallas_call(spread_kernel, grid=(row_tiles // per,), in_specs=[smem, v...  11.4 us
    ppermute x12, starting transfers between devices, exchange(): return lax.ppermute(x, DEV, pairing(level, dims))  11.2 us
    all_to_all x1, starting transfers between devices, on_device(): lax.all_to_all(table[:, :HALO_SLOTS + BATCH_SLOTS], DEV, 0, 0, tiled=True)  11.2 us
    pallas_call x2, Pallas kernels, peer_part(): pl.pallas_call(partial(peer_kernel, part), grid_spec=pltpu.PrefetchScalar...  10.8 us
    all_to_all x1, starting transfers between devices, on_device(): lax.all_to_all(errors_out[:, :BATCH_SLOTS], DEV, 0, 0, tiled=True)  10.1 us
  transfers between devices with their start and end apart: 18, of which 7 were waited for; matrix products, arithmetic and copies ran while one was open for 6% of the time, Pallas kernels for 25%

profile of v3, /device:TPU:0, one launch (start us, length us, event | category | flops | bytes accessed | tf_op | source)
XLA Modules:
  0.0 165.5 jit_solution(7922245749004605535)
XLA Ops:
  0.6 1.9 %request.1 = (s32[128,128]{1,0:T(8,128)}, s32[2,128]{1,0:T(2,128)}, s32[4,128]{1,0:T(4,128)}) custom-call(s32[2,128]{1,0:T(2,128)} %bitcast.54, s32[2,128]{1,0:T(2,128)} %bitcast.55, s32[4,128]{1,0:T(4,128)} %bitcast.50, s32[4,128]{1,0:T(4,128)} %bitcast.52), custom_call_target="tpu_custom_call" | custom-call | tf_op jit(solution)/shard_map/request/pallas_call | solution.py:432
  2.5 11.2 %all-to-all-start = ((s32[128,1,12]{2,1,0:T(1,128)}), s32[128,1,12]{2,1,0:T(1,128)S(1)}, u32[]{:S(2)}, u32[]{:S(2)}) async-start(s32[128,1,12]{2,1,0:T(1,128)} %bitcast.49), calls=%async_computation | async-start | bytes 131072 | tf_op jit(solution)/shard_map/all_to_all | solution.py:447
  13.8 0.7 select_bitcast_fusion.given
  14.5 0.8 copy.19.cols
  15.3 0.1 stack.23.place
  15.3 7.8 %all-to-all-done = s32[128,1,12]{2,1,0:T(1,128)S(1)} async-done(((s32[128,1,12]{2,1,0:T(1,128)}), s32[128,1,12]{2,1,0:T(1,128)S(1)}, u32[]{:S(2)}, u32[]{:S(2)}) %all-to-all-start) | async-done | bytes 6176 | tf_op jit(solution)/shard_map/all_to_all | solution.py:447
  23.2 0.1 reshape.82
  23.3 3.8 %gather_fusion = bf16[512,512]{1,0:T(8,128)(2,1)S(1)} fusion(bf16[2048,512]{1,0:T(8,128)(2,1)} %prior_far.1, s32[1024]{0:T(1024)S(1)} %pad_clamp_fusion), kind=kCustom, calls=%fused_computation | custom fusion | bytes 1050624 | tf_op jit(solution)/shard_map/gather | solution.py:449
  27.2 0.9 reshape.81
  28.1 4.8 %all-to-all-start.1 = ((bf16[128,4,512]{2,1,0:T(4,128)(2,1)}), bf16[128,4,512]{2,1,0:T(4,128)(2,1)S(1)}, u32[]{:S(2)}, u32[]{:S(2)}) async-start(bf16[128,4,512]{2,1,0:T(4,128)(2,1)} %reshape.81), calls=%async_computation.1 | async-start | bytes 1048576 | tf_op jit(solution)/shard_map/all_to_all | solution.py:450
  32.9 18.1 %first.1 = (bf16[1024,1024]{1,0:T(8,128)(2,1)S(1)}, bf16[2048,1024]{1,0:T(8,128)(2,1)}, f32[512,1024]{1,0:T(8,128)}) custom-call(s32[5]{0:T(128)S(1)} %stack.23.place, s32[128,12]{1,0:T(8,128)S(1)} %bitcast.33, bf16[2048,1024]{1,0:T(8,128)(2,1)} %features.1, bf16[128,32,1024]{2,1,0:T(8,128)(2,1)} %bitcast.35, bf16[128,32,512]{2,1,0:T(8,128)(2,1)} %bitcast.37), custom_call_target="tpu_custom_call" | custom-call | flops 10700000256 | bytes 16777216 | tf_op jit(solution)/shard_map/first/pallas_call | solution.py:466
  51.0 0.0 all-to-all-done.1.halo
  51.0 0.0 copy-start
  51.0 11.8 %second.1 = (bf16[4096,1024]{1,0:T(8,128)(2,1)S(1)}, bf16[128,32,512]{2,1,0:T(8,128)(2,1)S(1)}, f32[1024,512]{1,0:T(8,128)S(1)}, bf16[2048,512]{1,0:T(8,128)(2,1)S(1)}, bf16[16,8,128,128]{3,2,1,0:T(8,128)(2,1)S(1)}) custom-call(s32[5]{0:T(128)S(1)} %stack.23.place, bf16[1024,1024]{1,0:T(8,128)(2,1)S(1)} %get-tuple-element.32.x, ...), custom_call_target="tpu_custom_call" | custom-call | flops 6499999744 | bytes 23068672 | tf_op jit(solution)/shard_map/second/pallas_call | solution.py:486
  62.8 11.4 %spread.1 = (bf16[2048,512]{1,0:T(8,128)(2,1)}, bf16[1024,512]{1,0:T(8,128)(2,1)S(1)}, f32[128,128]{1,0:T(8,128)S(1)}) custom-call(s32[16,8]{1,0:T(8,128)S(1)} %copy.19.cols, bf16[16,8,128,128]{3,2,1,0:T(8,128)(2,1)S(1)} %get-tuple-element.35.weights, bf16[2048,512]{1,0:T(8,128)(2,1)S(1)} %get-tuple-element.36.prior, ...), custom_call_target="tpu_custom_call" | custom-call | flops 4300000256 | bytes 12582912 | tf_op jit(solution)/shard_map/spread/pallas_call | solution.py:523
  74.2 5.4 %shard_map.149 = bf16[1024,1536]{1,0:T(8,128)(2,1)S(1)} custom-call(s32[5]{0:T(128)S(1)} %stack.23.place, bf16[128,32,512]{2,1,0:T(8,128)(2,1)S(1)} %get-tuple-element.40.w_out, bf16[4096,1024]{1,0:T(8,128)(2,1)S(1)} %get-tuple-element.41.hidden, bf16[1024,512]{1,0:T(8,128)(2,1)S(1)} %get-tuple-element.42.residue, bf16[1024,1024]{1,0:T(8,128)(2,1)S(1)} %get-tuple-element.32.x), custom_call_target="tpu_custom_call" | custom-call | flops 4300000256 | bytes 9437184 | tf_op jit(solution)/shard_map/pallas_call | solution.py:560
  79.6 0.1 collective-permute-start.1
  79.7 5.4 %shard_map.147 = bf16[1024,1536]{1,0:T(8,128)(2,1)S(1)} custom-call(s32[5]{0:T(128)S(1)} %stack.23.place, bf16[128,32,512]{2,1,0:T(8,128)(2,1)S(1)} %get-tuple-element.40.w_out, bf16[4096,1024]{1,0:T(8,128)(2,1)S(1)} %get-tuple-element.41.hidden, bf16[1024,512]{1,0:T(8,128)(2,1)S(1)} %get-tuple-element.42.residue, bf16[1024,1024]{1,0:T(8,128)(2,1)S(1)} %get-tuple-element.32.x), custom_call_target="tpu_custom_call" | custom-call | flops 4300000256 | bytes 9437184 | tf_op jit(solution)/shard_map/pallas_call | solution.py:560
  85.1 0.6 collective-permute-start
  85.7 0.0 collective-permute-done.1.arrived
  85.7 6.9 %shard_map.150 = (bf16[1024,512]{1,0:T(8,128)(2,1)}, bf16[2,256,512]{2,1,0:T(8,128)(2,1)}, bf16[2,256,512]{2,1,0:T(8,128)(2,1)}, bf16[2,4,64,512]{3,2,1,0:T(8,12...) custom-call(s32[5]{0:T(128)S(1)} %stack.23.place, bf16[128,32,512]{2,1,0:T(8,128)(2,1)S(1)} %get-tuple-element.40.w_out, ...), custom_call_target="tpu_custom_call" | custom-call | flops 4300000256 | bytes 12582912 | tf_op jit(solution)/shard_map/pallas_call | solution.py:585
  92.6 1.0 collective-permute-start.11
  93.6 1.5 collective-permute-start.2
  95.1 0.0 collective-permute-done.arrived
  95.1 7.1 %shard_map.148 = (bf16[1024,512]{1,0:T(8,128)(2,1)}, bf16[2,256,512]{2,1,0:T(8,128)(2,1)}, bf16[2,256,512]{2,1,0:T(8,128)(2,1)}, bf16[2,4,64,512]{3,2,1,0:T(8,12...) custom-call(s32[5]{0:T(128)S(1)} %stack.23.place, bf16[128,32,512]{2,1,0:T(8,128)(2,1)S(1)} %get-tuple-element.40.w_out, ...), custom_call_target="tpu_custom_call" | custom-call | flops 4300000256 | bytes 12582912 | tf_op jit(solution)/shard_map/pallas_call | solution.py:585
  102.2 0.4 collective-permute-start.9
  102.6 1.5 collective-permute-start.6
  104.1 0.5 collective-permute-start.5
  104.6 0.0 collective-permute-done.11
  104.6 1.2 add_convert_fusion.5
  105.8 1.6 collective-permute-start.12
  107.4 4.3 %collective-permute-done.9 = bf16[2,4,64,512]{3,2,1,0:T(8,128)(2,1)S(1)} collective-permute-done((bf16[2,4,64,512]{3,2,1,0:T(8,128)(2,1)}, bf16[2,4,64,512]{3,2,1,0:T(8,128)(2,1)S(1)}, u32[]{:S(2)}, u32[]{:S(2)}) %collective-permute-start.9) | collective-permute-done | bytes 524320 | tf_op jit(solution)/shard_map/ppermute | solution.py:325
  111.7 1.7 %add_convert_fusion.7 = bf16[2,2,2,32,512]{4,3,2,1,0:T(8,128)(2,1)} fusion(bf16[2,4,2,32,512]{4,3,2,1,0:T(8,128)(2,1)S(1)} %bitcast.44, s32[]{:T(128)S(6)} %select_n.104, bf16[2,4,2,32,512]{4,3,2,1,0:T(8,128)(2,1)} %bitcast.42), kind=kLoop, calls=%fused_computation.9 | loop fusion | flops 524288 | bytes 786436 | tf_op jit(solution)/shard_map/convert_element_type | solution.py:383
  113.4 1.5 collective-permute-start.10
  114.9 0.0 collective-permute-done.6
  114.9 0.1 add_convert_fusion
  115.1 0.6 collective-permute-start.7
  115.6 0.0 collective-permute-done.2
  115.6 1.6 add_convert_fusion.3
  117.2 0.4 collective-permute-start.3
  117.6 0.0 collective-permute-done.5
  117.6 0.1 add_convert_fusion.1
  117.8 2.7 %collective-permute-done.12 = bf16[2,2,2,32,512]{4,3,2,1,0:T(8,128)(2,1)S(1)} collective-permute-done((bf16[2,2,2,32,512]{4,3,2,1,0:T(8,128)(2,1)S(1)}, bf16[2,2,2,32,512]{4,3,2,1,0:T(8,128)(2,1)S(1)}, u32[]{:S(2)}, u32[]{:S(2)}) %collective-permute-start.12) | collective-permute-done | bytes 262176 | tf_op jit(solution)/shard_map/ppermute | solution.py:325
  120.4 1.8 %add_convert_fusion.4 = bf16[2,2,2,32,512]{4,3,2,1,0:T(8,128)(2,1)} fusion(bf16[2,2,2,32,512]{4,3,2,1,0:T(8,128)(2,1)S(1)} %collective-permute-done.12, bf16[2,4,2,32,512]{4,3,2,1,0:T(8,128)(2,1)} %bitcast.26, s32[]{:T(128)S(6)} %select_n.102, bf16[2,4,2,32,512]{4,3,2,1,0:T(8,128)(2,1)S(1)} %bitcast.47), kind=kLoop, calls=%fused_computation.5 | loop fusion | flops 1048576 | bytes 1048580 | tf_op jit(solution)/shard_map/convert_element_type | solution.py:374
  122.2 1.3 collective-permute-start.13
  123.5 0.8 collective-permute-done.7
  124.3 0.1 add_convert_fusion.9
  124.5 0.4 collective-permute-start.8
  124.8 1.6 collective-permute-done.3
  126.5 0.8 add_convert_fusion.10
  127.3 0.5 collective-permute-start.4
  127.8 10.1 %all-to-all-start.2 = ((f32[128,1,8]{2,1,0:T(1,128)}), f32[128,1,8]{2,1,0:T(1,128)S(1)}, u32[]{:S(2)}, u32[]{:S(2)}) async-start(f32[128,1,8]{2,1,0:T(1,128)} %bitcast.16), calls=%async_computation.2 | async-start | bytes 131072 | tf_op jit(solution)/shard_map/all_to_all | solution.py:617
  138.0 0.0 collective-permute-done.10
  138.0 0.1 convert_add_fusion.k2
  138.1 0.0 collective-permute-done.13.r2
  138.1 0.0 collective-permute-done.8.r1
  138.1 0.0 collective-permute-done.4.r0
  138.2 1.0 deal.1
  139.2 8.3 %all-to-all-done.2 = f32[128,1,8]{2,1,0:T(1,128)S(1)} async-done(((f32[128,1,8]{2,1,0:T(1,128)}), f32[128,1,8]{2,1,0:T(1,128)S(1)}, u32[]{:S(2)}, u32[]{:S(2)}) %all-to-all-start.2) | async-done | bytes 4128 | tf_op jit(solution)/shard_map/all_to_all | solution.py:617
  147.5 8.7 %all-to-all-start.3 = ((bf16[8,32,1536]{2,1,0:T(8,128)(2,1)}), bf16[8,32,1536]{2,1,0:T(8,128)(2,1)S(1)}, u32[]{:S(2)}, u32[]{:S(2)}) async-start(bf16[8,32,1536]{2,1,0:T(8,128)(2,1)} %deal.1), calls=%async_computation.3 | async-start | bytes 1572864 | tf_op jit(solution)/shard_map/all_to_all | solution.py:403
  156.2 2.2 %returned.1 = f32[4,128]{1,0:T(4,128)} custom-call(f32[128,8]{1,0:T(8,128)} %bitcast.48, s32[4,128]{1,0:T(4,128)} %bitcast.51, s32[4,128]{1,0:T(4,128)} %get-tuple-element.45.brank), custom_call_target="tpu_custom_call" | custom-call | tf_op jit(solution)/shard_map/returned/pallas_call | solution.py:618
  158.4 4.3 %all-to-all-done.3.dealt = bf16[8,32,1536]{2,1,0:T(8,128)(2,1)S(1)} async-done(((bf16[8,32,1536]{2,1,0:T(8,128)(2,1)}), bf16[8,32,1536]{2,1,0:T(8,128)(2,1)S(1)}, u32[]{:S(2)}, u32[]{:S(2)}) %all-to-all-start.3) | async-done | bytes 786464 | tf_op jit(solution)/shard_map/all_to_all | solution.py:403
  162.7 0.9 copy-done.1
  163.6 1.9 %finish.1 = (f32[32,1024]{1,0:T(8,128)}, f32[32,512]{1,0:T(8,128)}) custom-call(bf16[8,32,1536]{2,1,0:T(8,128)(2,1)} %copy-done.1), custom_call_target="tpu_custom_call" | custom-call | tf_op jit(solution)/shard_map/finish/pallas_call | solution.py:404
  (16 shorter events, 0.0 us)
Async XLA Ops:
  2.5 20.6 %all-to-all-start = ((s32[128,1,12]{2,1,0:T(1,128)}), s32[128,1,12]{2,1,0:T(1,128)S(1)}, u32[]{:S(2)}, u32[]{:S(2)}) async-start(s32[128,1,12]{2,1,0:T(1,128)} %bitcast.49), calls=%async_computation | async-start | bytes 131072 | tf_op jit(solution)/shard_map/all_to_all | solution.py:447
  28.1 22.9 %all-to-all-start.1 = ((bf16[128,4,512]{2,1,0:T(4,128)(2,1)}), bf16[128,4,512]{2,1,0:T(4,128)(2,1)S(1)}, u32[]{:S(2)}, u32[]{:S(2)}) async-start(bf16[128,4,512]{2,1,0:T(4,128)(2,1)} %reshape.81), calls=%async_computation.1 | async-start | bytes 1048576 | tf_op jit(solution)/shard_map/all_to_all | solution.py:450
  51.0 11.8 %copy-start = (s32[2,128]{1,0:T(2,128)S(1)}, s32[2,128]{1,0:T(2,128)}, u32[]{:S(2)}) copy-start(s32[2,128]{1,0:T(2,128)} %get-tuple-element.37.hslot) | copy-start | bytes 3076
  79.6 6.1 %collective-permute-start.1 = (bf16[1024,1536]{1,0:T(8,128)(2,1)S(1)}, bf16[1024,1536]{1,0:T(8,128)(2,1)S(1)}, u32[]{:S(2)}, u32[]{:S(2)}) collective-permute-start(bf16[1024,1536]{1,0:T(8,128)(2,1)S(1)} %shard_map.149), channel_id=1, source_target_pairs={{0,1},{1,0},{2,3},{3,2},{4,5},{5,4},{6,7},{7,6},{8,9},{9,8},{10,11... | collective-permute-start | bytes 9437192 | tf_op jit(solution)/shard_map/ppermute | solution.py:577
  85.1 10.0 %collective-permute-start = (bf16[1024,1536]{1,0:T(8,128)(2,1)S(1)}, bf16[1024,1536]{1,0:T(8,128)(2,1)S(1)}, u32[]{:S(2)}, u32[]{:S(2)}) collective-permute-start(bf16[1024,1536]{1,0:T(8,128)(2,1)S(1)} %shard_map.147), channel_id=1, source_target_pairs={{0,1},{1,0},{2,3},{3,2},{4,5},{5,4},{6,7},{7,6},{8,9},{9,8},{10,11... | collective-permute-start | bytes 9437192 | tf_op jit(solution)/shard_map/ppermute | solution.py:577
  92.6 12.1 %collective-permute-start.11 = (bf16[2,4,64,512]{3,2,1,0:T(8,128)(2,1)}, bf16[2,4,64,512]{3,2,1,0:T(8,128)(2,1)}, u32[]{:S(2)}, u32[]{:S(2)}) collective-permute-start(bf16[2,4,64,512]{3,2,1,0:T(8,128)(2,1)} %get-tuple-element.55), channel_id=1, source_target_pairs={{0,2},{1,7},{2,0},{3,5},{4,6},{5,3},{6,4},{7,1},{8,10},{9,15},{10,... | collective-permute-start | bytes 1572872 | tf_op jit(solution)/shard_map/ppermute | solution.py:325
  93.5 21.4 %copy-start.4 = (bf16[2,256,512]{2,1,0:T(8,128)(2,1)S(1)}, bf16[2,256,512]{2,1,0:T(8,128)(2,1)}, u32[]{:S(2)}) copy-start(bf16[2,256,512]{2,1,0:T(8,128)(2,1)} %get-tuple-element.50) | copy-start | bytes 1572868
  93.6 22.1 %collective-permute-start.2 = (bf16[1024,512]{1,0:T(8,128)(2,1)}, bf16[1024,512]{1,0:T(8,128)(2,1)}, u32[]{:S(2)}, u32[]{:S(2)}) collective-permute-start(bf16[1024,512]{1,0:T(8,128)(2,1)} %get-tuple-element.47), channel_id=1, source_target_pairs={{0,32},{1,97},{2,34},{3,99},{4,36},{5,101},{6,38},{7,103},{8,40},{... | collective-permute-start | bytes 3145736 | tf_op jit(solution)/shard_map/ppermute | solution.py:325
  102.2 13.4 %copy-start.2 = (bf16[1024,512]{1,0:T(8,128)(2,1)S(1)}, bf16[1024,512]{1,0:T(8,128)(2,1)}, u32[]{:S(2)}) copy-start(bf16[1024,512]{1,0:T(8,128)(2,1)} %get-tuple-element.46) | copy-start | bytes 3145732
  102.2 9.5 %collective-permute-start.9 = (bf16[2,4,64,512]{3,2,1,0:T(8,128)(2,1)}, bf16[2,4,64,512]{3,2,1,0:T(8,128)(2,1)S(1)}, u32[]{:S(2)}, u32[]{:S(2)}) collective-permute-start(bf16[2,4,64,512]{3,2,1,0:T(8,128)(2,1)} %get-tuple-element.53), channel_id=1, source_target_pairs={{0,2},{1,7},{2,0},{3,5},{4,6},{5,3},{6,4},{7,1},{8,10},{9,15},{10,... | collective-permute-start | bytes 1572872 | tf_op jit(solution)/shard_map/ppermute | solution.py:325
  102.6 12.3 %collective-permute-start.6 = (bf16[2,256,512]{2,1,0:T(8,128)(2,1)}, bf16[2,256,512]{2,1,0:T(8,128)(2,1)S(1)}, u32[]{:S(2)}, u32[]{:S(2)}) collective-permute-start(bf16[2,256,512]{2,1,0:T(8,128)(2,1)} %get-tuple-element.51), channel_id=1, source_target_pairs={{0,8},{1,25},{2,10},{3,27},{4,12},{5,29},{6,14},{7,31},{8,0},{9,17... | collective-permute-start | bytes 1572872 | tf_op jit(solution)/shard_map/ppermute | solution.py:325
  104.1 13.5 %collective-permute-start.5 = (bf16[2,256,512]{2,1,0:T(8,128)(2,1)}, bf16[2,256,512]{2,1,0:T(8,128)(2,1)S(1)}, u32[]{:S(2)}, u32[]{:S(2)}) collective-permute-start(bf16[2,256,512]{2,1,0:T(8,128)(2,1)} %get-tuple-element.49), channel_id=1, source_target_pairs={{0,8},{1,25},{2,10},{3,27},{4,12},{5,29},{6,14},{7,31},{8,0},{9,17... | collective-permute-start | bytes 1572872 | tf_op jit(solution)/shard_map/ppermute | solution.py:325
  104.6 13.0 %copy-start.3 = (bf16[2,256,512]{2,1,0:T(8,128)(2,1)S(1)}, bf16[2,256,512]{2,1,0:T(8,128)(2,1)}, u32[]{:S(2)}) copy-start(bf16[2,256,512]{2,1,0:T(8,128)(2,1)} %get-tuple-element.48) | copy-start | bytes 1572868
  105.8 14.6 %collective-permute-start.12 = (bf16[2,2,2,32,512]{4,3,2,1,0:T(8,128)(2,1)S(1)}, bf16[2,2,2,32,512]{4,3,2,1,0:T(8,128)(2,1)S(1)}, u32[]{:S(2)}, u32[]{:S(2)}) collective-permute-start(bf16[2,2,2,32,512]{4,3,2,1,0:T(8,128)(2,1)S(1)} %add_convert_fusion.5), channel_id=1, source_target_pairs={{0,8},{1,25},{2,10},{3,27},{4,12},{5,29},{6,14},{7,31},{8,0},{9,17... | collective-permute-start | bytes 786440 | tf_op jit(solution)/shard_map/ppermute | solution.py:325
  113.4 24.6 %collective-permute-start.10 = (bf16[2,2,2,32,512]{4,3,2,1,0:T(8,128)(2,1)}, bf16[2,2,2,32,512]{4,3,2,1,0:T(8,128)(2,1)S(1)}, u32[]{:S(2)}, u32[]{:S(2)}) collective-permute-start(bf16[2,2,2,32,512]{4,3,2,1,0:T(8,128)(2,1)} %add_convert_fusion.7), channel_id=1, source_target_pairs={{0,8},{1,25},{2,10},{3,27},{4,12},{5,29},{6,14},{7,31},{8,0},{9,17... | collective-permute-start | bytes 786440 | tf_op jit(solution)/shard_map/ppermute | solution.py:325
  114.9 5.5 %copy-start.6 = (bf16[2,4,64,512]{3,2,1,0:T(8,128)(2,1)S(1)}, bf16[2,4,64,512]{3,2,1,0:T(8,128)(2,1)}, u32[]{:S(2)}) copy-start(bf16[2,4,64,512]{3,2,1,0:T(8,128)(2,1)} %get-tuple-element.54) | copy-start | bytes 1572868
  115.1 9.3 %collective-permute-start.7 = (bf16[2,2,4,32,512]{4,3,2,1,0:T(8,128)(2,1)S(1)}, bf16[2,2,4,32,512]{4,3,2,1,0:T(8,128)(2,1)S(1)}, u32[]{:S(2)}, u32[]{:S(2)}) collective-permute-start(bf16[2,2,4,32,512]{4,3,2,1,0:T(8,128)(2,1)S(1)} %bitcast.41), channel_id=1, source_target_pairs={{0,32},{1,97},{2,34},{3,99},{4,36},{5,101},{6,38},{7,103},{8,40},{... | collective-permute-start | bytes 1572872 | tf_op jit(solution)/shard_map/ppermute | solution.py:325
  117.2 9.3 %collective-permute-start.3 = (bf16[2,4,2,32,512]{4,3,2,1,0:T(8,128)(2,1)S(1)}, bf16[2,4,2,32,512]{4,3,2,1,0:T(8,128)(2,1)S(1)}, u32[]{:S(2)}, u32[]{:S(2)}) collective-permute-start(bf16[2,4,2,32,512]{4,3,2,1,0:T(8,128)(2,1)S(1)} %get-tuple-element.59), channel_id=1, source_target_pairs={{0,2},{1,7},{2,0},{3,5},{4,6},{5,3},{6,4},{7,1},{8,10},{9,15},{10,... | collective-permute-start | bytes 1572872 | tf_op jit(solution)/shard_map/ppermute | solution.py:325
  117.6 20.4 %copy-start.5 = (bf16[2,4,64,512]{3,2,1,0:T(8,128)(2,1)S(1)}, bf16[2,4,64,512]{3,2,1,0:T(8,128)(2,1)}, u32[]{:S(2)}) copy-start(bf16[2,4,64,512]{3,2,1,0:T(8,128)(2,1)} %get-tuple-element.52) | copy-start | bytes 1572868
  122.2 15.9 %collective-permute-start.13 = (bf16[2,2,2,32,512]{4,3,2,1,0:T(8,128)(2,1)}, bf16[2,2,2,32,512]{4,3,2,1,0:T(8,128)(2,1)S(1)}, u32[]{:S(2)}, u32[]{:S(2)}) collective-permute-start(bf16[2,2,2,32,512]{4,3,2,1,0:T(8,128)(2,1)} %add_convert_fusion.4), channel_id=1, source_target_pairs={{0,32},{1,97},{2,34},{3,99},{4,36},{5,101},{6,38},{7,103},{8,40},{... | collective-permute-start | bytes 786440 | tf_op jit(solution)/shard_map/ppermute | solution.py:325
  124.5 13.7 %collective-permute-start.8 = (bf16[2,2,2,32,512]{4,3,2,1,0:T(8,128)(2,1)S(1)}, bf16[2,2,2,32,512]{4,3,2,1,0:T(8,128)(2,1)S(1)}, u32[]{:S(2)}, u32[]{:S(2)}) collective-permute-start(bf16[2,2,2,32,512]{4,3,2,1,0:T(8,128)(2,1)S(1)} %get-tuple-element.60), channel_id=1, source_target_pairs={{0,2},{1,7},{2,0},{3,5},{4,6},{5,3},{6,4},{7,1},{8,10},{9,15},{10,... | collective-permute-start | bytes 786440 | tf_op jit(solution)/shard_map/ppermute | solution.py:325
  127.3 10.8 %collective-permute-start.4 = (bf16[2,2,2,32,512]{4,3,2,1,0:T(8,128)(2,1)}, bf16[2,2,2,32,512]{4,3,2,1,0:T(8,128)(2,1)S(1)}, u32[]{:S(2)}, u32[]{:S(2)}) collective-permute-start(bf16[2,2,2,32,512]{4,3,2,1,0:T(8,128)(2,1)} %get-tuple-element.62), channel_id=1, source_target_pairs={{0,8},{1,25},{2,10},{3,27},{4,12},{5,29},{6,14},{7,31},{8,0},{9,17... | collective-permute-start | bytes 786440 | tf_op jit(solution)/shard_map/ppermute | solution.py:325
  127.8 19.6 %all-to-all-start.2 = ((f32[128,1,8]{2,1,0:T(1,128)}), f32[128,1,8]{2,1,0:T(1,128)S(1)}, u32[]{:S(2)}, u32[]{:S(2)}) async-start(f32[128,1,8]{2,1,0:T(1,128)} %bitcast.16), calls=%async_computation.2 | async-start | bytes 131072 | tf_op jit(solution)/shard_map/all_to_all | solution.py:617
  147.5 8.7 %copy-start.7 = (f32[128,1,8]{2,1,0:T(1,128)}, f32[128,1,8]{2,1,0:T(1,128)S(1)}, u32[]{:S(2)}) copy-start(f32[128,1,8]{2,1,0:T(1,128)S(1)} %all-to-all-done.2) | copy-start | bytes 12292
  147.5 15.3 %all-to-all-start.3 = ((bf16[8,32,1536]{2,1,0:T(8,128)(2,1)}), bf16[8,32,1536]{2,1,0:T(8,128)(2,1)S(1)}, u32[]{:S(2)}, u32[]{:S(2)}) async-start(bf16[8,32,1536]{2,1,0:T(8,128)(2,1)} %deal.1), calls=%async_computation.3 | async-start | bytes 1572864 | tf_op jit(solution)/shard_map/all_to_all | solution.py:403
  162.7 0.9 copy-start.1

commit v4 on v3

--- a/solution.py
+++ b/solution.py
@@ -76,14 +76,12 @@
     table[...] = out.astype(jnp.int32) - 1
 
 
-def returned_kernel(errors, bo, brank, out):
-    device = lax.broadcasted_iota(jnp.int32, (LANES, LANES), 0)
-    for i in range(bo.shape[0]):
-        total = jnp.zeros((LANES, LANES), F32)
-        for s in range(BATCH_SLOTS):
-            hit = (device == bo[i : i + 1, :]) & (brank[i : i + 1, :] == s)
-            total = total + jnp.where(hit, errors[:, s : s + 1], 0.0)
-        out[i : i + 1, :] = jnp.sum(total, axis=0, keepdims=True)
+def device_at(core, high, low):
+    device = 0
+    for d in (2, 1, 0):
+        spot = (2 * ((high >> d) & 1) + ((low >> d) & 1) + 1 - core) % 4
+        device = device * 4 + spot
+    return device * 2 + core
 
 
 def pick_rows(table, first, count, nodes, onehot):
@@ -305,7 +303,17 @@
             keep_c[0] = right[:, half]
             send_c[0] = right[:, 1 - half]
 
-    errors_to[...] = errors[...]
+    if not part:
+        errors_to[...] = errors[...]
+        return
+
+    @pl.when(pl.program_id(0) == 0)
+    def _():
+        row = lax.broadcasted_iota(jnp.int32, (LANES, LANES), 0)
+        device = lax.broadcasted_iota(jnp.int32, (LANES, LANES), 1)
+        pick = (device_at(row >> 6, (row >> 3) & 7, row & 7) == device).astype(F32).astype(BF)
+        moved = [dot(pick, third, (1, 0)) for third in thirds(errors[...])]
+        errors_to[...] = moved[0] + moved[1] + moved[2]
 
 
 def pairing(level, dims):
@@ -326,33 +334,50 @@
 
 
 def corners():
-    groups = []
-    for core in range(2):
-        for high in range(8):
-            group = []
-            for low in range(8):
-                shifted = [2 * ((high >> (2 - d)) & 1) + ((low >> (2 - d)) & 1) for d in range(3)]
-                a, b, c = ((v + 1 - core) % 4 for v in shifted)
-                group.append(((a * 4 + b) * 4 + c) * 2 + core)
-            groups.append(group)
-    return groups
-
-
-def deal_kernel(k0, r0, k1, r1, k2, r2, pieces):
+    return [[device_at(core, high, low) for low in range(8)] for core in range(2) for high in range(8)]
+
+
+def across():
+    return [[device_at(core, high, low) for core in range(2) for high in range(8)] for low in range(8)]
+
+
+def thirds(value):
+    high = value.astype(BF)
+    rest = value - high.astype(F32)
+    middle = rest.astype(BF)
+    return high, middle, (rest - middle.astype(F32)).astype(BF)
+
+
+def deal_kernel(k0, r0, k1, r1, k2, r2, errors, pieces):
     for m in range(8):
         at = (m >> 2, (m >> 1) & 1, m & 1)
         for j, (k, r) in enumerate(((k0, r0), (k1, r1), (k2, r2))):
             piece = k[at].astype(F32) + r[at].astype(F32)
-            pieces[m, :, j * 512 : (j + 1) * 512] = piece.astype(BF)
-
-
-def finish_kernel(dealt, into, out):
-    total = jnp.sum(dealt[...].astype(F32), axis=0)
+            pieces[m, :UNITS, j * 512 : (j + 1) * 512] = piece.astype(BF)
+        for n, third in enumerate(thirds(errors[:, m, :])):
+            pieces[m, UNITS:, n * LANES : n * LANES + BATCH_SLOTS] = third
+
+
+def finish_kernel(dealt, bo, brank, into, out, row_error):
+    total = jnp.sum(dealt[:, :UNITS, :].astype(F32), axis=0)
     out[...] = total[:, :512]
     into[...] = total[:, 512:]
-
-
-def summed_over_chips(first, second, halves):
+    mine = []
+    for m in range(8):
+        parts = [dealt[m, UNITS:, n * LANES : n * LANES + BATCH_SLOTS].astype(F32) for n in range(3)]
+        mine.append(parts[0] + parts[1] + parts[2])
+    errors = jnp.concatenate(mine, axis=0)
+    row = lax.broadcasted_iota(jnp.int32, (LANES, LANES), 0)
+    device = device_at((row >> 3) & 1, row & 7, row >> 4)
+    for i in range(bo.shape[0]):
+        found = jnp.zeros((LANES, LANES), F32)
+        for s in range(BATCH_SLOTS):
+            hit = (device == bo[i : i + 1, :]) & (brank[i : i + 1, :] == s)
+            found = found + jnp.where(hit, errors[:, s : s + 1], 0.0)
+        row_error[i : i + 1, :] = jnp.sum(found, axis=0, keepdims=True)
+
+
+def summed_over_chips(first, second, halves, errors, bo, brank):
     shape_a, shape_b, shape_c = (2, 4, 4, UNITS, 512), (2, 2, 4, UNITS, 512), (2, 4, 2, UNITS, 512)
     send_a, send_b1, keep_b1, send_c1, keep_c1 = first
     keep_a, send_b2, keep_b2, send_c2, keep_c2 = second
@@ -374,6 +399,7 @@
         return exchange(value.astype(BF), 1, (dim,))
 
     _, hb, hc = halves
+    arrived = lax.all_to_all(errors, DEV, 0, 0, axis_index_groups=across(), tiled=True)
     c1_send = added(keep_c1, got_c1, 1, 1 - hb)
     c1_got = sent(c1_send, 1)
     b_send = added(keep_b1, got_b1)
@@ -394,19 +420,23 @@
     c = added(c2, c2_got)
     pieces = pl.pallas_call(
         deal_kernel,
-        in_specs=[pl.BlockSpec(memory_space=pltpu.VMEM)] * 6,
+        in_specs=[pl.BlockSpec(memory_space=pltpu.VMEM)] * 7,
         out_specs=pl.BlockSpec(memory_space=pltpu.VMEM),
-        out_shape=jax.ShapeDtypeStruct((8, UNITS, 1536), BF),
+        out_shape=jax.ShapeDtypeStruct((8, UNITS + 16, 1536), BF),
         compiler_params=params(16),
         name="deal",
-    )(a, a_last, b, b_last, c, c_last)
+    )(a, a_last, b, b_last, c, c_last, arrived.reshape(16, 8, BATCH_SLOTS))
     dealt = lax.all_to_all(pieces, DEV, 0, 0, axis_index_groups=corners(), tiled=True)
     return pl.pallas_call(
         finish_kernel,
-        in_specs=[pl.BlockSpec(memory_space=pltpu.VMEM)],
-        out_shape=[jax.ShapeDtypeStruct((UNITS, 1024), F32), jax.ShapeDtypeStruct((UNITS, 512), F32)],
+        in_specs=[pl.BlockSpec(memory_space=pltpu.VMEM)] * 3,
+        out_shape=[
+            jax.ShapeDtypeStruct((UNITS, 1024), F32),
+            jax.ShapeDtypeStruct((UNITS, 512), F32),
+            jax.ShapeDtypeStruct(bo.shape, F32),
+        ],
         name="finish",
-    )(dealt)
+    )(dealt, bo, brank)
 
 
 def on_device(prior, label_class, labeled, features, tile_cols, tile_weights, halo_owner, halo_local, batch_owner, batch_local, w_in, w_out):
@@ -612,16 +642,8 @@
     arrived = [peer_part(0), peer_part(1)]
     *first, _ = own_part(0, arrived[0])
     *second, errors_out = own_part(1, arrived[1])
-    grad_in, grad_out = summed_over_chips(first, second, halves)
-
-    back_errors = lax.all_to_all(errors_out[:, :BATCH_SLOTS], DEV, 0, 0, tiled=True)
-    row_error = pl.pallas_call(
-        returned_kernel,
-        in_specs=[vmem] * 3,
-        out_shape=jax.ShapeDtypeStruct((batch // LANES, LANES), F32),
-        name="returned",
-    )(back_errors, bo, brank).reshape(batch)
-    return prop, row_error, grad_in, grad_out
+    grad_in, grad_out, row_error = summed_over_chips(first, second, halves, errors_out[:, :BATCH_SLOTS], bo, brank)
+    return prop, row_error.reshape(batch), grad_in, grad_out
 
 
 def solution(mesh):

time: 166 us -> 165 us (level)
  the two profiles are of different devices: /device:TPU:0 before, /device:TPU:12 now
where the time goes in v4:
time: 165 us; the launch traced here: 162 us
  Pallas kernels  71.2 us (43%)
  starting transfers between devices  38.5 us (23%)
  waiting for transfers between devices  19.9 us (12%)
  blocking collectives  15 us (9%)
  other arithmetic  10.2 us (6%)
  local copies, waits for them, and re-layouts  6.39 us (4%)
    pallas_call x1, Pallas kernels, on_device(): pl.pallas_call(first_kernel, grid=(steps,), in_specs=[smem, once((LANES,...  18.1 us
    all_to_all x1, blocking collectives, summed_over_chips(): lax.all_to_all(pieces, DEV, 0, 0, axis_index_groups=corners(), tiled=True)  15 us
    pallas_call x2, Pallas kernels, own_part(): pl.pallas_call(partial(own_kernel, part), grid_spec=pltpu.PrefetchScalarG...  14.3 us
    ppermute x12, starting transfers between devices, exchange(): return lax.ppermute(x, DEV, pairing(level, dims))  12.6 us
    pallas_call x1, Pallas kernels, on_device(): pl.pallas_call(second_kernel, grid=(steps,), in_specs=[smem, vmem, hbm, h...  11.8 us
    pallas_call x1, Pallas kernels, on_device(): pl.pallas_call(spread_kernel, grid=(row_tiles // per,), in_specs=[smem, v...  11.4 us
    pallas_call x2, Pallas kernels, peer_part(): pl.pallas_call(partial(peer_kernel, part), grid_spec=pltpu.PrefetchScalar...  10.8 us
    all_to_all x1, starting transfers between devices, on_device(): lax.all_to_all(table[:, :HALO_SLOTS + BATCH_SLOTS], DEV, 0, 0, tiled=True)  10.4 us
  transfers between devices with their start and end apart: 17, of which 6 were waited for; matrix products, arithmetic and copies ran while one was open for 7% of the time, Pallas kernels for 23%

profile of v4, /device:TPU:12, one launch (start us, length us, event | category | flops | bytes accessed | tf_op | source)
XLA Modules:
  0.0 162.0 jit_solution(9356030257454561013)
XLA Ops:
  0.6 1.9 %request.1 = (s32[128,128]{1,0:T(8,128)}, s32[2,128]{1,0:T(2,128)}, s32[4,128]{1,0:T(4,128)}) custom-call(s32[2,128]{1,0:T(2,128)} %bitcast.49, s32[2,128]{1,0:T(2,128)} %bitcast.50, s32[4,128]{1,0:T(4,128)} %bitcast.46, s32[4,128]{1,0:T(4,128)} %bitcast.48), custom_call_target="tpu_custom_call" | custom-call | tf_op jit(solution)/shard_map/request/pallas_call | solution.py:462
  2.5 10.4 %all-to-all-start = ((s32[128,1,12]{2,1,0:T(1,128)}), s32[128,1,12]{2,1,0:T(1,128)S(1)}, u32[]{:S(2)}, u32[]{:S(2)}) async-start(s32[128,1,12]{2,1,0:T(1,128)} %bitcast.45), calls=%async_computation | async-start | bytes 131072 | tf_op jit(solution)/shard_map/all_to_all | solution.py:477
  13.0 0.7 select_bitcast_fusion.given
  13.7 0.8 copy.19.cols
  14.5 0.1 stack.23.place
  14.6 5.5 %all-to-all-done = s32[128,1,12]{2,1,0:T(1,128)S(1)} async-done(((s32[128,1,12]{2,1,0:T(1,128)}), s32[128,1,12]{2,1,0:T(1,128)S(1)}, u32[]{:S(2)}, u32[]{:S(2)}) %all-to-all-start) | async-done | bytes 6176 | tf_op jit(solution)/shard_map/all_to_all | solution.py:477
  20.1 0.1 reshape.84
  20.2 3.8 %gather_fusion = bf16[512,512]{1,0:T(8,128)(2,1)S(1)} fusion(bf16[2048,512]{1,0:T(8,128)(2,1)} %prior_far.1, s32[1024]{0:T(1024)S(1)} %pad_clamp_fusion), kind=kCustom, calls=%fused_computation | custom fusion | bytes 1050624 | tf_op jit(solution)/shard_map/gather | solution.py:479
  24.1 0.9 reshape.83
  25.0 6.9 %all-to-all-start.1 = ((bf16[128,4,512]{2,1,0:T(4,128)(2,1)}), bf16[128,4,512]{2,1,0:T(4,128)(2,1)S(1)}, u32[]{:S(2)}, u32[]{:S(2)}) async-start(bf16[128,4,512]{2,1,0:T(4,128)(2,1)} %reshape.83), calls=%async_computation.1 | async-start | bytes 1048576 | tf_op jit(solution)/shard_map/all_to_all | solution.py:480
  31.9 18.1 %first.1 = (bf16[1024,1024]{1,0:T(8,128)(2,1)S(1)}, bf16[2048,1024]{1,0:T(8,128)(2,1)}, f32[512,1024]{1,0:T(8,128)}) custom-call(s32[5]{0:T(128)S(1)} %stack.23.place, s32[128,12]{1,0:T(8,128)S(1)} %bitcast.30, bf16[2048,1024]{1,0:T(8,128)(2,1)} %features.1, bf16[128,32,1024]{2,1,0:T(8,128)(2,1)} %bitcast.32, bf16[128,32,512]{2,1,0:T(8,128)(2,1)} %bitcast.34), custom_call_target="tpu_custom_call" | custom-call | flops 10700000256 | bytes 16777216 | tf_op jit(solution)/shard_map/first/pallas_call | solution.py:496
  49.9 0.0 all-to-all-done.1.halo
  49.9 0.0 copy-start
  50.0 11.8 %second.1 = (bf16[4096,1024]{1,0:T(8,128)(2,1)S(1)}, bf16[128,32,512]{2,1,0:T(8,128)(2,1)S(1)}, f32[1024,512]{1,0:T(8,128)S(1)}, bf16[2048,512]{1,0:T(8,128)(2,1)S(1)}, bf16[16,8,128,128]{3,2,1,0:T(8,128)(2,1)S(1)}) custom-call(s32[5]{0:T(128)S(1)} %stack.23.place, bf16[1024,1024]{1,0:T(8,128)(2,1)S(1)} %get-tuple-element.33.x, ...), custom_call_target="tpu_custom_call" | custom-call | flops 6499999744 | bytes 23068672 | tf_op jit(solution)/shard_map/second/pallas_call | solution.py:516
  61.8 11.4 %spread.1 = (bf16[2048,512]{1,0:T(8,128)(2,1)}, bf16[1024,512]{1,0:T(8,128)(2,1)S(1)}, f32[128,128]{1,0:T(8,128)S(1)}) custom-call(s32[16,8]{1,0:T(8,128)S(1)} %copy.19.cols, bf16[16,8,128,128]{3,2,1,0:T(8,128)(2,1)S(1)} %get-tuple-element.36.weights, bf16[2048,512]{1,0:T(8,128)(2,1)S(1)} %get-tuple-element.37.prior, ...), custom_call_target="tpu_custom_call" | custom-call | flops 4300000256 | bytes 12582912 | tf_op jit(solution)/shard_map/spread/pallas_call | solution.py:553
  73.2 5.4 %shard_map.149 = bf16[1024,1536]{1,0:T(8,128)(2,1)S(1)} custom-call(s32[5]{0:T(128)S(1)} %stack.23.place, bf16[128,32,512]{2,1,0:T(8,128)(2,1)S(1)} %get-tuple-element.41.w_out, bf16[4096,1024]{1,0:T(8,128)(2,1)S(1)} %get-tuple-element.42.hidden, bf16[1024,512]{1,0:T(8,128)(2,1)S(1)} %get-tuple-element.43.residue, bf16[1024,1024]{1,0:T(8,128)(2,1)S(1)} %get-tuple-element.33.x), custom_call_target="tpu_custom_call" | custom-call | flops 4300000256 | bytes 9437184 | tf_op jit(solution)/shard_map/pallas_call | solution.py:590
  78.6 0.2 collective-permute-start.1
  78.8 5.4 %shard_map.147 = bf16[1024,1536]{1,0:T(8,128)(2,1)S(1)} custom-call(s32[5]{0:T(128)S(1)} %stack.23.place, bf16[128,32,512]{2,1,0:T(8,128)(2,1)S(1)} %get-tuple-element.41.w_out, bf16[4096,1024]{1,0:T(8,128)(2,1)S(1)} %get-tuple-element.42.hidden, bf16[1024,512]{1,0:T(8,128)(2,1)S(1)} %get-tuple-element.43.residue, bf16[1024,1024]{1,0:T(8,128)(2,1)S(1)} %get-tuple-element.33.x), custom_call_target="tpu_custom_call" | custom-call | flops 4300000256 | bytes 9437184 | tf_op jit(solution)/shard_map/pallas_call | solution.py:590
  84.2 0.5 collective-permute-start
  84.7 0.0 collective-permute-done.1.arrived
  84.7 6.9 %shard_map.150 = (bf16[1024,512]{1,0:T(8,128)(2,1)}, bf16[2,256,512]{2,1,0:T(8,128)(2,1)}, bf16[2,256,512]{2,1,0:T(8,128)(2,1)}, bf16[2,4,64,512]{3,2,1,0:T(8,12...) custom-call(s32[5]{0:T(128)S(1)} %stack.23.place, bf16[128,32,512]{2,1,0:T(8,128)(2,1)S(1)} %get-tuple-element.41.w_out, ...), custom_call_target="tpu_custom_call" | custom-call | flops 4300000256 | bytes 12582912 | tf_op jit(solution)/shard_map/pallas_call | solution.py:615
  91.6 1.8 %collective-permute-start.11 = (bf16[2,4,64,512]{3,2,1,0:T(8,128)(2,1)}, bf16[2,4,64,512]{3,2,1,0:T(8,128)(2,1)}, u32[]{:S(2)}, u32[]{:S(2)}) collective-permute-start(bf16[2,4,64,512]{3,2,1,0:T(8,128)(2,1)} %get-tuple-element.54), channel_id=1, source_target_pairs={{0,2},{1,7},{2,0},{3,5},{4,6},{5,3},{6,4},{7,1},{8,10},{9,15},{10,... | collective-permute-start | bytes 1572872 | tf_op jit(solution)/shard_map/ppermute | solution.py:333
  93.4 0.5 collective-permute-start.2
  93.9 0.0 collective-permute-done.arrived
  93.9 7.4 %shard_map.148 = (bf16[1024,512]{1,0:T(8,128)(2,1)}, bf16[2,256,512]{2,1,0:T(8,128)(2,1)}, bf16[2,256,512]{2,1,0:T(8,128)(2,1)}, bf16[2,4,64,512]{3,2,1,0:T(8,12...) custom-call(s32[5]{0:T(128)S(1)} %stack.23.place, bf16[128,32,512]{2,1,0:T(8,128)(2,1)S(1)} %get-tuple-element.41.w_out, ...), custom_call_target="tpu_custom_call" | custom-call | flops 4300000256 | bytes 12582912 | tf_op jit(solution)/shard_map/pallas_call | solution.py:615
  101.3 0.3 collective-permute-start.9
  101.6 1.2 collective-permute-start.6
  102.7 0.9 collective-permute-start.5
  103.6 0.0 collective-permute-done.11
  103.6 1.2 add_convert_fusion.5
  104.8 1.2 collective-permute-start.12
  106.0 4.6 %collective-permute-done.9 = bf16[2,4,64,512]{3,2,1,0:T(8,128)(2,1)S(1)} collective-permute-done((bf16[2,4,64,512]{3,2,1,0:T(8,128)(2,1)}, bf16[2,4,64,512]{3,2,1,0:T(8,128)(2,1)S(1)}, u32[]{:S(2)}, u32[]{:S(2)}) %collective-permute-start.9) | collective-permute-done | bytes 524320 | tf_op jit(solution)/shard_map/ppermute | solution.py:333
  110.7 1.9 %add_convert_fusion.7 = bf16[2,2,2,32,512]{4,3,2,1,0:T(8,128)(2,1)} fusion(bf16[2,4,2,32,512]{4,3,2,1,0:T(8,128)(2,1)S(1)} %bitcast.41, s32[]{:T(128)S(6)} %select_n.104, bf16[2,4,2,32,512]{4,3,2,1,0:T(8,128)(2,1)} %bitcast.39), kind=kLoop, calls=%fused_computation.9 | loop fusion | flops 524288 | bytes 786436 | tf_op jit(solution)/shard_map/convert_element_type | solution.py:409
  112.6 1.2 collective-permute-start.10
  113.8 0.0 collective-permute-done.6
  113.8 0.1 add_convert_fusion
  113.9 1.6 collective-permute-start.7
  115.5 0.0 collective-permute-done.2
  115.6 1.5 add_convert_fusion.3
  117.1 0.4 collective-permute-start.3
  117.5 0.0 collective-permute-done.5
  117.5 0.0 copy-done.5
  117.5 0.1 add_convert_fusion.1
  117.6 1.8 %collective-permute-done.12 = bf16[2,2,2,32,512]{4,3,2,1,0:T(8,128)(2,1)S(1)} collective-permute-done((bf16[2,2,2,32,512]{4,3,2,1,0:T(8,128)(2,1)S(1)}, bf16[2,2,2,32,512]{4,3,2,1,0:T(8,128)(2,1)S(1)}, u32[]{:S(2)}, u32[]{:S(2)}) %collective-permute-start.12) | collective-permute-done | bytes 262176 | tf_op jit(solution)/shard_map/ppermute | solution.py:333
  119.4 0.0 copy-done.7
  119.4 1.8 %add_convert_fusion.4 = bf16[2,2,2,32,512]{4,3,2,1,0:T(8,128)(2,1)} fusion(bf16[2,2,2,32,512]{4,3,2,1,0:T(8,128)(2,1)S(1)} %collective-permute-done.12, bf16[2,4,2,32,512]{4,3,2,1,0:T(8,128)(2,1)} %bitcast.22, s32[]{:T(128)S(6)} %select_n.102, bf16[2,4,2,32,512]{4,3,2,1,0:T(8,128)(2,1)S(1)} %bitcast.44), kind=kLoop, calls=%fused_computation.5 | loop fusion | flops 1048576 | bytes 1048580 | tf_op jit(solution)/shard_map/convert_element_type | solution.py:399
  121.2 1.5 collective-permute-start.13
  122.7 0.5 collective-permute-done.7
  123.2 0.8 add_convert_fusion.9
  124.0 1.2 collective-permute-start.8
  125.3 1.1 collective-permute-done.3
  126.4 0.9 add_convert_fusion.10
  127.2 0.9 collective-permute-start.4
  128.1 0.6 slice_bitcast_fusion
  128.7 8.0 %all-to-all-start.2 = ((f32[16,8,8]{2,1,0:T(8,128)}), f32[16,8,8]{2,1,0:T(8,128)S(1)}, u32[]{:S(2)}, u32[]{:S(2)}) async-start(f32[16,8,8]{2,1,0:T(8,128)} %slice_bitcast_fusion), calls=%async_computation.2 | async-start | bytes 131072 | tf_op jit(solution)/shard_map/all_to_all | solution.py:402
  136.7 0.0 collective-permute-done.10
  136.7 1.0 convert_add_fusion.k2
  137.8 6.3 %all-to-all-done.2.errors = f32[16,8,8]{2,1,0:T(8,128)S(1)} async-done(((f32[16,8,8]{2,1,0:T(8,128)}), f32[16,8,8]{2,1,0:T(8,128)S(1)}, u32[]{:S(2)}, u32[]{:S(2)}) %all-to-all-start.2) | async-done | bytes 4128 | tf_op jit(solution)/shard_map/all_to_all | solution.py:402
  144.1 0.0 collective-permute-done.13.r2
  144.1 0.0 collective-permute-done.8.r1
  144.1 0.0 collective-permute-done.4.r0
  144.1 0.4 deal.1
  144.5 15.0 %all_to_all.30.dealt = bf16[8,48,1536]{2,1,0:T(8,128)(2,1)} all-to-all(bf16[8,48,1536]{2,1,0:T(8,128)(2,1)S(1)} %deal.1), channel_id=1, replica_groups={{42,44,50,52,74,76,82,84},{46,40,54,48,78,72,86,80},{58,60,34,36,90,92,..., dimensions={0} | all-to-all | bytes 2359296 | tf_op jit(solution)/shard_map/all_to_all | solution.py:429
  159.5 2.5 %finish.1 = (f32[32,1024]{1,0:T(8,128)}, f32[32,512]{1,0:T(8,128)}, f32[4,128]{1,0:T(4,128)}) custom-call(bf16[8,48,1536]{2,1,0:T(8,128)(2,1)} %all_to_all.30.dealt, s32[4,128]{1,0:T(4,128)} %bitcast.47, s32[4,128]{1,0:T(4,128)} %get-tuple-element.56.brank), custom_call_target="tpu_custom_call" | custom-call | tf_op jit(solution)/shard_map/finish/pallas_call | solution.py:430
  (15 shorter events, 0.0 us)
Async XLA Ops:
  2.5 17.6 %all-to-all-start = ((s32[128,1,12]{2,1,0:T(1,128)}), s32[128,1,12]{2,1,0:T(1,128)S(1)}, u32[]{:S(2)}, u32[]{:S(2)}) async-start(s32[128,1,12]{2,1,0:T(1,128)} %bitcast.45), calls=%async_computation | async-start | bytes 131072 | tf_op jit(solution)/shard_map/all_to_all | solution.py:477
  25.0 24.9 %all-to-all-start.1 = ((bf16[128,4,512]{2,1,0:T(4,128)(2,1)}), bf16[128,4,512]{2,1,0:T(4,128)(2,1)S(1)}, u32[]{:S(2)}, u32[]{:S(2)}) async-start(bf16[128,4,512]{2,1,0:T(4,128)(2,1)} %reshape.83), calls=%async_computation.1 | async-start | bytes 1048576 | tf_op jit(solution)/shard_map/all_to_all | solution.py:480
  49.9 11.8 %copy-start = (s32[2,128]{1,0:T(2,128)S(1)}, s32[2,128]{1,0:T(2,128)}, u32[]{:S(2)}) copy-start(s32[2,128]{1,0:T(2,128)} %get-tuple-element.38.hslot) | copy-start | bytes 3076
  78.6 6.1 %collective-permute-start.1 = (bf16[1024,1536]{1,0:T(8,128)(2,1)S(1)}, bf16[1024,1536]{1,0:T(8,128)(2,1)S(1)}, u32[]{:S(2)}, u32[]{:S(2)}) collective-permute-start(bf16[1024,1536]{1,0:T(8,128)(2,1)S(1)} %shard_map.149), channel_id=1, source_target_pairs={{0,1},{1,0},{2,3},{3,2},{4,5},{5,4},{6,7},{7,6},{8,9},{9,8},{10,11... | collective-permute-start | bytes 9437192 | tf_op jit(solution)/shard_map/ppermute | solution.py:607
  84.2 9.7 %collective-permute-start = (bf16[1024,1536]{1,0:T(8,128)(2,1)S(1)}, bf16[1024,1536]{1,0:T(8,128)(2,1)S(1)}, u32[]{:S(2)}, u32[]{:S(2)}) collective-permute-start(bf16[1024,1536]{1,0:T(8,128)(2,1)S(1)} %shard_map.147), channel_id=1, source_target_pairs={{0,1},{1,0},{2,3},{3,2},{4,5},{5,4},{6,7},{7,6},{8,9},{9,8},{10,11... | collective-permute-start | bytes 9437192 | tf_op jit(solution)/shard_map/ppermute | solution.py:607
  91.6 12.0 %collective-permute-start.11 = (bf16[2,4,64,512]{3,2,1,0:T(8,128)(2,1)}, bf16[2,4,64,512]{3,2,1,0:T(8,128)(2,1)}, u32[]{:S(2)}, u32[]{:S(2)}) collective-permute-start(bf16[2,4,64,512]{3,2,1,0:T(8,128)(2,1)} %get-tuple-element.54), channel_id=1, source_target_pairs={{0,2},{1,7},{2,0},{3,5},{4,6},{5,3},{6,4},{7,1},{8,10},{9,15},{10,... | collective-permute-start | bytes 1572872 | tf_op jit(solution)/shard_map/ppermute | solution.py:333
  93.4 20.4 %copy-start.3 = (bf16[2,256,512]{2,1,0:T(8,128)(2,1)S(1)}, bf16[2,256,512]{2,1,0:T(8,128)(2,1)}, u32[]{:S(2)}) copy-start(bf16[2,256,512]{2,1,0:T(8,128)(2,1)} %get-tuple-element.49) | copy-start | bytes 1572868
  93.4 22.2 %collective-permute-start.2 = (bf16[1024,512]{1,0:T(8,128)(2,1)}, bf16[1024,512]{1,0:T(8,128)(2,1)}, u32[]{:S(2)}, u32[]{:S(2)}) collective-permute-start(bf16[1024,512]{1,0:T(8,128)(2,1)} %get-tuple-element.46), channel_id=1, source_target_pairs={{0,32},{1,97},{2,34},{3,99},{4,36},{5,101},{6,38},{7,103},{8,40},{... | collective-permute-start | bytes 3145736 | tf_op jit(solution)/shard_map/ppermute | solution.py:333
  101.3 14.3 %copy-start.1 = (bf16[1024,512]{1,0:T(8,128)(2,1)S(1)}, bf16[1024,512]{1,0:T(8,128)(2,1)}, u32[]{:S(2)}) copy-start(bf16[1024,512]{1,0:T(8,128)(2,1)} %get-tuple-element.45) | copy-start | bytes 3145732
  101.3 9.4 %collective-permute-start.9 = (bf16[2,4,64,512]{3,2,1,0:T(8,128)(2,1)}, bf16[2,4,64,512]{3,2,1,0:T(8,128)(2,1)S(1)}, u32[]{:S(2)}, u32[]{:S(2)}) collective-permute-start(bf16[2,4,64,512]{3,2,1,0:T(8,128)(2,1)} %get-tuple-element.52), channel_id=1, source_target_pairs={{0,2},{1,7},{2,0},{3,5},{4,6},{5,3},{6,4},{7,1},{8,10},{9,15},{10,... | collective-permute-start | bytes 1572872 | tf_op jit(solution)/shard_map/ppermute | solution.py:333
  101.6 12.2 %collective-permute-start.6 = (bf16[2,256,512]{2,1,0:T(8,128)(2,1)}, bf16[2,256,512]{2,1,0:T(8,128)(2,1)S(1)}, u32[]{:S(2)}, u32[]{:S(2)}) collective-permute-start(bf16[2,256,512]{2,1,0:T(8,128)(2,1)} %get-tuple-element.50), channel_id=1, source_target_pairs={{0,8},{1,25},{2,10},{3,27},{4,12},{5,29},{6,14},{7,31},{8,0},{9,17... | collective-permute-start | bytes 1572872 | tf_op jit(solution)/shard_map/ppermute | solution.py:333
  102.7 14.7 %collective-permute-start.5 = (bf16[2,256,512]{2,1,0:T(8,128)(2,1)}, bf16[2,256,512]{2,1,0:T(8,128)(2,1)S(1)}, u32[]{:S(2)}, u32[]{:S(2)}) collective-permute-start(bf16[2,256,512]{2,1,0:T(8,128)(2,1)} %get-tuple-element.48), channel_id=1, source_target_pairs={{0,8},{1,25},{2,10},{3,27},{4,12},{5,29},{6,14},{7,31},{8,0},{9,17... | collective-permute-start | bytes 1572872 | tf_op jit(solution)/shard_map/ppermute | solution.py:333
  103.6 13.9 %copy-start.2 = (bf16[2,256,512]{2,1,0:T(8,128)(2,1)S(1)}, bf16[2,256,512]{2,1,0:T(8,128)(2,1)}, u32[]{:S(2)}) copy-start(bf16[2,256,512]{2,1,0:T(8,128)(2,1)} %get-tuple-element.47) | copy-start | bytes 1572868
  104.8 14.6 %collective-permute-start.12 = (bf16[2,2,2,32,512]{4,3,2,1,0:T(8,128)(2,1)S(1)}, bf16[2,2,2,32,512]{4,3,2,1,0:T(8,128)(2,1)S(1)}, u32[]{:S(2)}, u32[]{:S(2)}) collective-permute-start(bf16[2,2,2,32,512]{4,3,2,1,0:T(8,128)(2,1)S(1)} %add_convert_fusion.5), channel_id=1, source_target_pairs={{0,8},{1,25},{2,10},{3,27},{4,12},{5,29},{6,14},{7,31},{8,0},{9,17... | collective-permute-start | bytes 786440 | tf_op jit(solution)/shard_map/ppermute | solution.py:333
  110.7 6.8 %copy-start.5 = (bf16[2,4,64,512]{3,2,1,0:T(8,128)(2,1)}, bf16[2,4,64,512]{3,2,1,0:T(8,128)(2,1)S(1)}, u32[]{:S(2)}) copy-start(bf16[2,4,64,512]{3,2,1,0:T(8,128)(2,1)S(1)} %collective-permute-done.9) | copy-start | bytes 1572868
  112.6 24.1 %collective-permute-start.10 = (bf16[2,2,2,32,512]{4,3,2,1,0:T(8,128)(2,1)}, bf16[2,2,2,32,512]{4,3,2,1,0:T(8,128)(2,1)}, u32[]{:S(2)}, u32[]{:S(2)}) collective-permute-start(bf16[2,2,2,32,512]{4,3,2,1,0:T(8,128)(2,1)} %add_convert_fusion.7), channel_id=1, source_target_pairs={{0,8},{1,25},{2,10},{3,27},{4,12},{5,29},{6,14},{7,31},{8,0},{9,17... | collective-permute-start | bytes 786440 | tf_op jit(solution)/shard_map/ppermute | solution.py:333
  113.8 5.6 %copy-start.7 = (bf16[2,4,64,512]{3,2,1,0:T(8,128)(2,1)S(1)}, bf16[2,4,64,512]{3,2,1,0:T(8,128)(2,1)}, u32[]{:S(2)}) copy-start(bf16[2,4,64,512]{3,2,1,0:T(8,128)(2,1)} %get-tuple-element.53) | copy-start | bytes 1572868
  113.9 9.3 %collective-permute-start.7 = (bf16[2,2,4,32,512]{4,3,2,1,0:T(8,128)(2,1)S(1)}, bf16[2,2,4,32,512]{4,3,2,1,0:T(8,128)(2,1)S(1)}, u32[]{:S(2)}, u32[]{:S(2)}) collective-permute-start(bf16[2,2,4,32,512]{4,3,2,1,0:T(8,128)(2,1)S(1)} %bitcast.38), channel_id=1, source_target_pairs={{0,32},{1,97},{2,34},{3,99},{4,36},{5,101},{6,38},{7,103},{8,40},{... | collective-permute-start | bytes 1572872 | tf_op jit(solution)/shard_map/ppermute | solution.py:333
  117.1 9.3 %collective-permute-start.3 = (bf16[2,4,2,32,512]{4,3,2,1,0:T(8,128)(2,1)S(1)}, bf16[2,4,2,32,512]{4,3,2,1,0:T(8,128)(2,1)S(1)}, u32[]{:S(2)}, u32[]{:S(2)}) collective-permute-start(bf16[2,4,2,32,512]{4,3,2,1,0:T(8,128)(2,1)S(1)} %get-tuple-element.61), channel_id=1, source_target_pairs={{0,2},{1,7},{2,0},{3,5},{4,6},{5,3},{6,4},{7,1},{8,10},{9,15},{10,... | collective-permute-start | bytes 1572872 | tf_op jit(solution)/shard_map/ppermute | solution.py:333
  117.5 19.2 %copy-start.4 = (bf16[2,4,64,512]{3,2,1,0:T(8,128)(2,1)S(1)}, bf16[2,4,64,512]{3,2,1,0:T(8,128)(2,1)}, u32[]{:S(2)}) copy-start(bf16[2,4,64,512]{3,2,1,0:T(8,128)(2,1)} %get-tuple-element.51) | copy-start | bytes 1572868
  117.5 19.2 %copy-start.6 = (bf16[2,4,64,512]{3,2,1,0:T(8,128)(2,1)S(1)}, bf16[2,4,64,512]{3,2,1,0:T(8,128)(2,1)}, u32[]{:S(2)}) copy-start(bf16[2,4,64,512]{3,2,1,0:T(8,128)(2,1)} %copy-done.5) | copy-start | bytes 1572868
  121.2 22.9 %collective-permute-start.13 = (bf16[2,2,2,32,512]{4,3,2,1,0:T(8,128)(2,1)}, bf16[2,2,2,32,512]{4,3,2,1,0:T(8,128)(2,1)S(1)}, u32[]{:S(2)}, u32[]{:S(2)}) collective-permute-start(bf16[2,2,2,32,512]{4,3,2,1,0:T(8,128)(2,1)} %add_convert_fusion.4), channel_id=1, source_target_pairs={{0,32},{1,97},{2,34},{3,99},{4,36},{5,101},{6,38},{7,103},{8,40},{... | collective-permute-start | bytes 786440 | tf_op jit(solution)/shard_map/ppermute | solution.py:333
  124.0 20.1 %collective-permute-start.8 = (bf16[2,2,2,32,512]{4,3,2,1,0:T(8,128)(2,1)}, bf16[2,2,2,32,512]{4,3,2,1,0:T(8,128)(2,1)S(1)}, u32[]{:S(2)}, u32[]{:S(2)}) collective-permute-start(bf16[2,2,2,32,512]{4,3,2,1,0:T(8,128)(2,1)} %get-tuple-element.62), channel_id=1, source_target_pairs={{0,2},{1,7},{2,0},{3,5},{4,6},{5,3},{6,4},{7,1},{8,10},{9,15},{10,... | collective-permute-start | bytes 786440 | tf_op jit(solution)/shard_map/ppermute | solution.py:333
  127.2 16.9 %collective-permute-start.4 = (bf16[2,2,2,32,512]{4,3,2,1,0:T(8,128)(2,1)}, bf16[2,2,2,32,512]{4,3,2,1,0:T(8,128)(2,1)S(1)}, u32[]{:S(2)}, u32[]{:S(2)}) collective-permute-start(bf16[2,2,2,32,512]{4,3,2,1,0:T(8,128)(2,1)} %get-tuple-element.64), channel_id=1, source_target_pairs={{0,8},{1,25},{2,10},{3,27},{4,12},{5,29},{6,14},{7,31},{8,0},{9,17... | collective-permute-start | bytes 786440 | tf_op jit(solution)/shard_map/ppermute | solution.py:333
  128.7 15.4 %all-to-all-start.2 = ((f32[16,8,8]{2,1,0:T(8,128)}), f32[16,8,8]{2,1,0:T(8,128)S(1)}, u32[]{:S(2)}, u32[]{:S(2)}) async-start(f32[16,8,8]{2,1,0:T(8,128)} %slice_bitcast_fusion), calls=%async_computation.2 | async-start | bytes 131072 | tf_op jit(solution)/shard_map/all_to_all | solution.py:402

commit v5 on v3

--- a/solution.py
+++ b/solution.py
@@ -111,7 +111,7 @@
         pltpu.make_async_copy(far.at[source], near.at[n], sem).start()
 
 
-def first_kernel(place, table, features, w_in, w_out, x, hidden, part, onehot, acc, nodes_x, in_buf, out_buf, nodes_sem, in_sem, out_sem):
+def first_kernel(place, table, features, w_in, x, hidden, onehot, nodes_x, in_buf, nodes_sem, in_sem):
     step = pl.program_id(0)
     steps = pl.num_programs(0)
     chunks = HBLK // UNITS
@@ -119,7 +119,6 @@
 
     def fetch(block, slot):
         fetch_chunks(core, block, w_in, in_buf.at[slot], in_sem.at[slot])
-        fetch_chunks(core, block, w_out, out_buf.at[slot], out_sem.at[slot])
 
     @pl.when(step == 0)
     def _():
@@ -129,7 +128,6 @@
         pick_rows(table, HALO_SLOTS, BATCH_SLOTS, features.shape[0], onehot)
         whole.wait()
         x[...] = dot(onehot[...], nodes_x[...], (1, 0)).astype(BF)
-        acc[...] = jnp.zeros(acc.shape, F32)
 
     slot = step % 2
 
@@ -138,18 +136,12 @@
         fetch(step + 1, 1 - slot)
 
     pltpu.make_async_copy(w_in.at[pl.ds(0, chunks)], in_buf.at[slot], in_sem.at[slot]).wait()
-    pltpu.make_async_copy(w_out.at[pl.ds(0, chunks)], out_buf.at[slot], out_sem.at[slot]).wait()
     h = jnp.tanh(dot(in_buf[slot].reshape(HBLK, in_buf.shape[3]), x[...], (1, 1))).astype(BF)
     hidden[...] = h
-    acc[...] += dot(out_buf[slot].reshape(HBLK, out_buf.shape[3]), h, (0, 0))
-
-    @pl.when(step == steps - 1)
-    def _():
-        part[...] = acc[...]
 
 
 def second_kernel(
-    place, x, w_in, w_out, hidden_far, part_far, prior_far, tiles_far, halo,
+    place, x, w_in, w_out, hidden_far, prior_far, tiles_far, halo,
     hidden, w_out_near, logits, prior, tiles,
     acc, in_buf, in_sem, out_sem, sems,
 ):
@@ -158,7 +150,7 @@
     chunks = HBLK // UNITS
     core = place[3]
     done = hidden_far.shape[0]
-    pairs = ((part_far, acc), (prior_far, prior), (tiles_far, tiles), (hidden_far, hidden.at[pl.ds(0, done)]))
+    pairs = ((hidden_far, hidden.at[pl.ds(0, done)]), (prior_far, prior), (tiles_far, tiles))
     copies = [pltpu.make_async_copy(far, near, sems.at[n]) for n, (far, near) in enumerate(pairs)]
 
     def fetch(block, slot):
@@ -172,7 +164,7 @@
     def _():
         fetch(steps, 0)
         fetch_out(steps)
-        copies[0].start()
+        acc[...] = jnp.zeros(acc.shape, F32)
 
     slot = step % 2
 
@@ -183,11 +175,10 @@
 
     @pl.when(step == 0)
     def _():
-        for copy in copies[1:]:
+        for copy in copies:
             copy.start()
         for block in range(4):
             fetch_out(block)
-        copies[0].wait()
 
     def out_wait(block):
         here = w_out_near.at[pl.ds(block * chunks, chunks)]
@@ -200,13 +191,23 @@
     w_out_here = w_out_near[pl.ds((steps + step) * chunks, chunks)].reshape(HBLK, w_out_near.shape[2])
     acc[...] += dot(w_out_here, h, (0, 0))
 
+    @pl.when(step == steps - 2)
+    def _():
+        copies[0].wait()
+
+    @pl.when(step >= steps - 2)
+    def _():
+        pair = 2 * (step - (steps - 2))
+        out_wait(pair)
+        out_wait(pair + 1)
+        early = w_out_near[pl.ds(pair * chunks, 2 * chunks)].reshape(2 * HBLK, w_out_near.shape[2])
+        acc[...] += dot(early, hidden[pl.ds(pl.multiple_of(pair * HBLK, HBLK), 2 * HBLK), :], (0, 0))
+
     @pl.when(step == steps - 1)
     def _():
         logits[...] = acc[...].T
         for copy in copies[1:]:
             copy.wait()
-        for block in range(4):
-            out_wait(block)
 
 
 def spread_kernel(
@@ -388,7 +389,8 @@
     c2 = added(keep_c2, got_c2, 1, hb).astype(BF)
     b_last = sent(added(b, b_got, 2, 1 - hc), 2)
     a_last = sent(added(a, a_got, 1, 1 - hb), 1)
-    c_last = sent(added(c1, c1_got), 0)
+    c_send = added(c1, c1_got).astype(BF)
+    c_last = sent(c_send, 0)
     b = added(b, b_got, 2, hc)
     a = added(a, a_got, 1, hb)
     c = added(c2, c2_got)
@@ -406,7 +408,7 @@
         in_specs=[pl.BlockSpec(memory_space=pltpu.VMEM)],
         out_shape=[jax.ShapeDtypeStruct((UNITS, 1024), F32), jax.ShapeDtypeStruct((UNITS, 512), F32)],
         name="finish",
-    )(dealt)
+    )(pltpu.with_memory_space_constraint(dealt, pltpu.VMEM))
 
 
 def on_device(prior, label_class, labeled, features, tile_cols, tile_weights, halo_owner, halo_local, batch_owner, batch_local, w_in, w_out):
@@ -463,30 +465,27 @@
     steps = hid // HBLK // 2
     w_in = w_in.reshape(128, UNITS, feat)
     w_out = w_out.reshape(128, UNITS, classes)
-    x, hidden_first, part = pl.pallas_call(
+    x, hidden_first = pl.pallas_call(
         first_kernel,
         grid=(steps,),
-        in_specs=[smem, once((LANES, slots)), hbm, hbm, hbm],
-        out_specs=[vmem, rows_at(0, rows), whole((classes, rows))],
-        out_shape=[pltpu.VMEM((rows, feat), BF), pltpu.HBM((hid // 2, rows), BF), pltpu.HBM((classes, rows), F32)],
+        in_specs=[smem, once((LANES, slots)), hbm, hbm],
+        out_specs=[vmem, rows_at(0, rows)],
+        out_shape=[pltpu.VMEM((rows, feat), BF), pltpu.HBM((hid // 2, rows), BF)],
         scratch_shapes=[
             pltpu.VMEM((rows, nodes), BF),
-            pltpu.VMEM((classes, rows), F32),
             pltpu.VMEM((nodes, feat), BF),
             pltpu.VMEM((2, chunks, UNITS, feat), BF),
-            pltpu.VMEM((2, chunks, UNITS, classes), BF),
             pltpu.SemaphoreType.DMA,
             pltpu.SemaphoreType.DMA((2,)),
-            pltpu.SemaphoreType.DMA((2,)),
-        ],
-        compiler_params=params(32),
-        cost_estimate=cost(10.7, 16, 0.0021),
+        ],
+        compiler_params=params(28),
+        cost_estimate=cost(8.6, 14, 0.0021),
         name="first",
-    )(place, asked, in_hbm(features), in_hbm(w_in), in_hbm(w_out))
+    )(place, asked, in_hbm(features), in_hbm(w_in))
     hidden, w_out_o, logits, prior_near, tiles_near = pl.pallas_call(
         second_kernel,
         grid=(steps,),
-        in_specs=[smem, vmem, hbm, hbm, hbm, hbm, hbm, hbm, hbm],
+        in_specs=[smem, vmem, hbm, hbm, hbm, hbm, hbm, hbm],
         out_specs=[vmem] * 5,
         out_shape=[
             pltpu.VMEM((hid, rows), BF),
@@ -500,10 +499,10 @@
             pltpu.VMEM((2, chunks, UNITS, feat), BF),
             pltpu.SemaphoreType.DMA((2,)),
             pltpu.SemaphoreType.DMA((8,)),
-            pltpu.SemaphoreType.DMA((4,)),
+            pltpu.SemaphoreType.DMA((3,)),
         ],
         compiler_params=params(16),
-        cost_estimate=cost(6.5, 22, 0.0021),
+        cost_estimate=cost(8.6, 18, 0.0021),
         name="second",
     )(
         place,
@@ -511,7 +510,6 @@
         in_hbm(w_in),
         in_hbm(w_out),
         in_hbm(hidden_first),
-        in_hbm(part),
         in_hbm(prior),
         in_hbm(tile_weights),
         halo,

time: 166 us -> 163 us (0.982)
  Pallas kernels: 73 us -> 70.6 us
    pallas_call x1, Pallas kernels: 18.1 us -> 14.7 us  [on_device(): pl.pallas_call(first_kernel, grid=(steps,), in_specs=[smem, once((LANES,...]
    pallas_call x1, Pallas kernels: 11.8 us -> 13.7 us  [on_device(): pl.pallas_call(second_kernel, grid=(steps,), in_specs=[smem, vmem, hbm, h...]
    convert_element_type x0 -> x1, other arithmetic: none -> 1.76 us  [summed_over_chips(): c_send = added(c1, c1_got).astype(BF)]
    convert_element_type x5 -> x4, other arithmetic: 4.03 us -> 2.28 us  [sent(): return exchange(value.astype(BF), 1, (dim,))]
  transfers between devices with their start and end apart: 18 -> 18, of which waited for: 7 -> 7; matrix products, arithmetic and copies ran while one was open for 6% -> 6% of each run, Pallas kernels for 25% -> 23%
where the time goes in v5:
time: 163 us; the launch traced here: 162 us
  Pallas kernels  70.6 us (43%)
  starting transfers between devices  46.6 us (29%)
  waiting for transfers between devices  30 us (18%)
  other arithmetic  8.3 us (5%)
  local copies, waits for them, and re-layouts  5.74 us (4%)
    pallas_call x1, Pallas kernels, on_device(): pl.pallas_call(first_kernel, grid=(steps,), in_specs=[smem, once((LANES,...  14.7 us
    pallas_call x2, Pallas kernels, own_part(): pl.pallas_call(partial(own_kernel, part), grid_spec=pltpu.PrefetchScalarG...  14 us
    pallas_call x1, Pallas kernels, on_device(): pl.pallas_call(second_kernel, grid=(steps,), in_specs=[smem, vmem, hbm, h...  13.7 us
    pallas_call x1, Pallas kernels, on_device(): pl.pallas_call(spread_kernel, grid=(row_tiles // per,), in_specs=[smem, v...  11.4 us
    all_to_all x1, starting transfers between devices, on_device(): lax.all_to_all(table[:, :HALO_SLOTS + BATCH_SLOTS], DEV, 0, 0, tiled=True)  11.2 us
    ppermute x12, starting transfers between devices, exchange(): return lax.ppermute(x, DEV, pairing(level, dims))  11.2 us
    pallas_call x2, Pallas kernels, peer_part(): pl.pallas_call(partial(peer_kernel, part), grid_spec=pltpu.PrefetchScalar...  10.8 us
    all_to_all x1, starting transfers between devices, on_device(): lax.all_to_all(errors_out[:, :BATCH_SLOTS], DEV, 0, 0, tiled=True)  10.1 us
  transfers between devices with their start and end apart: 18, of which 7 were waited for; matrix products, arithmetic and copies ran while one was open for 6% of the time, Pallas kernels for 23%

profile of v5, /device:TPU:0, one launch (start us, length us, event | category | flops | bytes accessed | tf_op | source)
XLA Modules:
  0.0 162.2 jit_solution(15867259561495922556)
XLA Ops:
  0.6 1.9 %request.1 = (s32[128,128]{1,0:T(8,128)}, s32[2,128]{1,0:T(2,128)}, s32[4,128]{1,0:T(4,128)}) custom-call(s32[2,128]{1,0:T(2,128)} %bitcast.50, s32[2,128]{1,0:T(2,128)} %bitcast.51, s32[4,128]{1,0:T(4,128)} %bitcast.46, s32[4,128]{1,0:T(4,128)} %bitcast.48), custom_call_target="tpu_custom_call" | custom-call | tf_op jit(solution)/shard_map/request/pallas_call | solution.py:434
  2.5 11.2 %all-to-all-start = ((s32[128,1,12]{2,1,0:T(1,128)}), s32[128,1,12]{2,1,0:T(1,128)S(1)}, u32[]{:S(2)}, u32[]{:S(2)}) async-start(s32[128,1,12]{2,1,0:T(1,128)} %bitcast.45), calls=%async_computation | async-start | bytes 131072 | tf_op jit(solution)/shard_map/all_to_all | solution.py:449
  13.8 0.7 select_bitcast_fusion.given
  14.5 0.8 copy.19.cols
  15.3 0.1 stack.23.place
  15.3 7.8 %all-to-all-done = s32[128,1,12]{2,1,0:T(1,128)S(1)} async-done(((s32[128,1,12]{2,1,0:T(1,128)}), s32[128,1,12]{2,1,0:T(1,128)S(1)}, u32[]{:S(2)}, u32[]{:S(2)}) %all-to-all-start) | async-done | bytes 6176 | tf_op jit(solution)/shard_map/all_to_all | solution.py:449
  23.2 0.1 reshape.82
  23.3 3.8 %gather_fusion = bf16[512,512]{1,0:T(8,128)(2,1)S(1)} fusion(bf16[2048,512]{1,0:T(8,128)(2,1)} %prior_far.1, s32[1024]{0:T(1024)S(1)} %pad_clamp_fusion), kind=kCustom, calls=%fused_computation | custom fusion | bytes 1050624 | tf_op jit(solution)/shard_map/gather | solution.py:451
  27.2 0.9 reshape.81
  28.1 4.8 %all-to-all-start.1 = ((bf16[128,4,512]{2,1,0:T(4,128)(2,1)}), bf16[128,4,512]{2,1,0:T(4,128)(2,1)S(1)}, u32[]{:S(2)}, u32[]{:S(2)}) async-start(bf16[128,4,512]{2,1,0:T(4,128)(2,1)} %reshape.81), calls=%async_computation.1 | async-start | bytes 1048576 | tf_op jit(solution)/shard_map/all_to_all | solution.py:452
  32.9 14.7 %first.1 = (bf16[1024,1024]{1,0:T(8,128)(2,1)S(1)}, bf16[2048,1024]{1,0:T(8,128)(2,1)}) custom-call(s32[5]{0:T(128)S(1)} %stack.23.place, s32[128,12]{1,0:T(8,128)S(1)} %bitcast.33, bf16[2048,1024]{1,0:T(8,128)(2,1)} %features.1, bf16[128,32,1024]{2,1,0:T(8,128)(2,1)} %bitcast.52), custom_call_target="tpu_custom_call" | custom-call | flops 8600000512 | bytes 14680064 | tf_op jit(solution)/shard_map/first/pallas_call | solution.py:468
  47.6 0.0 all-to-all-done.1.halo
  47.6 0.0 copy-start
  47.6 13.7 %second.1 = (bf16[4096,1024]{1,0:T(8,128)(2,1)S(1)}, bf16[128,32,512]{2,1,0:T(8,128)(2,1)S(1)}, f32[1024,512]{1,0:T(8,128)S(1)}, bf16[2048,512]{1,0:T(8,128)(2,1)S(1)}, bf16[16,8,128,128]{3,2,1,0:T(8,128)(2,1)S(1)}) custom-call(s32[5]{0:T(128)S(1)} %stack.23.place, bf16[1024,1024]{1,0:T(8,128)(2,1)S(1)} %get-tuple-element.31.x, ...), custom_call_target="tpu_custom_call" | custom-call | flops 8600000512 | bytes 18874368 | tf_op jit(solution)/shard_map/second/pallas_call | solution.py:485
  61.4 0.0 copy-done
  61.4 11.4 %spread.1 = (bf16[2048,512]{1,0:T(8,128)(2,1)}, bf16[1024,512]{1,0:T(8,128)(2,1)S(1)}, f32[128,128]{1,0:T(8,128)S(1)}) custom-call(s32[16,8]{1,0:T(8,128)S(1)} %copy.19.cols, bf16[16,8,128,128]{3,2,1,0:T(8,128)(2,1)S(1)} %get-tuple-element.33.weights, bf16[2048,512]{1,0:T(8,128)(2,1)S(1)} %get-tuple-element.34.prior, ...), custom_call_target="tpu_custom_call" | custom-call | flops 4300000256 | bytes 12582912 | tf_op jit(solution)/shard_map/spread/pallas_call | solution.py:521
  72.8 5.4 %shard_map.149 = bf16[1024,1536]{1,0:T(8,128)(2,1)S(1)} custom-call(s32[5]{0:T(128)S(1)} %stack.23.place, bf16[128,32,512]{2,1,0:T(8,128)(2,1)S(1)} %get-tuple-element.38.w_out, bf16[4096,1024]{1,0:T(8,128)(2,1)S(1)} %get-tuple-element.39.hidden, bf16[1024,512]{1,0:T(8,128)(2,1)S(1)} %get-tuple-element.40.residue, bf16[1024,1024]{1,0:T(8,128)(2,1)S(1)} %get-tuple-element.31.x), custom_call_target="tpu_custom_call" | custom-call | flops 4300000256 | bytes 9437184 | tf_op jit(solution)/shard_map/pallas_call | solution.py:558
  78.3 0.1 collective-permute-start.1
  78.4 5.4 %shard_map.147 = bf16[1024,1536]{1,0:T(8,128)(2,1)S(1)} custom-call(s32[5]{0:T(128)S(1)} %stack.23.place, bf16[128,32,512]{2,1,0:T(8,128)(2,1)S(1)} %get-tuple-element.38.w_out, bf16[4096,1024]{1,0:T(8,128)(2,1)S(1)} %get-tuple-element.39.hidden, bf16[1024,512]{1,0:T(8,128)(2,1)S(1)} %get-tuple-element.40.residue, bf16[1024,1024]{1,0:T(8,128)(2,1)S(1)} %get-tuple-element.31.x), custom_call_target="tpu_custom_call" | custom-call | flops 4300000256 | bytes 9437184 | tf_op jit(solution)/shard_map/pallas_call | solution.py:558
  83.8 0.6 collective-permute-start
  84.3 0.0 collective-permute-done.1.arrived
  84.4 6.9 %shard_map.150 = (bf16[1024,512]{1,0:T(8,128)(2,1)}, bf16[2,256,512]{2,1,0:T(8,128)(2,1)}, bf16[2,256,512]{2,1,0:T(8,128)(2,1)}, bf16[2,4,64,512]{3,2,1,0:T(8,12...) custom-call(s32[5]{0:T(128)S(1)} %stack.23.place, bf16[128,32,512]{2,1,0:T(8,128)(2,1)S(1)} %get-tuple-element.38.w_out, ...), custom_call_target="tpu_custom_call" | custom-call | flops 4300000256 | bytes 12582912 | tf_op jit(solution)/shard_map/pallas_call | solution.py:583
  91.2 1.0 collective-permute-start.11
  92.2 1.5 collective-permute-start.2
  93.8 0.0 collective-permute-done.arrived
  93.8 7.1 %shard_map.148 = (bf16[1024,512]{1,0:T(8,128)(2,1)}, bf16[2,256,512]{2,1,0:T(8,128)(2,1)}, bf16[2,256,512]{2,1,0:T(8,128)(2,1)}, bf16[2,4,64,512]{3,2,1,0:T(8,12...) custom-call(s32[5]{0:T(128)S(1)} %stack.23.place, bf16[128,32,512]{2,1,0:T(8,128)(2,1)S(1)} %get-tuple-element.38.w_out, ...), custom_call_target="tpu_custom_call" | custom-call | flops 4300000256 | bytes 12582912 | tf_op jit(solution)/shard_map/pallas_call | solution.py:583
  100.9 0.4 collective-permute-start.9
  101.3 1.5 collective-permute-start.6
  102.8 0.5 collective-permute-start.5
  103.3 0.0 collective-permute-done.11
  103.3 1.2 add_convert_fusion.5
  104.5 1.6 collective-permute-start.12
  106.1 4.3 %collective-permute-done.9 = bf16[2,4,64,512]{3,2,1,0:T(8,128)(2,1)S(1)} collective-permute-done((bf16[2,4,64,512]{3,2,1,0:T(8,128)(2,1)}, bf16[2,4,64,512]{3,2,1,0:T(8,128)(2,1)S(1)}, u32[]{:S(2)}, u32[]{:S(2)}) %collective-permute-start.9) | collective-permute-done | bytes 524320 | tf_op jit(solution)/shard_map/ppermute | solution.py:326
  110.4 1.7 %add_convert_fusion.7 = bf16[2,2,2,32,512]{4,3,2,1,0:T(8,128)(2,1)} fusion(bf16[2,4,2,32,512]{4,3,2,1,0:T(8,128)(2,1)S(1)} %bitcast.40, s32[]{:T(128)S(6)} %select_n.104, bf16[2,4,2,32,512]{4,3,2,1,0:T(8,128)(2,1)} %bitcast.38), kind=kLoop, calls=%fused_computation.9 | loop fusion | flops 524288 | bytes 786436 | tf_op jit(solution)/shard_map/convert_element_type | solution.py:384
  112.1 1.5 collective-permute-start.10
  113.6 0.0 collective-permute-done.6
  113.6 0.1 add_convert_fusion
  113.7 0.6 collective-permute-start.7
  114.3 0.0 collective-permute-done.2
  114.3 1.6 add_convert_fusion.3
  115.9 0.4 collective-permute-start.3
  116.3 0.0 collective-permute-done.5
  116.3 0.1 add_convert_fusion.1
  116.4 2.7 %collective-permute-done.12 = bf16[2,2,2,32,512]{4,3,2,1,0:T(8,128)(2,1)S(1)} collective-permute-done((bf16[2,2,2,32,512]{4,3,2,1,0:T(8,128)(2,1)S(1)}, bf16[2,2,2,32,512]{4,3,2,1,0:T(8,128)(2,1)S(1)}, u32[]{:S(2)}, u32[]{:S(2)}) %collective-permute-start.12) | collective-permute-done | bytes 262176 | tf_op jit(solution)/shard_map/ppermute | solution.py:326
  119.1 1.8 %add_convert_fusion.4 = bf16[2,2,2,32,512]{4,3,2,1,0:T(8,128)(2,1)} fusion(bf16[2,2,2,32,512]{4,3,2,1,0:T(8,128)(2,1)S(1)} %collective-permute-done.12, bf16[2,4,2,32,512]{4,3,2,1,0:T(8,128)(2,1)} %bitcast.26, s32[]{:T(128)S(6)} %select_n.102, bf16[2,4,2,32,512]{4,3,2,1,0:T(8,128)(2,1)S(1)} %bitcast.43), kind=kLoop, calls=%fused_computation.5 | loop fusion | flops 1048576 | bytes 1048580 | tf_op jit(solution)/shard_map/convert_element_type | solution.py:392
  120.9 1.3 collective-permute-start.13
  122.2 0.8 collective-permute-done.7
  123.0 0.1 add_convert_fusion.9
  123.1 0.4 collective-permute-start.8
  123.5 1.6 %collective-permute-done.3 = bf16[2,4,2,32,512]{4,3,2,1,0:T(8,128)(2,1)S(1)} collective-permute-done((bf16[2,4,2,32,512]{4,3,2,1,0:T(8,128)(2,1)S(1)}, bf16[2,4,2,32,512]{4,3,2,1,0:T(8,128)(2,1)S(1)}, u32[]{:S(2)}, u32[]{:S(2)}) %collective-permute-start.3) | collective-permute-done | bytes 524320 | tf_op jit(solution)/shard_map/ppermute | solution.py:326
  125.1 0.9 add_convert_fusion.10
  126.0 0.5 collective-permute-start.4
  126.5 10.1 %all-to-all-start.2 = ((f32[128,1,8]{2,1,0:T(1,128)}), f32[128,1,8]{2,1,0:T(1,128)S(1)}, u32[]{:S(2)}, u32[]{:S(2)}) async-start(f32[128,1,8]{2,1,0:T(1,128)} %bitcast.16), calls=%async_computation.2 | async-start | bytes 131072 | tf_op jit(solution)/shard_map/all_to_all | solution.py:615
  136.7 0.0 collective-permute-done.10
  136.7 0.1 convert_add_fusion.k2
  136.8 0.0 collective-permute-done.13.r2
  136.8 0.0 collective-permute-done.8.r1
  136.8 0.0 collective-permute-done.4.r0
  136.8 1.0 deal.1
  137.9 8.3 %all-to-all-done.2 = f32[128,1,8]{2,1,0:T(1,128)S(1)} async-done(((f32[128,1,8]{2,1,0:T(1,128)}), f32[128,1,8]{2,1,0:T(1,128)S(1)}, u32[]{:S(2)}, u32[]{:S(2)}) %all-to-all-start.2) | async-done | bytes 4128 | tf_op jit(solution)/shard_map/all_to_all | solution.py:615
  146.2 8.7 %all-to-all-start.3 = ((bf16[8,32,1536]{2,1,0:T(8,128)(2,1)}), bf16[8,32,1536]{2,1,0:T(8,128)(2,1)S(1)}, u32[]{:S(2)}, u32[]{:S(2)}) async-start(bf16[8,32,1536]{2,1,0:T(8,128)(2,1)} %deal.1), calls=%async_computation.3 | async-start | bytes 1572864 | tf_op jit(solution)/shard_map/all_to_all | solution.py:405
  154.9 2.2 %returned.1 = f32[4,128]{1,0:T(4,128)} custom-call(f32[128,8]{1,0:T(8,128)} %bitcast.44, s32[4,128]{1,0:T(4,128)} %bitcast.47, s32[4,128]{1,0:T(4,128)} %get-tuple-element.43.brank), custom_call_target="tpu_custom_call" | custom-call | tf_op jit(solution)/shard_map/returned/pallas_call | solution.py:616
  157.1 4.3 %all-to-all-done.3.dealt = bf16[8,32,1536]{2,1,0:T(8,128)(2,1)S(1)} async-done(((bf16[8,32,1536]{2,1,0:T(8,128)(2,1)}), bf16[8,32,1536]{2,1,0:T(8,128)(2,1)S(1)}, u32[]{:S(2)}, u32[]{:S(2)}) %all-to-all-start.3) | async-done | bytes 786464 | tf_op jit(solution)/shard_map/all_to_all | solution.py:405
  161.4 0.8 finish.1
  (14 shorter events, 0.0 us)
Async XLA Ops:
  2.5 20.6 %all-to-all-start = ((s32[128,1,12]{2,1,0:T(1,128)}), s32[128,1,12]{2,1,0:T(1,128)S(1)}, u32[]{:S(2)}, u32[]{:S(2)}) async-start(s32[128,1,12]{2,1,0:T(1,128)} %bitcast.45), calls=%async_computation | async-start | bytes 131072 | tf_op jit(solution)/shard_map/all_to_all | solution.py:449
  28.1 19.5 %all-to-all-start.1 = ((bf16[128,4,512]{2,1,0:T(4,128)(2,1)}), bf16[128,4,512]{2,1,0:T(4,128)(2,1)S(1)}, u32[]{:S(2)}, u32[]{:S(2)}) async-start(bf16[128,4,512]{2,1,0:T(4,128)(2,1)} %reshape.81), calls=%async_computation.1 | async-start | bytes 1048576 | tf_op jit(solution)/shard_map/all_to_all | solution.py:452
  47.6 13.8 %copy-start = (s32[2,128]{1,0:T(2,128)S(1)}, s32[2,128]{1,0:T(2,128)}, u32[]{:S(2)}) copy-start(s32[2,128]{1,0:T(2,128)} %get-tuple-element.35.hslot) | copy-start | bytes 3076
  78.3 6.1 %collective-permute-start.1 = (bf16[1024,1536]{1,0:T(8,128)(2,1)S(1)}, bf16[1024,1536]{1,0:T(8,128)(2,1)S(1)}, u32[]{:S(2)}, u32[]{:S(2)}) collective-permute-start(bf16[1024,1536]{1,0:T(8,128)(2,1)S(1)} %shard_map.149), channel_id=1, source_target_pairs={{0,1},{1,0},{2,3},{3,2},{4,5},{5,4},{6,7},{7,6},{8,9},{9,8},{10,11... | collective-permute-start | bytes 9437192 | tf_op jit(solution)/shard_map/ppermute | solution.py:575
  83.8 10.0 %collective-permute-start = (bf16[1024,1536]{1,0:T(8,128)(2,1)S(1)}, bf16[1024,1536]{1,0:T(8,128)(2,1)S(1)}, u32[]{:S(2)}, u32[]{:S(2)}) collective-permute-start(bf16[1024,1536]{1,0:T(8,128)(2,1)S(1)} %shard_map.147), channel_id=1, source_target_pairs={{0,1},{1,0},{2,3},{3,2},{4,5},{5,4},{6,7},{7,6},{8,9},{9,8},{10,11... | collective-permute-start | bytes 9437192 | tf_op jit(solution)/shard_map/ppermute | solution.py:575
  91.2 12.1 %collective-permute-start.11 = (bf16[2,4,64,512]{3,2,1,0:T(8,128)(2,1)}, bf16[2,4,64,512]{3,2,1,0:T(8,128)(2,1)}, u32[]{:S(2)}, u32[]{:S(2)}) collective-permute-start(bf16[2,4,64,512]{3,2,1,0:T(8,128)(2,1)} %get-tuple-element.53), channel_id=1, source_target_pairs={{0,2},{1,7},{2,0},{3,5},{4,6},{5,3},{6,4},{7,1},{8,10},{9,15},{10,... | collective-permute-start | bytes 1572872 | tf_op jit(solution)/shard_map/ppermute | solution.py:326
  92.2 21.4 %copy-start.3 = (bf16[2,256,512]{2,1,0:T(8,128)(2,1)S(1)}, bf16[2,256,512]{2,1,0:T(8,128)(2,1)}, u32[]{:S(2)}) copy-start(bf16[2,256,512]{2,1,0:T(8,128)(2,1)} %get-tuple-element.48) | copy-start | bytes 1572868
  92.2 22.1 %collective-permute-start.2 = (bf16[1024,512]{1,0:T(8,128)(2,1)}, bf16[1024,512]{1,0:T(8,128)(2,1)}, u32[]{:S(2)}, u32[]{:S(2)}) collective-permute-start(bf16[1024,512]{1,0:T(8,128)(2,1)} %get-tuple-element.45), channel_id=1, source_target_pairs={{0,32},{1,97},{2,34},{3,99},{4,36},{5,101},{6,38},{7,103},{8,40},{... | collective-permute-start | bytes 3145736 | tf_op jit(solution)/shard_map/ppermute | solution.py:326
  100.9 13.4 %copy-start.1 = (bf16[1024,512]{1,0:T(8,128)(2,1)S(1)}, bf16[1024,512]{1,0:T(8,128)(2,1)}, u32[]{:S(2)}) copy-start(bf16[1024,512]{1,0:T(8,128)(2,1)} %get-tuple-element.44) | copy-start | bytes 3145732
  100.9 9.5 %collective-permute-start.9 = (bf16[2,4,64,512]{3,2,1,0:T(8,128)(2,1)}, bf16[2,4,64,512]{3,2,1,0:T(8,128)(2,1)S(1)}, u32[]{:S(2)}, u32[]{:S(2)}) collective-permute-start(bf16[2,4,64,512]{3,2,1,0:T(8,128)(2,1)} %get-tuple-element.51), channel_id=1, source_target_pairs={{0,2},{1,7},{2,0},{3,5},{4,6},{5,3},{6,4},{7,1},{8,10},{9,15},{10,... | collective-permute-start | bytes 1572872 | tf_op jit(solution)/shard_map/ppermute | solution.py:326
  101.3 12.3 %collective-permute-start.6 = (bf16[2,256,512]{2,1,0:T(8,128)(2,1)}, bf16[2,256,512]{2,1,0:T(8,128)(2,1)S(1)}, u32[]{:S(2)}, u32[]{:S(2)}) collective-permute-start(bf16[2,256,512]{2,1,0:T(8,128)(2,1)} %get-tuple-element.49), channel_id=1, source_target_pairs={{0,8},{1,25},{2,10},{3,27},{4,12},{5,29},{6,14},{7,31},{8,0},{9,17... | collective-permute-start | bytes 1572872 | tf_op jit(solution)/shard_map/ppermute | solution.py:326
  102.8 13.5 %collective-permute-start.5 = (bf16[2,256,512]{2,1,0:T(8,128)(2,1)}, bf16[2,256,512]{2,1,0:T(8,128)(2,1)S(1)}, u32[]{:S(2)}, u32[]{:S(2)}) collective-permute-start(bf16[2,256,512]{2,1,0:T(8,128)(2,1)} %get-tuple-element.47), channel_id=1, source_target_pairs={{0,8},{1,25},{2,10},{3,27},{4,12},{5,29},{6,14},{7,31},{8,0},{9,17... | collective-permute-start | bytes 1572872 | tf_op jit(solution)/shard_map/ppermute | solution.py:326
  103.3 13.0 %copy-start.2 = (bf16[2,256,512]{2,1,0:T(8,128)(2,1)S(1)}, bf16[2,256,512]{2,1,0:T(8,128)(2,1)}, u32[]{:S(2)}) copy-start(bf16[2,256,512]{2,1,0:T(8,128)(2,1)} %get-tuple-element.46) | copy-start | bytes 1572868
  104.5 14.6 %collective-permute-start.12 = (bf16[2,2,2,32,512]{4,3,2,1,0:T(8,128)(2,1)S(1)}, bf16[2,2,2,32,512]{4,3,2,1,0:T(8,128)(2,1)S(1)}, u32[]{:S(2)}, u32[]{:S(2)}) collective-permute-start(bf16[2,2,2,32,512]{4,3,2,1,0:T(8,128)(2,1)S(1)} %add_convert_fusion.5), channel_id=1, source_target_pairs={{0,8},{1,25},{2,10},{3,27},{4,12},{5,29},{6,14},{7,31},{8,0},{9,17... | collective-permute-start | bytes 786440 | tf_op jit(solution)/shard_map/ppermute | solution.py:326
  112.1 24.6 %collective-permute-start.10 = (bf16[2,2,2,32,512]{4,3,2,1,0:T(8,128)(2,1)}, bf16[2,2,2,32,512]{4,3,2,1,0:T(8,128)(2,1)S(1)}, u32[]{:S(2)}, u32[]{:S(2)}) collective-permute-start(bf16[2,2,2,32,512]{4,3,2,1,0:T(8,128)(2,1)} %add_convert_fusion.7), channel_id=1, source_target_pairs={{0,8},{1,25},{2,10},{3,27},{4,12},{5,29},{6,14},{7,31},{8,0},{9,17... | collective-permute-start | bytes 786440 | tf_op jit(solution)/shard_map/ppermute | solution.py:326
  113.6 5.5 %copy-start.5 = (bf16[2,4,64,512]{3,2,1,0:T(8,128)(2,1)S(1)}, bf16[2,4,64,512]{3,2,1,0:T(8,128)(2,1)}, u32[]{:S(2)}) copy-start(bf16[2,4,64,512]{3,2,1,0:T(8,128)(2,1)} %get-tuple-element.52) | copy-start | bytes 1572868
  113.7 9.3 %collective-permute-start.7 = (bf16[2,2,4,32,512]{4,3,2,1,0:T(8,128)(2,1)S(1)}, bf16[2,2,4,32,512]{4,3,2,1,0:T(8,128)(2,1)S(1)}, u32[]{:S(2)}, u32[]{:S(2)}) collective-permute-start(bf16[2,2,4,32,512]{4,3,2,1,0:T(8,128)(2,1)S(1)} %bitcast.37), channel_id=1, source_target_pairs={{0,32},{1,97},{2,34},{3,99},{4,36},{5,101},{6,38},{7,103},{8,40},{... | collective-permute-start | bytes 1572872 | tf_op jit(solution)/shard_map/ppermute | solution.py:326
  115.9 9.3 %collective-permute-start.3 = (bf16[2,4,2,32,512]{4,3,2,1,0:T(8,128)(2,1)S(1)}, bf16[2,4,2,32,512]{4,3,2,1,0:T(8,128)(2,1)S(1)}, u32[]{:S(2)}, u32[]{:S(2)}) collective-permute-start(bf16[2,4,2,32,512]{4,3,2,1,0:T(8,128)(2,1)S(1)} %get-tuple-element.57), channel_id=1, source_target_pairs={{0,2},{1,7},{2,0},{3,5},{4,6},{5,3},{6,4},{7,1},{8,10},{9,15},{10,... | collective-permute-start | bytes 1572872 | tf_op jit(solution)/shard_map/ppermute | solution.py:326
  116.3 20.4 %copy-start.4 = (bf16[2,4,64,512]{3,2,1,0:T(8,128)(2,1)S(1)}, bf16[2,4,64,512]{3,2,1,0:T(8,128)(2,1)}, u32[]{:S(2)}) copy-start(bf16[2,4,64,512]{3,2,1,0:T(8,128)(2,1)} %get-tuple-element.50) | copy-start | bytes 1572868
  120.9 16.0 %collective-permute-start.13 = (bf16[2,2,2,32,512]{4,3,2,1,0:T(8,128)(2,1)}, bf16[2,2,2,32,512]{4,3,2,1,0:T(8,128)(2,1)S(1)}, u32[]{:S(2)}, u32[]{:S(2)}) collective-permute-start(bf16[2,2,2,32,512]{4,3,2,1,0:T(8,128)(2,1)} %add_convert_fusion.4), channel_id=1, source_target_pairs={{0,32},{1,97},{2,34},{3,99},{4,36},{5,101},{6,38},{7,103},{8,40},{... | collective-permute-start | bytes 786440 | tf_op jit(solution)/shard_map/ppermute | solution.py:326
  123.1 13.7 %collective-permute-start.8 = (bf16[2,2,2,32,512]{4,3,2,1,0:T(8,128)(2,1)S(1)}, bf16[2,2,2,32,512]{4,3,2,1,0:T(8,128)(2,1)S(1)}, u32[]{:S(2)}, u32[]{:S(2)}) collective-permute-start(bf16[2,2,2,32,512]{4,3,2,1,0:T(8,128)(2,1)S(1)} %get-tuple-element.58), channel_id=1, source_target_pairs={{0,2},{1,7},{2,0},{3,5},{4,6},{5,3},{6,4},{7,1},{8,10},{9,15},{10,... | collective-permute-start | bytes 786440 | tf_op jit(solution)/shard_map/ppermute | solution.py:326
  126.0 10.8 %collective-permute-start.4 = (bf16[2,2,2,32,512]{4,3,2,1,0:T(8,128)(2,1)}, bf16[2,2,2,32,512]{4,3,2,1,0:T(8,128)(2,1)S(1)}, u32[]{:S(2)}, u32[]{:S(2)}) collective-permute-start(bf16[2,2,2,32,512]{4,3,2,1,0:T(8,128)(2,1)} %get-tuple-element.60), channel_id=1, source_target_pairs={{0,8},{1,25},{2,10},{3,27},{4,12},{5,29},{6,14},{7,31},{8,0},{9,17... | collective-permute-start | bytes 786440 | tf_op jit(solution)/shard_map/ppermute | solution.py:326
  126.5 19.6 %all-to-all-start.2 = ((f32[128,1,8]{2,1,0:T(1,128)}), f32[128,1,8]{2,1,0:T(1,128)S(1)}, u32[]{:S(2)}, u32[]{:S(2)}) async-start(f32[128,1,8]{2,1,0:T(1,128)} %bitcast.16), calls=%async_computation.2 | async-start | bytes 131072 | tf_op jit(solution)/shard_map/all_to_all | solution.py:615
  146.1 8.7 %copy-start.6 = (f32[128,1,8]{2,1,0:T(1,128)}, f32[128,1,8]{2,1,0:T(1,128)S(1)}, u32[]{:S(2)}) copy-start(f32[128,1,8]{2,1,0:T(1,128)S(1)} %all-to-all-done.2) | copy-start | bytes 12292
  146.2 15.3 %all-to-all-start.3 = ((bf16[8,32,1536]{2,1,0:T(8,128)(2,1)}), bf16[8,32,1536]{2,1,0:T(8,128)(2,1)S(1)}, u32[]{:S(2)}, u32[]{:S(2)}) async-start(bf16[8,32,1536]{2,1,0:T(8,128)(2,1)} %deal.1), calls=%async_computation.3 | async-start | bytes 1572864 | tf_op jit(solution)/shard_map/all_to_all | solution.py:405
